TPU v7x, 256 devices: a whole 4x4x8 slice. The times are simulated.
256 devices in a mesh: gx: 8 (over z), gy: 4 (over x), gz: 8 (over y, core).
Axes of the slice: x: 4, y: 4, z: 8, core: 2. Of those that a mesh axis runs over, the one named last changes fastest.
Arguments:
- east_wind: float32 [96, 1024, 512], P('gz', 'gx', 'gy'), may hold values from -6 to 6
- north_wind: float32 [96, 1024, 512], P('gz', 'gx', 'gy'), may hold values from -6 to 6
- vertical_wind: float32 [96, 1024, 512], P('gz', 'gx', 'gy'), may hold values from -6 to 6
- geopotential: float32 [96, 1024, 512], P('gz', 'gx', 'gy'), may hold values from -6 to 6
- pressure: float32 [96, 1024, 512], P('gz', 'gx', 'gy'), may hold values from -6 to 6
- column_mass: float32 [1024, 512], P('gx', 'gy'), may hold values from 0.5 to 2
Outputs:
- east_after: float32 [96, 1024, 512], P('gz', 'gx', 'gy')
- north_after: float32 [96, 1024, 512], P('gz', 'gx', 'gy')
- vertical_after: float32 [96, 1024, 512], P('gz', 'gx', 'gy')
- geo_after: float32 [96, 1024, 512], P('gz', 'gx', 'gy')
- pressure_after: float32 [96, 1024, 512], P('gz', 'gx', 'gy')
All inputs are finite; a program needn't handle non-finite values.
Results may differ from a plain program's by a relative error of at most 0.0003.
Values sent between devices are 32-bit elements; how exact they have to be, the bound alone decides.
No kernel may reach another device: no remote copies, remote signals or barrier semaphores. Data moves between devices by JAX's collectives and lax.ppermute only.
A program may use at most 64 MiB of HBM per device.

v0:
```python
import functools

import jax
import jax.numpy as jnp
from jax import lax
from jax.experimental import pallas as pl
from jax.experimental.pallas import tpu as pltpu
from jax.sharding import PartitionSpec as P


ITERS = 3
GRANT = 64800

horiz_push = 0.25
mass_flux = 0.2
buoy_coupling = 0.5
geo_rate = 0.5
level_flux = 0.5
stiffness = 30.0


F32 = jnp.float32
NZ = 96
LV = 24
HALF = 12
RX = 64
LN = 128
TILES = RX // 8
EDGE = 2 * LV
PART = 2 * HALF
VMEM = pl.BlockSpec(memory_space=pltpu.VMEM)
HBM = pl.BlockSpec(memory_space=pltpu.HBM)
PRESS, EAST, NORTH, WIND, GEO = range(5)


def shape(*dims):
    return jax.ShapeDtypeStruct(dims, F32)


def call(body, outs, args, in_specs=None, scratch=(), cost=4_000_000, out_specs=None, grant=24 * 1024):
    return pl.pallas_call(
        body,
        out_shape=outs,
        in_specs=in_specs or [VMEM] * len(args),
        out_specs=out_specs or [VMEM] * len(outs),
        scratch_shapes=list(scratch),
        cost_estimate=pl.CostEstimate(flops=cost, bytes_accessed=1_000_000, transcendentals=0),
        compiler_params=pltpu.CompilerParams(vmem_limit_bytes=grant * 1024),
    )(*args)


def core_of():
    return lax.rem(lax.axis_index("gz"), 2)


def chip_of():
    return lax.div(lax.axis_index("gz"), 2)


def lanes():
    return lax.broadcasted_iota(jnp.int32, (8, LN), 1)


def roll_lanes(value, amount):
    return pltpu.roll(value, amount % LN, 1)


def rows_at(start):
    return pl.ds(pl.multiple_of(start, 8), 8)


def pack_columns(tile_at, out, base, groups):
    lane = lanes()
    for g in range(groups):
        acc = jnp.zeros((8, LN), F32)
        for j in range(4):
            for t in range(TILES):
                slot = 8 * j + t
                moved = roll_lanes(tile_at(4 * g + j, t), 4 * slot - 126)
                acc = jnp.where(lane // 4 == slot, moved, acc)
        out[base + 8 * g : base + 8 * g + 8, :] = acc


def pack_rows(tile_at, groups):
    firsts, lasts = [], []
    for g in range(groups):
        first = [tile_at(4 * g + j, 0)[0:2] for j in range(4)]
        last = [tile_at(4 * g + j, TILES - 1)[6:8] for j in range(4)]
        firsts.append(jnp.concatenate(first, 0))
        lasts.append(jnp.concatenate(last, 0))
    return firsts, lasts


def tiles_of(ref, *lead):
    return lambda k, t: ref[(*lead, k, slice(8 * t, 8 * t + 8), slice(None))]


def split_kernel(*refs):
    ins, (send, keep, give, whole, part, sem) = refs[:5], refs[5:]
    core = core_of()
    ours = pl.ds(pl.multiple_of(core * RX, RX), RX)
    theirs = pl.ds(pl.multiple_of((1 - core) * RX, RX), RX)
    copies = []
    for f in range(5):
        if f < 3:
            copy = pltpu.make_async_copy(ins[f], whole.at[f], sem.at[f])
        else:
            copy = pltpu.make_async_copy(ins[f].at[:, theirs, :], part.at[f - 3], sem.at[f])
        copy.start()
        copies.append(copy)
    for f in range(5):
        copies[f].wait()
        source = whole.at[f, :, theirs, :] if f < 3 else part.at[f - 3]
        copy = pltpu.make_async_copy(source, send.at[f], sem.at[5 + f])
        copy.start()
        copies.append(copy)

    def half(f, which):
        def tile_at(k, t):
            return whole[f, k, rows_at(which * RX + 8 * t), :]

        return tile_at

    for out, near in ((keep, core), (give, 1 - core)):
        pack_columns(half(PRESS, near), out, 0, 3)
        pack_columns(half(NORTH, near), out, PART, 3)
        for part_at, (which, f) in enumerate(((near, PRESS), (near, EAST), (1 - near, PRESS), (1 - near, EAST))):
            for g, (first, last) in enumerate(zip(*pack_rows(half(f, which), 3))):
                base = (2 + part_at) * PART + 8 * g
                out[base : base + 8, :] = jnp.where(near == 0, first, last)
    for copy in copies[5:]:
        copy.wait()


def split(*fields):
    edges = shape(6 * PART, LN)
    return call(
        split_kernel,
        [shape(5, HALF, RX, LN), edges, edges],
        fields,
        in_specs=[HBM] * 5,
        out_specs=[HBM, VMEM, VMEM],
        scratch=[
            pltpu.VMEM((3, HALF, 2 * RX, LN), F32),
            pltpu.VMEM((2, HALF, RX, LN), F32),
            pltpu.SemaphoreType.DMA((10,)),
        ],
        grant=GRANT,
    )


def edges_kernel(keep, got, cols, outer, mid):
    core = core_of()
    for which, out in enumerate((cols, outer, mid)):
        for f in range(2):
            part = slice((2 * which + f) * PART, (2 * which + f + 1) * PART)
            for piece in range(2):
                at = (2 * f + piece) * PART
                out[at : at + PART, :] = jnp.where(core == piece, keep[part, :], got[part, :])


def merge_kernel(count, own, got, *refs):
    outs, sem = refs[:count], refs[-1]
    if len(refs) > count + 1:
        refs[count][...] = jnp.zeros((8, LN), F32)
    core = core_of()
    copies = []
    for f in range(count):
        for which, src in ((core, own), (1 - core, got)):
            rows = pl.ds(pl.multiple_of(which * RX, RX), RX)
            copy = pltpu.make_async_copy(src.at[f], outs[f].at[:, rows, :], sem.at[len(copies)])
            copy.start()
            copies.append(copy)
    for copy in copies:
        copy.wait()


def merge(own, got, token=False):
    count = own.shape[0]
    return call(
        functools.partial(merge_kernel, count),
        [shape(HALF, 2 * RX, LN)] * count + [shape(8, LN)] * token,
        [own, got],
        out_specs=[HBM] * count + [VMEM] * token,
        scratch=[pltpu.SemaphoreType.DMA((2 * count,))],
    )


def inner_kernel(first, *refs):
    if first:
        ins, (got, mass, east_out, north_out, star, ends) = refs[:3], refs[3:]
    else:
        (press, east, north, wind, geo, mass, east_fix) = refs[:7]
        (east_out, north_out, star, ends, heave, geo_out) = refs[7:]
    core = core_of()
    row = lax.broadcasted_iota(jnp.int32, (8, LN), 0)
    zero = jnp.zeros((8, LN), F32)

    def row_difference(tiles):
        above = [pltpu.roll(tile, 7, 0) for tile in tiles] + [zero]
        below = [zero] + [pltpu.roll(tile, 1, 0) for tile in tiles]
        return [
            jnp.where(row == 7, above[t + 1], above[t]) - jnp.where(row == 0, below[t], below[t + 1])
            for t in range(TILES)
        ]

    def group(g, carry):
        piece = g // 3

        def tile_at(f, k, t):
            tile = slice(8 * t, 8 * t + 8)
            if not first:
                return (press, east, north)[f][k, tile, :]
            k = k - HALF * piece
            return jnp.where(core == piece, ins[f][k, rows_at(core * RX + 8 * t), :], got[f, k, tile, :])

        rows = rows_at(8 * g)
        end_rows = []
        if not first:
            e_fix = east_fix[rows, :]
        for j in range(4):
            k = 4 * g + j
            p = [tile_at(PRESS, k, t) for t in range(TILES)]
            end_rows += [p[0][0:1], p[-1][7:8]]
            e = [tile_at(EAST, k, t) for t in range(TILES)]
            if not first:
                e[0] = e[0] + jnp.where(row == 0, e_fix[2 * j : 2 * j + 1], 0.0)
                e[-1] = e[-1] + jnp.where(row == 7, e_fix[2 * j + 1 : 2 * j + 2], 0.0)
            e = [tile - horiz_push * step for tile, step in zip(e, row_difference(p))]
            spread = row_difference(e)
            for t in range(TILES):
                tile = slice(8 * t, 8 * t + 8)
                east_out[k, tile, :] = e[t]
                n = tile_at(NORTH, k, t)
                n = n - horiz_push * (roll_lanes(p[t], -1) - roll_lanes(p[t], 1))
                north_out[k, tile, :] = n
                divergence = spread[t] + (roll_lanes(n, -1) - roll_lanes(n, 1))
                star[k, tile, :] = p[t] - mass_flux * mass[tile, :] * divergence
                if not first:
                    moved = wind[k + 1, tile, :]
                    geo_now = geo[k, tile, :] + geo_rate * moved
                    geo_out[k, tile, :] = geo_now
                    heave[k, tile, :] = moved + buoy_coupling * geo_now
        ends[rows, :] = jnp.concatenate(end_rows, 0)
        return carry

    lax.fori_loop(0, LV // 4, group, 0)


def inner(first, *args):
    field = shape(LV, RX, LN)
    return call(
        functools.partial(inner_kernel, first),
        [field, field, field, shape(EDGE, LN)] + ([] if first else [field, field]),
        args,
    )


def heave_kernel(wind, geo, got, heave, geo_out):
    core = core_of()
    rows = pl.ds(pl.multiple_of(core * RX, RX), RX)

    def level(k, carry):
        here, there = core * HALF + k, (1 - core) * HALF + k
        geo_out[here] = geo[k, rows, :]
        heave[here] = wind[k, rows, :] + buoy_coupling * geo[k, rows, :]
        geo_out[there] = got[GEO, k]
        heave[there] = got[WIND, k] + buoy_coupling * got[GEO, k]
        return carry

    lax.fori_loop(0, HALF, level, 0)


def rim_kernel(first, last, *refs):
    (star_in, heave, ends, mass, rate, up, down, mid, outer, left, right, own_cols) = refs[:12]
    refs = refs[12:]
    if not first:
        (north_fix_in, east_edge, north_own, north_edge), refs = refs[:4], refs[4:]
    (star, forced, to_next, to_far, to_prev, east_fix, north_fix) = refs[:7]
    if not last:
        east_edge_out, north_own_out, north_edge_out = refs[7:]
    core, chip = core_of(), chip_of()
    lane = lanes()
    quarter = lane % 4
    rim_lane = jnp.logical_or(lane < 2, lane >= LN - 2)
    row = lax.broadcasted_iota(jnp.int32, (8, LN), 0)
    odd = row % 2 == 1
    ratio, inverse, scale = rate[0], rate[1], rate[3]

    for g in range(LV // 4):
        rows = slice(8 * g, 8 * g + 8)
        more = slice(EDGE + 8 * g, EDGE + 8 * g + 8)
        p_low = jnp.where(core == 0, outer[rows, :], mid[rows, :])
        p_high = jnp.where(core == 0, mid[rows, :], outer[rows, :])
        p_edge = jnp.where(quarter < 2, left[rows, :], right[rows, :])
        p_own = own_cols[rows, :]
        if first:
            e_edge = jnp.where(
                odd,
                jnp.where(core == 0, outer[more, :], mid[more, :]),
                jnp.where(core == 0, mid[more, :], outer[more, :]),
            )
            n_own, n_edge = own_cols[more, :], jnp.where(quarter < 2, left[more, :], right[more, :])
        else:
            e_edge, n_own, n_edge = east_edge[rows, :], north_own[rows, :], north_edge[rows, :]
        own_up, own_down = roll_lanes(p_own, -1), roll_lanes(p_own, 1)
        edge_up, edge_down = roll_lanes(p_edge, -1), roll_lanes(p_edge, 1)
        low_side = quarter == 1
        n_edge = n_edge - horiz_push * jnp.where(low_side, own_up - edge_down, edge_up - own_down)
        n_own = n_own - horiz_push * jnp.where(low_side, edge_up - own_down, own_up - edge_down)
        n_fix = -horiz_push * jnp.where(low_side, edge_up - own_up, own_down - edge_down)
        if not first:
            n_fix = n_fix + north_fix_in[rows, :]
        gap = n_edge - (n_own - n_fix)
        north_fix[rows, :] = n_fix
        if not last:
            north_own_out[rows, :] = n_own
            north_edge_out[rows, :] = n_edge
        spread = jnp.where(
            quarter == 0,
            roll_lanes(n_fix, -1),
            jnp.where(
                quarter == 1,
                roll_lanes(gap, -1),
                -jnp.where(quarter == 2, roll_lanes(gap, 1), roll_lanes(n_fix, 1)),
            ),
        )
        tips = ends[rows, :]
        edges, fixes = [], []
        for j in range(4):
            a, b = 2 * j, 2 * j + 1
            over = e_edge[a : a + 1] - horiz_push * (p_high[b : b + 1] - tips[b : b + 1])
            under = e_edge[b : b + 1] - horiz_push * (tips[a : a + 1] - p_low[a : a + 1])
            lift, sink = horiz_push * p_low[b : b + 1], -horiz_push * p_high[a : a + 1]
            edges += [over, under]
            fixes += [lift, sink]
            for t in range(TILES):
                tile = slice(8 * t, 8 * t + 8)
                term = jnp.where(rim_lane, roll_lanes(spread, 126 - 4 * (8 * j + t)), 0.0)
                if t == 0:
                    term = term - jnp.where(row == 0, under, jnp.where(row == 1, lift, 0.0))
                if t == TILES - 1:
                    term = term + jnp.where(row == 7, over, jnp.where(row == 6, sink, 0.0))
                k = 4 * g + j
                star[k, tile, :] = star_in[k, tile, :] - mass_flux * mass[tile, :] * term
        if not last:
            east_edge_out[rows, :] = jnp.concatenate(edges, 0)
        east_fix[rows, :] = jnp.concatenate(fixes, 0)

    for t in range(TILES):
        tile = slice(8 * t, 8 * t + 8)
        rho, inv, factor = ratio[tile], inverse[tile], scale[tile]
        bottom, top = factor * star[0, tile, :], factor * star[LV - 1, tile, :]
        total = -up[0, tile, :] * bottom
        tail = -inv * down[0, tile, :] * bottom
        power = None
        for k in range(LV):
            f = heave[k, tile, :]
            if k < LV - 1:
                f = f - star[k + 1, tile, :]
            if k > 0:
                f = f + star[k - 1, tile, :]
            f = factor * f
            forced[k, tile, :] = f
            total = rho * total + up[k + 1, tile, :] * f
            weighted = down[k + 1, tile, :] * f
            tail = tail + (weighted if k == 0 else power * weighted)
            power = rho if k == 0 else power * rho
        total = total + inv * up[LV + 1, tile, :] * top
        tail = tail + power * (down[LV + 1, tile, :] * top)
        to_next[0, tile, :] = jnp.where(chip < 3, total, tail)
        to_next[1, tile, :] = top
        to_far[tile, :] = jnp.where(chip < 2, total, tail)
        to_prev[0, tile, :] = jnp.where(chip > 0, tail, total)
        to_prev[1, tile, :] = bottom


def rim(first, last, *args):
    edge, field, pair = shape(EDGE, LN), shape(LV, RX, LN), shape(2, RX, LN)
    return call(
        functools.partial(rim_kernel, first, last),
        [field, field, pair, shape(RX, LN), pair] + [edge] * (2 if last else 5),
        args,
    )


def solve_kernel(last, *refs):
    (star, forced, geo, mass, rate, up, down, from_prev, from_far, from_next) = refs[:10]
    refs = refs[10:]
    if last:
        (after, mine, theirs, sums, wind, geo_out, press) = refs
    else:
        (wind, press, mid, outer, cols, sums) = refs
    core, chip = core_of(), chip_of()

    for t in range(TILES):
        tile = slice(8 * t, 8 * t + 8)
        ratio, inverse, deep, scale = (rate[i, tile, :] for i in range(4))
        zero = jnp.zeros((8, LN), F32)
        prev, far, after = from_prev[0, tile, :], from_far[tile, :], from_next[0, tile, :]
        star_under = jnp.where(chip > 0, from_prev[1, tile, :], zero)
        star_over = jnp.where(chip < 3, from_next[1, tile, :], zero)
        far_deep = deep * far
        enter = jnp.where(
            chip == 0,
            zero,
            prev + jnp.where(chip >= 2, far_deep, zero) + jnp.where(chip == 3, deep * deep * after, zero),
        )
        above = jnp.where(
            chip == 3,
            zero,
            after + jnp.where(chip <= 1, far_deep, zero) + jnp.where(chip == 0, deep * deep * prev, zero),
        )
        enter = enter - inverse * up[1, tile, :] * star_under - up[0, tile, :] * (scale * star[0, tile, :])
        above = above + inverse * down[LV, tile, :] * star_over + down[LV + 1, tile, :] * (scale * star[LV - 1, tile, :])

        def force(k):
            f = forced[k, tile, :]
            if k == 0:
                f = f + star_under
            if k == LV - 1:
                f = f - star_over
            return f

        total = enter
        for k in range(LV):
            total = ratio * total + up[k + 1, tile, :] * force(k)
            sums[k, tile, :] = total
        carried = ratio * above
        higher = down[LV + 1, tile, :] * (ratio * total) + up[LV + 1, tile, :] * above
        wind[LV + 1, tile, :] = higher
        flux = level_flux * mass[tile, :]
        here = None
        for k in range(LV - 1, -1, -1):
            solved = down[k + 1, tile, :] * sums[k, tile, :] + up[k + 1, tile, :] * carried
            wind[k + 1, tile, :] = solved
            if last:
                geo_out[k, tile, :] = geo[k, tile, :] + geo_rate * solved
            if k < LV - 1:
                press[k + 1, tile, :] = star[k + 1, tile, :] - flux * (higher - solved)
                higher = here
            here = solved
            carried = ratio * (carried + down[k + 1, tile, :] * force(k))
        lowest = down[0, tile, :] * enter + up[0, tile, :] * carried
        wind[0, tile, :] = lowest
        press[0, tile, :] = star[0, tile, :] - flux * (higher - lowest)

    if last:
        here, there = core * HALF, (1 - core) * HALF
        for k in range(HALF):
            for f, (source, off) in enumerate(((wind, 1), (geo_out, 0), (press, 0))):
                mine[f, k] = source[here + k + off]
                theirs[f, k] = source[there + k + off]
    else:
        for g, (first_rows, last_rows) in enumerate(zip(*pack_rows(tiles_of(press), LV // 4))):
            rows = slice(8 * g, 8 * g + 8)
            mid[rows, :] = jnp.where(core == 0, last_rows, first_rows)
            outer[rows, :] = jnp.where(core == 0, first_rows, last_rows)
        pack_columns(tiles_of(press), cols, 0, LV // 4)


def solve(last, *args):
    edge, field, tall = shape(EDGE, LN), shape(LV, RX, LN), shape(LV + 2, RX, LN)
    if last:
        outs = [shape(3, HALF, RX, LN)] * 2
        scratch = [pltpu.VMEM(s.shape, F32) for s in (field, tall, field, field)]
    else:
        outs = [tall, field, edge, edge, edge]
        scratch = [pltpu.VMEM(field.shape, F32)]
    return call(functools.partial(solve_kernel, last), outs, args, scratch=scratch)


def sort_winds_kernel(east, north, east_fix, north_fix, mine, theirs):
    core = core_of()
    lane = lanes()
    inner_lane = jnp.logical_or(lane == 0, lane == LN - 1)
    row = lax.broadcasted_iota(jnp.int32, (8, LN), 0)

    def group(g, carry):
        for out, piece in ((mine, core), (theirs, 1 - core)):
            rows = rows_at(8 * (3 * piece + g))
            e_fix, n_fix = east_fix[rows, :], north_fix[rows, :]
            for j in range(4):
                k = HALF * piece + 4 * g + j
                for t in range(TILES):
                    tile = slice(8 * t, 8 * t + 8)
                    e, n = east[k, tile, :], north[k, tile, :]
                    if t == 0:
                        e = e + jnp.where(row == 0, e_fix[2 * j : 2 * j + 1], 0.0)
                    if t == TILES - 1:
                        e = e + jnp.where(row == 7, e_fix[2 * j + 1 : 2 * j + 2], 0.0)
                    n = n + jnp.where(inner_lane, roll_lanes(n_fix, 126 - 4 * (8 * j + t)), 0.0)
                    out[0, 4 * g + j, tile, :] = e
                    out[1, 4 * g + j, tile, :] = n
        return carry

    lax.fori_loop(0, 3, group, 0)


def local(east_wind, north_wind, vertical_wind, geopotential, pressure, column_mass):
    columns, tiles, pieces = lax.axis_size("gx"), lax.axis_size("gy"), lax.axis_size("gz")
    core, chip = core_of(), chip_of()
    swap = [(i, i ^ 1) for i in range(pieces)]

    def along(distance):
        return [(i, (i + 2 * distance) % pieces) for i in range(pieces)]

    outward = [
        (a * pieces + z, (a + (1 if z % 2 else -1)) % columns * pieces + (z ^ 1))
        for a in range(columns)
        for z in range(pieces)
    ]
    east_ring = [(i, (i + 1) % tiles) for i in range(tiles)]
    west_ring = [(i, (i - 1) % tiles) for i in range(tiles)]

    fields = (pressure, east_wind, north_wind, vertical_wind, geopotential)
    send, keep, give = split(*fields)
    got_edges = lax.ppermute(give, "gz", swap)
    wide = shape(2 * EDGE, LN)
    send, got_edges = lax.optimization_barrier((send, got_edges))
    got = lax.ppermute(send, "gz", swap)
    cols, outer, mid = call(edges_kernel, [wide] * 3, [keep, got_edges])

    mass = lax.dynamic_slice_in_dim(column_mass, core * RX, RX, 0)
    stiff_ratio = stiffness * mass
    root = jnp.sqrt(1.0 + 4.0 * stiff_ratio)
    ratio = (1.0 + 2.0 * stiff_ratio - root) / (2.0 * stiff_ratio)
    log_ratio = jnp.log(ratio)
    level = (chip * LV - 1 + lax.iota(jnp.int32, LV + 2)).astype(F32)[:, None, None]
    up = 1.0 - jnp.exp((2.0 * (level + 1.0)) * log_ratio)
    down = 1.0 - jnp.exp((2.0 * (NZ - level)) * log_ratio)
    scale = 1.0 / (root * (1.0 - jnp.exp((2.0 * (NZ + 1.0)) * log_ratio)))
    rate = jnp.stack([ratio, 1.0 / ratio, jnp.exp(float(LV) * log_ratio), scale])

    field = shape(LV, RX, LN)
    for substep in range(ITERS):
        first, last = substep == 0, substep == ITERS - 1
        left = lax.ppermute(cols, "gy", east_ring)
        right = lax.ppermute(cols, "gy", west_ring)
        outer_in = lax.ppermute(outer, ("gx", "gz"), outward)
        if first:
            mid_in = mid
            east, north, star, ends = inner(first, *fields[:3], got, mass)
            heave, geo = call(heave_kernel, [field, field], [*fields[3:], got])
        else:
            mid_in = lax.ppermute(mid, "gz", swap)
            east, north, star, ends, heave, geo = inner(first, press, east, north, wind, geo, mass, east_fix)
        args = [star, heave, ends, mass, rate, up, down, mid_in, outer_in, left, right, cols]
        if not first:
            args += [north_fix, *edges]
        star, forced, to_next, to_far, to_prev, east_fix, north_fix, *edges = rim(first, last, *args)
        from_far = lax.ppermute(to_far, "gz", along(2))
        from_prev = lax.ppermute(to_next, "gz", along(1))
        from_next = lax.ppermute(to_prev, "gz", along(3))
        args = [star, forced, geo, mass, rate, up, down, from_prev, from_far, from_next]
        if last:
            half = shape(2, HALF, RX, LN)
            own_hor, send_hor = call(sort_winds_kernel, [half, half], [east, north, east_fix, north_fix])
            got_hor = lax.ppermute(send_hor, "gz", swap)
            east_after, north_after, written = merge(own_hor, got_hor, token=True)
            own_ver, send_ver = solve(last, *args, written)
        else:
            wind, press, mid, outer, cols = solve(last, *args)
    got_ver = lax.ppermute(send_ver, "gz", swap)
    vertical_after, geo_after, pressure_after = merge(own_ver, got_ver)
    return east_after, north_after, vertical_after, geo_after, pressure_after


def solution(mesh):
    spec = P("gz", "gx", "gy")
    return jax.shard_map(
        local, mesh=mesh, in_specs=(spec,) * 5 + (P("gx", "gy"),), out_specs=(spec,) * 5, check_vma=False
    )
```

profile of v0, /device:TPU:1, one launch (start us, length us, event | category | flops | bytes accessed | tf_op | source)
XLA Modules:
  0.0 70.5 jit_solution(13611693086015128274)
XLA Ops:
  0.6 3.8 %shard_map.101 = (f32[5,12,64,128]{3,2,1,0:T(8,128)}, f32[144,128]{1,0:T(8,128)}, f32[144,128]{1,0:T(8,128)}) custom-call(f32[12,128,128]{2,1,0:T(8,128)} %refs_0_.3, f32[12,128,128]{2,1,0:T(8,128)} %refs_1_.3, f32[12,128,128]{2,1,0:T(8,128)} %refs_2_.3, f32[12,128,128]{2,1,0:T(8,128)} %wind.1, f32[12,128,128]{2,1,0:T(8,128)} %geo.1), custom_call_target="tpu_custom_call" | custom-call | flops 4000000 | bytes 1000000 | tf_op jit(solution)/shard_map/pallas_call | solution.py:41
  4.5 0.0 copy-start.5
  4.5 3.2 %collective-permute-start = (f32[144,128]{1,0:T(8,128)}, f32[144,128]{1,0:T(8,128)S(1)}, u32[]{:S(2)}, u32[]{:S(2)}) collective-permute-start(f32[144,128]{1,0:T(8,128)} %get-tuple-element.79), channel_id=1, source_target_pairs={{0,1},{1,0},{2,3},{3,2},{4,5},{5,4},{6,7},{7,6},{8,9},{9,8},{10,11... | collective-permute-start | bytes 221192 | tf_op jit(solution)/shard_map/ppermute | solution.py:518
  7.7 1.1 %collective-permute-done.got = f32[144,128]{1,0:T(8,128)S(1)} collective-permute-done((f32[144,128]{1,0:T(8,128)}, f32[144,128]{1,0:T(8,128)S(1)}, u32[]{:S(2)}, u32[]{:S(2)}) %collective-permute-start) | collective-permute-done | bytes 73760 | tf_op jit(solution)/shard_map/ppermute | solution.py:518
  8.8 0.4 collective-permute-start.1
  9.2 0.0 copy-start
  9.2 0.0 copy-start.1
  9.3 0.1 fusion.2
  9.3 0.3 exponential_subtract_fusion
  9.7 0.8 %collective-permute-start.4 = (f32[96,128]{1,0:T(8,128)S(1)}, f32[96,128]{1,0:T(8,128)S(1)}, u32[]{:S(2)}, u32[]{:S(2)}) collective-permute-start(f32[96,128]{1,0:T(8,128)S(1)} %get-tuple-element.88.refs_11_), channel_id=1, source_target_pairs={{0,24},{8,0},{16,8},{24,16},{1,25},{9,1},{17,9},{25,17},{2,26},{10... | collective-permute-start | bytes 147464 | tf_op jit(solution)/shard_map/ppermute | solution.py:539
  10.5 0.7 collective-permute-start.3
  11.2 1.3 %collective-permute-start.2 = (f32[96,128]{1,0:T(8,128)S(1)}, f32[96,128]{1,0:T(8,128)S(1)}, u32[]{:S(2)}, u32[]{:S(2)}) collective-permute-start(f32[96,128]{1,0:T(8,128)S(1)} %get-tuple-element.87), channel_id=1, source_target_pairs={{0,225},{1,32},{2,227},{3,34},{4,229},{5,36},{6,231},{7,38},{32,1}... | collective-permute-start | bytes 147464 | tf_op jit(solution)/shard_map/ppermute | solution.py:540
  12.5 0.0 copy-start.2
  12.5 0.0 copy-start.3
  12.5 0.0 copy-start.4
  12.5 0.5 collective-permute-done.1.refs_3_.got
  13.0 0.1 shard_map.103
  13.2 0.4 copy-done.2
  13.6 0.2 copy-done.3
  13.9 0.3 copy-done.4
  14.2 1.6 %shard_map.102 = (f32[24,64,128]{2,1,0:T(8,128)S(1)}, f32[24,64,128]{2,1,0:T(8,128)S(1)}, f32[24,64,128]{2,1,0:T(8,128)S(1)}, f32[48,128]{1,0:T(8,128)S(1)}) custom-call(f32[12,128,128]{2,1,0:T(8,128)S(1)} %copy-done.2, f32[12,128,128]{2,1,0:T(8,128)S(1)} %copy-done.3, f32[12,128,128]{2,1,0:T(8,128)S(1)} %copy-done.4, ...), custom_call_target="tpu_custom_call" | custom-call | flops 4000000 | bytes 1000000 | tf_op jit(solution)/shard_map/pallas_call | solution.py:41
  15.8 0.0 collective-permute-done.3.refs_9_
  15.8 0.7 shard_map.105
  16.5 1.4 %collective-permute-start.5 = (f32[2,64,128]{2,1,0:T(8,128)S(1)}, f32[2,64,128]{2,1,0:T(8,128)S(1)}, u32[]{:S(2)}, u32[]{:S(2)}) collective-permute-start(f32[2,64,128]{2,1,0:T(8,128)S(1)} %get-tuple-element.92), channel_id=1, source_target_pairs={{0,2},{1,3},{2,4},{3,5},{4,6},{5,7},{6,0},{7,1},{8,10},{9,11},{10,... | collective-permute-start | bytes 196616 | tf_op jit(solution)/shard_map/ppermute | solution.py:553
  17.9 1.5 %collective-permute-start.7 = (f32[2,64,128]{2,1,0:T(8,128)S(1)}, f32[2,64,128]{2,1,0:T(8,128)S(1)}, u32[]{:S(2)}, u32[]{:S(2)}) collective-permute-start(f32[2,64,128]{2,1,0:T(8,128)S(1)} %get-tuple-element.94), channel_id=1, source_target_pairs={{0,6},{1,7},{2,0},{3,1},{4,2},{5,3},{6,4},{7,5},{8,14},{9,15},{10,... | collective-permute-start | bytes 196616 | tf_op jit(solution)/shard_map/ppermute | solution.py:554
  19.4 1.6 %collective-permute-start.6 = (f32[64,128]{1,0:T(8,128)S(1)}, f32[64,128]{1,0:T(8,128)S(1)}, u32[]{:S(2)}, u32[]{:S(2)}) collective-permute-start(f32[64,128]{1,0:T(8,128)S(1)} %get-tuple-element.93), channel_id=1, source_target_pairs={{0,4},{1,5},{2,6},{3,7},{4,0},{5,1},{6,2},{7,3},{8,12},{9,13},{10,... | collective-permute-start | bytes 98312 | tf_op jit(solution)/shard_map/ppermute | solution.py:552
  20.9 2.7 %collective-permute-done.6.refs_8_ = f32[64,128]{1,0:T(8,128)S(1)} collective-permute-done((f32[64,128]{1,0:T(8,128)S(1)}, f32[64,128]{1,0:T(8,128)S(1)}, u32[]{:S(2)}, u32[]{:S(2)}) %collective-permute-start.6) | collective-permute-done | bytes 32800 | tf_op jit(solution)/shard_map/ppermute | solution.py:552
  23.7 0.6 shard_map.106
  24.3 5.7 %collective-permute-start.8 = (f32[48,128]{1,0:T(8,128)S(1)}, f32[48,128]{1,0:T(8,128)S(1)}, u32[]{:S(2)}, u32[]{:S(2)}) collective-permute-start(f32[48,128]{1,0:T(8,128)S(1)} %get-tuple-element.103), channel_id=1, source_target_pairs={{0,1},{1,0},{2,3},{3,2},{4,5},{5,4},{6,7},{7,6},{8,9},{9,8},{10,11... | collective-permute-start | bytes 73736 | tf_op jit(solution)/shard_map/ppermute | solution.py:546
  30.0 0.0 collective-permute-start.9
  30.0 2.7 %collective-permute-start.11 = (f32[48,128]{1,0:T(8,128)S(1)}, f32[48,128]{1,0:T(8,128)S(1)}, u32[]{:S(2)}, u32[]{:S(2)}) collective-permute-start(f32[48,128]{1,0:T(8,128)S(1)} %get-tuple-element.105.refs_11_), channel_id=1, source_target_pairs={{0,24},{8,0},{16,8},{24,16},{1,25},{9,1},{17,9},{25,17},{2,26},{10... | collective-permute-start | bytes 73736 | tf_op jit(solution)/shard_map/ppermute | solution.py:539
  32.6 0.0 collective-permute-start.10
  32.6 1.6 %shard_map.107 = (f32[24,64,128]{2,1,0:T(8,128)S(1)}, f32[24,64,128]{2,1,0:T(8,128)S(1)}, f32[24,64,128]{2,1,0:T(8,128)S(1)}, f32[48,128]{1,0:T(8,128)S(1)}, f32...) custom-call(f32[24,64,128]{2,1,0:T(8,128)S(1)} %get-tuple-element.95.refs_0_, ...), custom_call_target="tpu_custom_call" | custom-call | flops 4000000 | bytes 1000000 | tf_op jit(solution)/shard_map/pallas_call | solution.py:41
  34.3 0.0 collective-permute-done.9.refs_8_
  34.3 0.0 collective-permute-done.11.refs_10_
  34.3 2.2 %collective-permute-done.10.refs_9_ = f32[48,128]{1,0:T(8,128)S(1)} collective-permute-done((f32[48,128]{1,0:T(8,128)S(1)}, f32[48,128]{1,0:T(8,128)S(1)}, u32[]{:S(2)}, u32[]{:S(2)}) %collective-permute-start.10) | collective-permute-done | bytes 24608 | tf_op jit(solution)/shard_map/ppermute | solution.py:538
  36.5 0.7 %shard_map.108 = (f32[24,64,128]{2,1,0:T(8,128)S(1)}, f32[24,64,128]{2,1,0:T(8,128)S(1)}, f32[2,64,128]{2,1,0:T(8,128)S(1)}, f32[64,128]{1,0:T(8,128)S(1)}, f32[...) custom-call(f32[24,64,128]{2,1,0:T(8,128)S(1)} %get-tuple-element.10, ...), custom_call_target="tpu_custom_call" | custom-call | flops 4000000 | bytes 1000000 | tf_op jit(solution)/shard_map/pallas_call | solution.py:41
  37.3 0.2 collective-permute-start.12
  37.4 2.6 %collective-permute-start.14 = (f32[2,64,128]{2,1,0:T(8,128)S(1)}, f32[2,64,128]{2,1,0:T(8,128)S(1)}, u32[]{:S(2)}, u32[]{:S(2)}) collective-permute-start(f32[2,64,128]{2,1,0:T(8,128)S(1)} %get-tuple-element.115), channel_id=1, source_target_pairs={{0,6},{1,7},{2,0},{3,1},{4,2},{5,3},{6,4},{7,5},{8,14},{9,15},{10,... | collective-permute-start | bytes 196616 | tf_op jit(solution)/shard_map/ppermute | solution.py:554
  40.0 0.5 collective-permute-start.13
  40.5 4.1 %collective-permute-done.13.refs_8_ = f32[64,128]{1,0:T(8,128)S(1)} collective-permute-done((f32[64,128]{1,0:T(8,128)S(1)}, f32[64,128]{1,0:T(8,128)S(1)}, u32[]{:S(2)}, u32[]{:S(2)}) %collective-permute-start.13) | collective-permute-done | bytes 32800 | tf_op jit(solution)/shard_map/ppermute | solution.py:552
  44.6 0.0 collective-permute-done.12.refs_7_
  44.6 0.0 collective-permute-done.14.refs_9_
  44.6 0.6 shard_map.109
  45.2 4.1 %collective-permute-start.15 = (f32[48,128]{1,0:T(8,128)S(1)}, f32[48,128]{1,0:T(8,128)S(1)}, u32[]{:S(2)}, u32[]{:S(2)}) collective-permute-start(f32[48,128]{1,0:T(8,128)S(1)} %get-tuple-element.126), channel_id=1, source_target_pairs={{0,1},{1,0},{2,3},{3,2},{4,5},{5,4},{6,7},{7,6},{8,9},{9,8},{10,11... | collective-permute-start | bytes 73736 | tf_op jit(solution)/shard_map/ppermute | solution.py:546
  49.3 0.7 %collective-permute-start.16 = (f32[48,128]{1,0:T(8,128)S(1)}, f32[48,128]{1,0:T(8,128)S(1)}, u32[]{:S(2)}, u32[]{:S(2)}) collective-permute-start(f32[48,128]{1,0:T(8,128)S(1)} %get-tuple-element.127), channel_id=1, source_target_pairs={{0,225},{1,32},{2,227},{3,34},{4,229},{5,36},{6,231},{7,38},{32,1}... | collective-permute-start | bytes 73736 | tf_op jit(solution)/shard_map/ppermute | solution.py:540
  50.0 0.0 collective-permute-start.18
  50.0 1.5 %collective-permute-start.17 = (f32[48,128]{1,0:T(8,128)S(1)}, f32[48,128]{1,0:T(8,128)S(1)}, u32[]{:S(2)}, u32[]{:S(2)}) collective-permute-start(f32[48,128]{1,0:T(8,128)S(1)} %get-tuple-element.128.refs_11_), channel_id=1, source_target_pairs={{0,8},{8,16},{16,24},{24,0},{1,9},{9,17},{17,25},{25,1},{2,10},{10... | collective-permute-start | bytes 73736 | tf_op jit(solution)/shard_map/ppermute | solution.py:538
  51.5 1.6 %shard_map.110 = (f32[24,64,128]{2,1,0:T(8,128)S(1)}, f32[24,64,128]{2,1,0:T(8,128)S(1)}, f32[24,64,128]{2,1,0:T(8,128)S(1)}, f32[48,128]{1,0:T(8,128)S(1)}, f32...) custom-call(f32[24,64,128]{2,1,0:T(8,128)S(1)} %get-tuple-element.116.refs_0_, ...), custom_call_target="tpu_custom_call" | custom-call | flops 4000000 | bytes 1000000 | tf_op jit(solution)/shard_map/pallas_call | solution.py:41
  53.1 0.0 collective-permute-done.15.refs_7_
  53.1 0.0 collective-permute-done.18.refs_10_
  53.1 0.8 %collective-permute-done.17.refs_9_ = f32[48,128]{1,0:T(8,128)S(1)} collective-permute-done((f32[48,128]{1,0:T(8,128)S(1)}, f32[48,128]{1,0:T(8,128)S(1)}, u32[]{:S(2)}, u32[]{:S(2)}) %collective-permute-start.17) | collective-permute-done | bytes 24608 | tf_op jit(solution)/shard_map/ppermute | solution.py:538
  53.9 0.7 %shard_map.111 = (f32[24,64,128]{2,1,0:T(8,128)S(1)}, f32[24,64,128]{2,1,0:T(8,128)S(1)}, f32[2,64,128]{2,1,0:T(8,128)S(1)}, f32[64,128]{1,0:T(8,128)S(1)}, f32[...) custom-call(f32[24,64,128]{2,1,0:T(8,128)S(1)} %get-tuple-element.123.refs_0_, ...), custom_call_target="tpu_custom_call" | custom-call | flops 4000000 | bytes 1000000 | tf_op jit(solution)/shard_map/pallas_call | solution.py:41
  54.6 0.4 shard_map.112
  55.0 1.8 %collective-permute-start.19 = (f32[2,12,64,128]{3,2,1,0:T(8,128)S(1)}, f32[2,12,64,128]{3,2,1,0:T(8,128)S(1)}, u32[]{:S(2)}, u32[]{:S(2)}) collective-permute-start(f32[2,12,64,128]{3,2,1,0:T(8,128)S(1)} %get-tuple-element.136), channel_id=1, source_target_pairs={{0,1},{1,0},{2,3},{3,2},{4,5},{5,4},{6,7},{7,6},{8,9},{9,8},{10,11... | collective-permute-start | bytes 2359304 | tf_op jit(solution)/shard_map/ppermute | solution.py:559
  56.9 2.7 %collective-permute-start.22 = (f32[2,64,128]{2,1,0:T(8,128)S(1)}, f32[2,64,128]{2,1,0:T(8,128)S(1)}, u32[]{:S(2)}, u32[]{:S(2)}) collective-permute-start(f32[2,64,128]{2,1,0:T(8,128)S(1)} %get-tuple-element.144), channel_id=1, source_target_pairs={{0,6},{1,7},{2,0},{3,1},{4,2},{5,3},{6,4},{7,5},{8,14},{9,15},{10,... | collective-permute-start | bytes 196616 | tf_op jit(solution)/shard_map/ppermute | solution.py:554
  59.5 0.0 collective-permute-start.21
  59.5 0.0 collective-permute-done.19.got
  59.5 1.2 %shard_map.113 = (f32[12,128,128]{2,1,0:T(8,128)}, f32[12,128,128]{2,1,0:T(8,128)}, f32[8,128]{1,0:T(8,128)S(1)}) custom-call(f32[2,12,64,128]{3,2,1,0:T(8,128)S(1)} %get-tuple-element.135.own, f32[2,12,64,128]{3,2,1,0:T(8,128)S(1)} %collective-permute-done.19.got), custom_call_target="tpu_custom_call" | custom-call | flops 4000000 | bytes 1000000 | tf_op jit(solution)/shard_map/pallas_call | solution.py:41
  60.7 3.1 %collective-permute-done.21.refs_8_ = f32[64,128]{1,0:T(8,128)S(1)} collective-permute-done((f32[64,128]{1,0:T(8,128)S(1)}, f32[64,128]{1,0:T(8,128)S(1)}, u32[]{:S(2)}, u32[]{:S(2)}) %collective-permute-start.21) | collective-permute-done | bytes 32800 | tf_op jit(solution)/shard_map/ppermute | solution.py:552
  63.8 0.8 %shard_map.114 = (f32[3,12,64,128]{3,2,1,0:T(8,128)S(1)}, f32[3,12,64,128]{3,2,1,0:T(8,128)S(1)}) custom-call(f32[24,64,128]{2,1,0:T(8,128)S(1)} %get-tuple-element.139.refs_0_, f32[24,64,128]{2,1,0:T(8,128)S(1)} %get-tuple-element.140.refs_1_, f32[24,64,128]{2,1,0:T(8,128)S(1)} %get-tuple-element.141.refs_2_, ...), custom_call_target="tpu_custom_call" | custom-call | flops 4000000 | bytes 1000000 | tf_op jit(solution)/shard_map/pallas_call | solution.py:41
  64.6 1.9 %collective-permute-start.23 = (f32[3,12,64,128]{3,2,1,0:T(8,128)S(1)}, f32[3,12,64,128]{3,2,1,0:T(8,128)S(1)}, u32[]{:S(2)}, u32[]{:S(2)}) collective-permute-start(f32[3,12,64,128]{3,2,1,0:T(8,128)S(1)} %get-tuple-element.147), channel_id=1, source_target_pairs={{0,1},{1,0},{2,3},{3,2},{4,5},{5,4},{6,7},{7,6},{8,9},{9,8},{10,11... | collective-permute-start | bytes 3538952 | tf_op jit(solution)/shard_map/ppermute | solution.py:564
  66.5 2.5 %collective-permute-done.23.got = f32[3,12,64,128]{3,2,1,0:T(8,128)S(1)} collective-permute-done((f32[3,12,64,128]{3,2,1,0:T(8,128)S(1)}, f32[3,12,64,128]{3,2,1,0:T(8,128)S(1)}, u32[]{:S(2)}, u32[]{:S(2)}) %collective-permute-start.23) | collective-permute-done | bytes 1179680 | tf_op jit(solution)/shard_map/ppermute | solution.py:564
  68.9 1.4 %shard_map.115 = (f32[12,128,128]{2,1,0:T(8,128)}, f32[12,128,128]{2,1,0:T(8,128)}, f32[12,128,128]{2,1,0:T(8,128)}) custom-call(f32[3,12,64,128]{3,2,1,0:T(8,128)S(1)} %get-tuple-element.146.own, f32[3,12,64,128]{3,2,1,0:T(8,128)S(1)} %collective-permute-done.23.got), custom_call_target="tpu_custom_call" | custom-call | flops 4000000 | bytes 1000000 | tf_op jit(solution)/shard_map/pallas_call | solution.py:41
  (18 shorter events, 0.1 us)
Async XLA Ops:
  0.6 8.6 %copy-start.6 = (f32[128,128]{1,0:T(8,128)S(1)}, f32[128,128]{1,0:T(8,128)}, u32[]{:S(2)}) copy-start(f32[128,128]{1,0:T(8,128)} %param.11) | copy-start | bytes 196612
  4.5 5.1 %copy-start.5 = (f32[144,128]{1,0:T(8,128)S(1)}, f32[144,128]{1,0:T(8,128)}, u32[]{:S(2)}) copy-start(f32[144,128]{1,0:T(8,128)} %get-tuple-element.84.keep) | copy-start | bytes 221188
  4.5 4.4 %collective-permute-start = (f32[144,128]{1,0:T(8,128)}, f32[144,128]{1,0:T(8,128)S(1)}, u32[]{:S(2)}, u32[]{:S(2)}) collective-permute-start(f32[144,128]{1,0:T(8,128)} %get-tuple-element.79), channel_id=1, source_target_pairs={{0,1},{1,0},{2,3},{3,2},{4,5},{5,4},{6,7},{7,6},{8,9},{9,8},{10,11... | collective-permute-start | bytes 221192 | tf_op jit(solution)/shard_map/ppermute | solution.py:518
  8.8 4.2 %collective-permute-start.1 = (f32[5,12,64,128]{3,2,1,0:T(8,128)}, f32[5,12,64,128]{3,2,1,0:T(8,128)S(1)}, u32[]{:S(2)}, u32[]{:S(2)}) collective-permute-start(f32[5,12,64,128]{3,2,1,0:T(8,128)} %get-tuple-element.80), channel_id=1, source_target_pairs={{0,1},{1,0},{2,3},{3,2},{4,5},{5,4},{6,7},{7,6},{8,9},{9,8},{10,11... | collective-permute-start | bytes 5898248 | tf_op jit(solution)/shard_map/ppermute | solution.py:521
  9.2 3.8 %copy-start = (f32[12,128,128]{2,1,0:T(8,128)S(1)}, f32[12,128,128]{2,1,0:T(8,128)}, u32[]{:S(2)}) copy-start(f32[12,128,128]{2,1,0:T(8,128)} %wind.1) | copy-start | bytes 2359300
  9.2 3.8 %copy-start.1 = (f32[12,128,128]{2,1,0:T(8,128)S(1)}, f32[12,128,128]{2,1,0:T(8,128)}, u32[]{:S(2)}) copy-start(f32[12,128,128]{2,1,0:T(8,128)} %geo.1) | copy-start | bytes 2359300
  9.7 6.1 %collective-permute-start.4 = (f32[96,128]{1,0:T(8,128)S(1)}, f32[96,128]{1,0:T(8,128)S(1)}, u32[]{:S(2)}, u32[]{:S(2)}) collective-permute-start(f32[96,128]{1,0:T(8,128)S(1)} %get-tuple-element.88.refs_11_), channel_id=1, source_target_pairs={{0,24},{8,0},{16,8},{24,16},{1,25},{9,1},{17,9},{25,17},{2,26},{10... | collective-permute-start | bytes 147464 | tf_op jit(solution)/shard_map/ppermute | solution.py:539
  10.5 5.3 %collective-permute-start.3 = (f32[96,128]{1,0:T(8,128)S(1)}, f32[96,128]{1,0:T(8,128)S(1)}, u32[]{:S(2)}, u32[]{:S(2)}) collective-permute-start(f32[96,128]{1,0:T(8,128)S(1)} %get-tuple-element.88.refs_11_), channel_id=1, source_target_pairs={{0,8},{8,16},{16,24},{24,0},{1,9},{9,17},{17,25},{25,1},{2,10},{10... | collective-permute-start | bytes 147464 | tf_op jit(solution)/shard_map/ppermute | solution.py:538
  11.2 4.6 %collective-permute-start.2 = (f32[96,128]{1,0:T(8,128)S(1)}, f32[96,128]{1,0:T(8,128)S(1)}, u32[]{:S(2)}, u32[]{:S(2)}) collective-permute-start(f32[96,128]{1,0:T(8,128)S(1)} %get-tuple-element.87), channel_id=1, source_target_pairs={{0,225},{1,32},{2,227},{3,34},{4,229},{5,36},{6,231},{7,38},{32,1}... | collective-permute-start | bytes 147464 | tf_op jit(solution)/shard_map/ppermute | solution.py:540
  12.5 1.1 %copy-start.2 = (f32[12,128,128]{2,1,0:T(8,128)S(1)}, f32[12,128,128]{2,1,0:T(8,128)}, u32[]{:S(2)}) copy-start(f32[12,128,128]{2,1,0:T(8,128)} %refs_0_.3) | copy-start | bytes 2359300
  12.5 1.4 %copy-start.3 = (f32[12,128,128]{2,1,0:T(8,128)S(1)}, f32[12,128,128]{2,1,0:T(8,128)}, u32[]{:S(2)}) copy-start(f32[12,128,128]{2,1,0:T(8,128)} %refs_1_.3) | copy-start | bytes 2359300
  12.5 1.6 %copy-start.4 = (f32[12,128,128]{2,1,0:T(8,128)S(1)}, f32[12,128,128]{2,1,0:T(8,128)}, u32[]{:S(2)}) copy-start(f32[12,128,128]{2,1,0:T(8,128)} %refs_2_.3) | copy-start | bytes 2359300
  16.5 7.2 %collective-permute-start.5 = (f32[2,64,128]{2,1,0:T(8,128)S(1)}, f32[2,64,128]{2,1,0:T(8,128)S(1)}, u32[]{:S(2)}, u32[]{:S(2)}) collective-permute-start(f32[2,64,128]{2,1,0:T(8,128)S(1)} %get-tuple-element.92), channel_id=1, source_target_pairs={{0,2},{1,3},{2,4},{3,5},{4,6},{5,7},{6,0},{7,1},{8,10},{9,11},{10,... | collective-permute-start | bytes 196616 | tf_op jit(solution)/shard_map/ppermute | solution.py:553
  17.9 5.8 %collective-permute-start.7 = (f32[2,64,128]{2,1,0:T(8,128)S(1)}, f32[2,64,128]{2,1,0:T(8,128)S(1)}, u32[]{:S(2)}, u32[]{:S(2)}) collective-permute-start(f32[2,64,128]{2,1,0:T(8,128)S(1)} %get-tuple-element.94), channel_id=1, source_target_pairs={{0,6},{1,7},{2,0},{3,1},{4,2},{5,3},{6,4},{7,5},{8,14},{9,15},{10,... | collective-permute-start | bytes 196616 | tf_op jit(solution)/shard_map/ppermute | solution.py:554
  19.4 4.3 %collective-permute-start.6 = (f32[64,128]{1,0:T(8,128)S(1)}, f32[64,128]{1,0:T(8,128)S(1)}, u32[]{:S(2)}, u32[]{:S(2)}) collective-permute-start(f32[64,128]{1,0:T(8,128)S(1)} %get-tuple-element.93), channel_id=1, source_target_pairs={{0,4},{1,5},{2,6},{3,7},{4,0},{5,1},{6,2},{7,3},{8,12},{9,13},{10,... | collective-permute-start | bytes 98312 | tf_op jit(solution)/shard_map/ppermute | solution.py:552
  24.3 10.0 %collective-permute-start.8 = (f32[48,128]{1,0:T(8,128)S(1)}, f32[48,128]{1,0:T(8,128)S(1)}, u32[]{:S(2)}, u32[]{:S(2)}) collective-permute-start(f32[48,128]{1,0:T(8,128)S(1)} %get-tuple-element.103), channel_id=1, source_target_pairs={{0,1},{1,0},{2,3},{3,2},{4,5},{5,4},{6,7},{7,6},{8,9},{9,8},{10,11... | collective-permute-start | bytes 73736 | tf_op jit(solution)/shard_map/ppermute | solution.py:546
  30.0 4.3 %collective-permute-start.9 = (f32[48,128]{1,0:T(8,128)S(1)}, f32[48,128]{1,0:T(8,128)S(1)}, u32[]{:S(2)}, u32[]{:S(2)}) collective-permute-start(f32[48,128]{1,0:T(8,128)S(1)} %get-tuple-element.104), channel_id=1, source_target_pairs={{0,225},{1,32},{2,227},{3,34},{4,229},{5,36},{6,231},{7,38},{32,1}... | collective-permute-start | bytes 73736 | tf_op jit(solution)/shard_map/ppermute | solution.py:540
  30.0 4.3 %collective-permute-start.11 = (f32[48,128]{1,0:T(8,128)S(1)}, f32[48,128]{1,0:T(8,128)S(1)}, u32[]{:S(2)}, u32[]{:S(2)}) collective-permute-start(f32[48,128]{1,0:T(8,128)S(1)} %get-tuple-element.105.refs_11_), channel_id=1, source_target_pairs={{0,24},{8,0},{16,8},{24,16},{1,25},{9,1},{17,9},{25,17},{2,26},{10... | collective-permute-start | bytes 73736 | tf_op jit(solution)/shard_map/ppermute | solution.py:539
  32.6 3.9 %collective-permute-start.10 = (f32[48,128]{1,0:T(8,128)S(1)}, f32[48,128]{1,0:T(8,128)S(1)}, u32[]{:S(2)}, u32[]{:S(2)}) collective-permute-start(f32[48,128]{1,0:T(8,128)S(1)} %get-tuple-element.105.refs_11_), channel_id=1, source_target_pairs={{0,8},{8,16},{16,24},{24,0},{1,9},{9,17},{17,25},{25,1},{2,10},{10... | collective-permute-start | bytes 73736 | tf_op jit(solution)/shard_map/ppermute | solution.py:538
  37.3 7.3 %collective-permute-start.12 = (f32[2,64,128]{2,1,0:T(8,128)S(1)}, f32[2,64,128]{2,1,0:T(8,128)S(1)}, u32[]{:S(2)}, u32[]{:S(2)}) collective-permute-start(f32[2,64,128]{2,1,0:T(8,128)S(1)} %get-tuple-element.113), channel_id=1, source_target_pairs={{0,2},{1,3},{2,4},{3,5},{4,6},{5,7},{6,0},{7,1},{8,10},{9,11},{10,... | collective-permute-start | bytes 196616 | tf_op jit(solution)/shard_map/ppermute | solution.py:553
  37.4 7.2 %collective-permute-start.14 = (f32[2,64,128]{2,1,0:T(8,128)S(1)}, f32[2,64,128]{2,1,0:T(8,128)S(1)}, u32[]{:S(2)}, u32[]{:S(2)}) collective-permute-start(f32[2,64,128]{2,1,0:T(8,128)S(1)} %get-tuple-element.115), channel_id=1, source_target_pairs={{0,6},{1,7},{2,0},{3,1},{4,2},{5,3},{6,4},{7,5},{8,14},{9,15},{10,... | collective-permute-start | bytes 196616 | tf_op jit(solution)/shard_map/ppermute | solution.py:554
  40.0 4.6 %collective-permute-start.13 = (f32[64,128]{1,0:T(8,128)S(1)}, f32[64,128]{1,0:T(8,128)S(1)}, u32[]{:S(2)}, u32[]{:S(2)}) collective-permute-start(f32[64,128]{1,0:T(8,128)S(1)} %get-tuple-element.114), channel_id=1, source_target_pairs={{0,4},{1,5},{2,6},{3,7},{4,0},{5,1},{6,2},{7,3},{8,12},{9,13},{10,... | collective-permute-start | bytes 98312 | tf_op jit(solution)/shard_map/ppermute | solution.py:552
  45.2 7.9 %collective-permute-start.15 = (f32[48,128]{1,0:T(8,128)S(1)}, f32[48,128]{1,0:T(8,128)S(1)}, u32[]{:S(2)}, u32[]{:S(2)}) collective-permute-start(f32[48,128]{1,0:T(8,128)S(1)} %get-tuple-element.126), channel_id=1, source_target_pairs={{0,1},{1,0},{2,3},{3,2},{4,5},{5,4},{6,7},{7,6},{8,9},{9,8},{10,11... | collective-permute-start | bytes 73736 | tf_op jit(solution)/shard_map/ppermute | solution.py:546
  49.3 3.8 %collective-permute-start.16 = (f32[48,128]{1,0:T(8,128)S(1)}, f32[48,128]{1,0:T(8,128)S(1)}, u32[]{:S(2)}, u32[]{:S(2)}) collective-permute-start(f32[48,128]{1,0:T(8,128)S(1)} %get-tuple-element.127), channel_id=1, source_target_pairs={{0,225},{1,32},{2,227},{3,34},{4,229},{5,36},{6,231},{7,38},{32,1}... | collective-permute-start | bytes 73736 | tf_op jit(solution)/shard_map/ppermute | solution.py:540
  50.0 3.1 %collective-permute-start.18 = (f32[48,128]{1,0:T(8,128)S(1)}, f32[48,128]{1,0:T(8,128)S(1)}, u32[]{:S(2)}, u32[]{:S(2)}) collective-permute-start(f32[48,128]{1,0:T(8,128)S(1)} %get-tuple-element.128.refs_11_), channel_id=1, source_target_pairs={{0,24},{8,0},{16,8},{24,16},{1,25},{9,1},{17,9},{25,17},{2,26},{10... | collective-permute-start | bytes 73736 | tf_op jit(solution)/shard_map/ppermute | solution.py:539
  50.0 3.9 %collective-permute-start.17 = (f32[48,128]{1,0:T(8,128)S(1)}, f32[48,128]{1,0:T(8,128)S(1)}, u32[]{:S(2)}, u32[]{:S(2)}) collective-permute-start(f32[48,128]{1,0:T(8,128)S(1)} %get-tuple-element.128.refs_11_), channel_id=1, source_target_pairs={{0,8},{8,16},{16,24},{24,0},{1,9},{9,17},{17,25},{25,1},{2,10},{10... | collective-permute-start | bytes 73736 | tf_op jit(solution)/shard_map/ppermute | solution.py:538
  55.0 4.5 %collective-permute-start.19 = (f32[2,12,64,128]{3,2,1,0:T(8,128)S(1)}, f32[2,12,64,128]{3,2,1,0:T(8,128)S(1)}, u32[]{:S(2)}, u32[]{:S(2)}) collective-permute-start(f32[2,12,64,128]{3,2,1,0:T(8,128)S(1)} %get-tuple-element.136), channel_id=1, source_target_pairs={{0,1},{1,0},{2,3},{3,2},{4,5},{5,4},{6,7},{7,6},{8,9},{9,8},{10,11... | collective-permute-start | bytes 2359304 | tf_op jit(solution)/shard_map/ppermute | solution.py:559
  56.9 7.0 %collective-permute-start.20 = (f32[2,64,128]{2,1,0:T(8,128)S(1)}, f32[2,64,128]{2,1,0:T(8,128)S(1)}, u32[]{:S(2)}, u32[]{:S(2)}) collective-permute-start(f32[2,64,128]{2,1,0:T(8,128)S(1)} %get-tuple-element.142), channel_id=1, source_target_pairs={{0,2},{1,3},{2,4},{3,5},{4,6},{5,7},{6,0},{7,1},{8,10},{9,11},{10,... | collective-permute-start | bytes 196616 | tf_op jit(solution)/shard_map/ppermute | solution.py:553
  56.9 7.0 %collective-permute-start.22 = (f32[2,64,128]{2,1,0:T(8,128)S(1)}, f32[2,64,128]{2,1,0:T(8,128)S(1)}, u32[]{:S(2)}, u32[]{:S(2)}) collective-permute-start(f32[2,64,128]{2,1,0:T(8,128)S(1)} %get-tuple-element.144), channel_id=1, source_target_pairs={{0,6},{1,7},{2,0},{3,1},{4,2},{5,3},{6,4},{7,5},{8,14},{9,15},{10,... | collective-permute-start | bytes 196616 | tf_op jit(solution)/shard_map/ppermute | solution.py:554
  59.5 4.3 %collective-permute-start.21 = (f32[64,128]{1,0:T(8,128)S(1)}, f32[64,128]{1,0:T(8,128)S(1)}, u32[]{:S(2)}, u32[]{:S(2)}) collective-permute-start(f32[64,128]{1,0:T(8,128)S(1)} %get-tuple-element.143), channel_id=1, source_target_pairs={{0,4},{1,5},{2,6},{3,7},{4,0},{5,1},{6,2},{7,3},{8,12},{9,13},{10,... | collective-permute-start | bytes 98312 | tf_op jit(solution)/shard_map/ppermute | solution.py:552
  64.6 4.4 %collective-permute-start.23 = (f32[3,12,64,128]{3,2,1,0:T(8,128)S(1)}, f32[3,12,64,128]{3,2,1,0:T(8,128)S(1)}, u32[]{:S(2)}, u32[]{:S(2)}) collective-permute-start(f32[3,12,64,128]{3,2,1,0:T(8,128)S(1)} %get-tuple-element.147), channel_id=1, source_target_pairs={{0,1},{1,0},{2,3},{3,2},{4,5},{5,4},{6,7},{7,6},{8,9},{9,8},{10,11... | collective-permute-start | bytes 3538952 | tf_op jit(solution)/shard_map/ppermute | solution.py:564
where the time goes:
time: 70.7 us; the launch traced here: 70.5 us
  starting transfers between devices  35.1 us (50%)
  waiting for transfers between devices  17 us (24%)
  Pallas kernels  16 us (23%)
  between operations  1.06 us (1%)
  local copies, waits for them, and re-layouts  1.01 us (1%)
    pallas_call x15, Pallas kernels, call(): pl.pallas_call(body, out_shape=outs, in_specs=in_specs or [VMEM] * len(ar...  16 us
    ppermute x3, waiting for transfers between devices, local(): from_far = lax.ppermute(to_far, 'gz', along(2))  9.86 us
    ppermute x2, starting transfers between devices, local(): mid_in = lax.ppermute(mid, 'gz', swap)  9.72 us
    ppermute x3, starting transfers between devices, local(): from_next = lax.ppermute(to_prev, 'gz', along(3))  6.79 us
    ppermute x3, starting transfers between devices, local(): right = lax.ppermute(cols, 'gy', west_ring)  3.52 us
    ppermute x1, starting transfers between devices, local(): got_edges = lax.ppermute(give, 'gz', swap)  3.23 us
    ppermute x3, waiting for transfers between devices, local(): left = lax.ppermute(cols, 'gy', east_ring)  3 us
    ppermute x1, waiting for transfers between devices, local(): got_ver = lax.ppermute(send_ver, 'gz', swap)  2.47 us
  transfers between devices with their start and end apart: 24, of which 8 were waited for; matrix products, arithmetic and copies ran while one was open for 1% of the time, Pallas kernels for 9%

commit v1 on v0

--- a/solution.py
+++ b/solution.py
@@ -9,7 +9,7 @@
 
 
 ITERS = 3
-GRANT = 64800
+GRANT = 54800
 
 horiz_push = 0.25
 mass_flux = 0.2
@@ -69,16 +69,18 @@
     return pl.ds(pl.multiple_of(start, 8), 8)
 
 
-def pack_columns(tile_at, out, base, groups):
+def pack_columns(groups):
     lane = lanes()
-    for g in range(groups):
-        acc = jnp.zeros((8, LN), F32)
-        for j in range(4):
-            for t in range(TILES):
-                slot = 8 * j + t
-                moved = roll_lanes(tile_at(4 * g + j, t), 4 * slot - 126)
-                acc = jnp.where(lane // 4 == slot, moved, acc)
-        out[base + 8 * g : base + 8 * g + 8, :] = acc
+    packed = [jnp.zeros((8, LN), F32)] * len(groups)
+    for slot in range(4 * TILES):
+        j, t = divmod(slot, TILES)
+        here = lane // 4 == slot
+        packed = [
+            jnp.where(here, roll_lanes(tile_at(k + j, t), 4 * slot - 126), acc)
+            for acc, (tile_at, k, _, _) in zip(packed, groups)
+        ]
+    for acc, (_, _, out, row) in zip(packed, groups):
+        out[row : row + 8, :] = acc
 
 
 def pack_rows(tile_at, groups):
@@ -100,20 +102,22 @@
     core = core_of()
     ours = pl.ds(pl.multiple_of(core * RX, RX), RX)
     theirs = pl.ds(pl.multiple_of((1 - core) * RX, RX), RX)
-    copies = []
+    loads, stores = [], []
+
+    def store(f):
+        loads[f].wait()
+        source = whole.at[f, :, theirs, :] if f < 3 else part.at[f - 3]
+        stores.append(pltpu.make_async_copy(source, send.at[f], sem.at[5 + f]))
+        stores[-1].start()
+
     for f in range(5):
         if f < 3:
-            copy = pltpu.make_async_copy(ins[f], whole.at[f], sem.at[f])
+            loads.append(pltpu.make_async_copy(ins[f], whole.at[f], sem.at[f]))
         else:
-            copy = pltpu.make_async_copy(ins[f].at[:, theirs, :], part.at[f - 3], sem.at[f])
-        copy.start()
-        copies.append(copy)
-    for f in range(5):
-        copies[f].wait()
-        source = whole.at[f, :, theirs, :] if f < 3 else part.at[f - 3]
-        copy = pltpu.make_async_copy(source, send.at[f], sem.at[5 + f])
-        copy.start()
-        copies.append(copy)
+            loads.append(pltpu.make_async_copy(ins[f].at[:, theirs, :], part.at[f - 3], sem.at[f]))
+        loads[-1].start()
+    for f in range(3):
+        store(f)
 
     def half(f, which):
         def tile_at(k, t):
@@ -121,14 +125,23 @@
 
         return tile_at
 
-    for out, near in ((keep, core), (give, 1 - core)):
-        pack_columns(half(PRESS, near), out, 0, 3)
-        pack_columns(half(NORTH, near), out, PART, 3)
+    jobs = ((give, 1 - core), (keep, core))
+    for out, near in jobs:
         for part_at, (which, f) in enumerate(((near, PRESS), (near, EAST), (1 - near, PRESS), (1 - near, EAST))):
             for g, (first, last) in enumerate(zip(*pack_rows(half(f, which), 3))):
                 base = (2 + part_at) * PART + 8 * g
                 out[base : base + 8, :] = jnp.where(near == 0, first, last)
-    for copy in copies[5:]:
+    for f in range(3, 5):
+        store(f)
+    pack_columns(
+        [
+            (half(f, near), 4 * g, out, i * PART + 8 * g)
+            for out, near in jobs
+            for i, f in enumerate((PRESS, NORTH))
+            for g in range(3)
+        ]
+    )
+    for copy in stores:
         copy.wait()
 
 
@@ -159,30 +172,50 @@
                 out[at : at + PART, :] = jnp.where(core == piece, keep[part, :], got[part, :])
 
 
-def merge_kernel(count, own, got, *refs):
-    outs, sem = refs[:count], refs[-1]
-    if len(refs) > count + 1:
-        refs[count][...] = jnp.zeros((8, LN), F32)
+def winds_out_kernel(own, got, east, north, sem):
     core = core_of()
     copies = []
-    for f in range(count):
+    for f, out in enumerate((east, north)):
         for which, src in ((core, own), (1 - core, got)):
             rows = pl.ds(pl.multiple_of(which * RX, RX), RX)
-            copy = pltpu.make_async_copy(src.at[f], outs[f].at[:, rows, :], sem.at[len(copies)])
+            copy = pltpu.make_async_copy(src.at[f], out.at[:, rows, :], sem.at[len(copies)])
             copy.start()
             copies.append(copy)
     for copy in copies:
         copy.wait()
 
 
-def merge(own, got, token=False):
-    count = own.shape[0]
+def solved_out_kernel(own, got, got_wind, mass, wind, geo, press, fill, sem):
+    core = core_of()
+    copies = []
+
+    def write(source, out, which):
+        rows = pl.ds(pl.multiple_of(which * RX, RX), RX)
+        copies.append(pltpu.make_async_copy(source, out.at[:, rows, :], sem.at[len(copies)]))
+        copies[-1].start()
+
+    for f, out in enumerate((wind, geo, press)):
+        write(own.at[f], out, core)
+    write(got_wind.at[pl.ds(1, HALF)], wind, 1 - core)
+    flux = level_flux * mass[...]
+    for f, out in enumerate((geo, press)):
+        for k in range(HALF):
+            if f == 0:
+                fill[0, k] = got[2, k] + geo_rate * got_wind[k + 1]
+            else:
+                fill[1, k] = got[3, k] - flux * (got_wind[k + 2] - got_wind[k])
+        write(fill.at[f], out, 1 - core)
+    for copy in copies:
+        copy.wait()
+
+
+def write_out(body, count, scratch, *args):
     return call(
-        functools.partial(merge_kernel, count),
-        [shape(HALF, 2 * RX, LN)] * count + [shape(8, LN)] * token,
-        [own, got],
-        out_specs=[HBM] * count + [VMEM] * token,
-        scratch=[pltpu.SemaphoreType.DMA((2 * count,))],
+        body,
+        [shape(HALF, 2 * RX, LN)] * count,
+        args,
+        out_specs=[HBM] * count,
+        scratch=[*scratch, pltpu.SemaphoreType.DMA((2 * count,))],
     )
 
 
@@ -256,7 +289,7 @@
     )
 
 
-def heave_kernel(wind, geo, got, heave, geo_out):
+def heave_kernel(wind, geo, got, after, heave, geo_out):
     core = core_of()
     rows = pl.ds(pl.multiple_of(core * RX, RX), RX)
 
@@ -388,7 +421,7 @@
     (star, forced, geo, mass, rate, up, down, from_prev, from_far, from_next) = refs[:10]
     refs = refs[10:]
     if last:
-        (after, mine, theirs, sums, wind, geo_out, press) = refs
+        (mine, wind_theirs, sums, wind, geo_out, press) = refs
     else:
         (wind, press, mid, outer, cols, sums) = refs
     core, chip = core_of(), chip_of()
@@ -450,19 +483,20 @@
         for k in range(HALF):
             for f, (source, off) in enumerate(((wind, 1), (geo_out, 0), (press, 0))):
                 mine[f, k] = source[here + k + off]
-                theirs[f, k] = source[there + k + off]
+        for k in range(HALF + 2):
+            wind_theirs[k] = wind[there + k]
     else:
         for g, (first_rows, last_rows) in enumerate(zip(*pack_rows(tiles_of(press), LV // 4))):
             rows = slice(8 * g, 8 * g + 8)
             mid[rows, :] = jnp.where(core == 0, last_rows, first_rows)
             outer[rows, :] = jnp.where(core == 0, first_rows, last_rows)
-        pack_columns(tiles_of(press), cols, 0, LV // 4)
+        pack_columns([(tiles_of(press), 4 * g, cols, 8 * g) for g in range(LV // 4)])
 
 
 def solve(last, *args):
     edge, field, tall = shape(EDGE, LN), shape(LV, RX, LN), shape(LV + 2, RX, LN)
     if last:
-        outs = [shape(3, HALF, RX, LN)] * 2
+        outs = [shape(3, HALF, RX, LN), shape(HALF + 2, RX, LN)]
         scratch = [pltpu.VMEM(s.shape, F32) for s in (field, tall, field, field)]
     else:
         outs = [tall, field, edge, edge, edge]
@@ -470,7 +504,7 @@
     return call(functools.partial(solve_kernel, last), outs, args, scratch=scratch)
 
 
-def sort_winds_kernel(east, north, east_fix, north_fix, mine, theirs):
+def sort_kernel(east, north, east_fix, north_fix, geo, star, mine, theirs):
     core = core_of()
     lane = lanes()
     inner_lane = jnp.logical_or(lane == 0, lane == LN - 1)
@@ -492,6 +526,9 @@
                     n = n + jnp.where(inner_lane, roll_lanes(n_fix, 126 - 4 * (8 * j + t)), 0.0)
                     out[0, 4 * g + j, tile, :] = e
                     out[1, 4 * g + j, tile, :] = n
+                if out is theirs:
+                    out[2, 4 * g + j] = geo[k]
+                    out[3, 4 * g + j] = star[k]
         return carry
 
     lax.fori_loop(0, 3, group, 0)
@@ -541,7 +578,7 @@
         if first:
             mid_in = mid
             east, north, star, ends = inner(first, *fields[:3], got, mass)
-            heave, geo = call(heave_kernel, [field, field], [*fields[3:], got])
+            heave, geo = call(heave_kernel, [field, field], [*fields[3:], got, ends])
         else:
             mid_in = lax.ppermute(mid, "gz", swap)
             east, north, star, ends, heave, geo = inner(first, press, east, north, wind, geo, mass, east_fix)
@@ -554,16 +591,21 @@
         from_next = lax.ppermute(to_prev, "gz", along(3))
         args = [star, forced, geo, mass, rate, up, down, from_prev, from_far, from_next]
         if last:
-            half = shape(2, HALF, RX, LN)
-            own_hor, send_hor = call(sort_winds_kernel, [half, half], [east, north, east_fix, north_fix])
-            got_hor = lax.ppermute(send_hor, "gz", swap)
-            east_after, north_after, written = merge(own_hor, got_hor, token=True)
-            own_ver, send_ver = solve(last, *args, written)
+            own_part, send_part = call(
+                sort_kernel,
+                [shape(2, HALF, RX, LN), shape(4, HALF, RX, LN)],
+                [east, north, east_fix, north_fix, geo, star],
+            )
+            got_part = lax.ppermute(send_part, "gz", swap)
+            solved, send_solved = solve(last, *args)
+            got_solved = lax.ppermute(send_solved, "gz", swap)
+            winds_after = write_out(winds_out_kernel, 2, (), own_part, got_part)
+            other = lax.dynamic_slice_in_dim(column_mass, (1 - core) * RX, RX, 0)
+            fill = pltpu.VMEM((2, HALF, RX, LN), F32)
+            solved_after = write_out(solved_out_kernel, 3, (fill,), solved, got_part, got_solved, other)
         else:
             wind, press, mid, outer, cols = solve(last, *args)
-    got_ver = lax.ppermute(send_ver, "gz", swap)
-    vertical_after, geo_after, pressure_after = merge(own_ver, got_ver)
-    return east_after, north_after, vertical_after, geo_after, pressure_after
+    return *winds_after, *solved_after
 
 
 def solution(mesh):

time: 70.7 us -> 71.9 us (1.017)
  local copies, waits for them, and re-layouts: 1.01 us -> 3.05 us
  waiting for transfers between devices: 17 us -> 15.6 us
  Pallas kernels: 16 us -> 15.1 us
  other arithmetic: 0.39 us -> 1.23 us
    ppermute x2, waiting for transfers between devices: 2.48 us -> 0.27 us  [the longest x1 0.26 us: local(): got_solved = lax.ppermute(send_solved, 'gz', swap)]
    unnamed x14 -> x18, local copies, waits for them, and re-layouts: 1.01 us -> 3.05 us
    ppermute x2, starting transfers between devices: 9.72 us -> 10.9 us  [local(): mid_in = lax.ppermute(mid, 'gz', swap)]
    pallas_call x15, Pallas kernels: 16 us -> 15.1 us  [call(): pl.pallas_call(body, out_shape=outs, in_specs=in_specs or [VMEM] * len(ar...]
    ppermute x3, waiting for transfers between devices: 9.86 us -> 10.8 us  [local(): from_far = lax.ppermute(to_far, 'gz', along(2))]
    log x1, other arithmetic: 0.03 us -> 0.87 us  [local(): log_ratio = jnp.log(ratio)]
    ppermute x3, starting transfers between devices: 1.99 us -> 1.27 us  [local(): outer_in = lax.ppermute(outer, ('gx', 'gz'), outward)]
  transfers between devices with their start and end apart: 24 -> 24, of which waited for: 8 -> 9; matrix products, arithmetic and copies ran while one was open for 1% -> 2% of each run, Pallas kernels for 9% -> 10%
where the time goes in v1:
time: 71.9 us; the launch traced here: 71.7 us
  starting transfers between devices  35.7 us (50%)
  waiting for transfers between devices  15.6 us (22%)
  Pallas kernels  15.1 us (21%)
  local copies, waits for them, and re-layouts  3.05 us (4%)
  other arithmetic  1.23 us (2%)
  between operations  1.04 us (1%)
    pallas_call x15, Pallas kernels, call(): pl.pallas_call(body, out_shape=outs, in_specs=in_specs or [VMEM] * len(ar...  15.1 us
    ppermute x2, starting transfers between devices, local(): mid_in = lax.ppermute(mid, 'gz', swap)  10.9 us
    ppermute x3, waiting for transfers between devices, local(): from_far = lax.ppermute(to_far, 'gz', along(2))  10.8 us
    ppermute x3, starting transfers between devices, local(): from_next = lax.ppermute(to_prev, 'gz', along(3))  6.79 us
    ppermute x3, starting transfers between devices, local(): right = lax.ppermute(cols, 'gy', west_ring)  3.52 us
    ppermute x1, starting transfers between devices, local(): got_edges = lax.ppermute(give, 'gz', swap)  3.15 us
    ppermute x3, waiting for transfers between devices, local(): left = lax.ppermute(cols, 'gy', east_ring)  3.14 us
    unnamed x18, local copies, waits for them, and re-layouts  3.05 us
  transfers between devices with their start and end apart: 24, of which 9 were waited for; matrix products, arithmetic and copies ran while one was open for 2% of the time, Pallas kernels for 10%

profile of v1, /device:TPU:1, one launch (start us, length us, event | category | flops | bytes accessed | tf_op | source)
XLA Modules:
  0.0 71.7 jit_solution(6346058955015088041)
XLA Ops:
  0.6 2.9 %shard_map.101 = (f32[5,12,64,128]{3,2,1,0:T(8,128)}, f32[144,128]{1,0:T(8,128)S(1)}, f32[144,128]{1,0:T(8,128)S(1)}) custom-call(f32[12,128,128]{2,1,0:T(8,128)} %refs_0_.3, f32[12,128,128]{2,1,0:T(8,128)} %refs_1_.3, f32[12,128,128]{2,1,0:T(8,128)} %refs_2_.3, f32[12,128,128]{2,1,0:T(8,128)} %wind.1, f32[12,128,128]{2,1,0:T(8,128)} %geo.1), custom_call_target="tpu_custom_call" | custom-call | flops 4000000 | bytes 1000000 | tf_op jit(solution)/shard_map/pallas_call | solution.py:41
  3.5 0.0 copy-start.5
  3.5 0.6 copy-done.5
  4.2 3.1 %collective-permute-start = (f32[144,128]{1,0:T(8,128)S(1)}, f32[144,128]{1,0:T(8,128)S(1)}, u32[]{:S(2)}, u32[]{:S(2)}) collective-permute-start(f32[144,128]{1,0:T(8,128)S(1)} %get-tuple-element.78), channel_id=1, source_target_pairs={{0,1},{1,0},{2,3},{3,2},{4,5},{5,4},{6,7},{7,6},{8,9},{9,8},{10,11... | collective-permute-start | bytes 221192 | tf_op jit(solution)/shard_map/ppermute | solution.py:555
  7.3 0.9 %collective-permute-done.got = f32[144,128]{1,0:T(8,128)S(1)} collective-permute-done((f32[144,128]{1,0:T(8,128)S(1)}, f32[144,128]{1,0:T(8,128)S(1)}, u32[]{:S(2)}, u32[]{:S(2)}) %collective-permute-start) | collective-permute-done | bytes 73760 | tf_op jit(solution)/shard_map/ppermute | solution.py:555
  8.2 0.6 copy-done.7
  8.8 0.4 collective-permute-start.1
  9.2 0.9 %fusion.1 = (f32[64,128]{1,0:T(8,128)S(1)}, f32[64,128]{1,0:T(8,128)S(1)}, f32[64,128]{1,0:T(8,128)S(1)}) fusion(f32[128,128]{1,0:T(8,128)} %param.11, s32[]{:T(128)S(6)} %select_n.6, s32[]{:T(128)S(6)} %select_n.7), kind=kLoop, calls=%fused_computation.9 | loop fusion | flops 49152 | bytes 163848 | tf_op jit(solution)/shard_map/log | solution.py:565
  10.1 0.1 fusion.2
  10.1 0.3 exponential_subtract_fusion
  10.4 0.0 copy-start.6
  10.5 0.9 %copy-done.6 = f32[144,128]{1,0:T(8,128)S(1)} copy-done((f32[144,128]{1,0:T(8,128)S(1)}, f32[144,128]{1,0:T(8,128)}, u32[]{:S(2)}) %copy-start.6) | copy-done | bytes 73752
  11.3 0.9 %copy-done.8 = f32[144,128]{1,0:T(8,128)S(1)} copy-done((f32[144,128]{1,0:T(8,128)S(1)}, f32[144,128]{1,0:T(8,128)}, u32[]{:S(2)}) %copy-start.8) | copy-done | bytes 73752
  12.2 0.8 %collective-permute-start.4 = (f32[96,128]{1,0:T(8,128)S(1)}, f32[96,128]{1,0:T(8,128)S(1)}, u32[]{:S(2)}, u32[]{:S(2)}) collective-permute-start(f32[96,128]{1,0:T(8,128)S(1)} %get-tuple-element.87.refs_11_), channel_id=1, source_target_pairs={{0,24},{8,0},{16,8},{24,16},{1,25},{9,1},{17,9},{25,17},{2,26},{10... | collective-permute-start | bytes 147464 | tf_op jit(solution)/shard_map/ppermute | solution.py:576
  13.1 0.7 collective-permute-start.3
  13.8 1.3 %collective-permute-start.2 = (f32[96,128]{1,0:T(8,128)S(1)}, f32[96,128]{1,0:T(8,128)S(1)}, u32[]{:S(2)}, u32[]{:S(2)}) collective-permute-start(f32[96,128]{1,0:T(8,128)S(1)} %get-tuple-element.86), channel_id=1, source_target_pairs={{0,225},{1,32},{2,227},{3,34},{4,229},{5,36},{6,231},{7,38},{32,1}... | collective-permute-start | bytes 147464 | tf_op jit(solution)/shard_map/ppermute | solution.py:577
  15.1 0.0 copy-start
  15.1 0.0 copy-start.1
  15.1 0.0 collective-permute-done.1.refs_3_.got
  15.1 1.6 %shard_map.102 = (f32[24,64,128]{2,1,0:T(8,128)S(1)}, f32[24,64,128]{2,1,0:T(8,128)S(1)}, f32[24,64,128]{2,1,0:T(8,128)S(1)}, f32[48,128]{1,0:T(8,128)S(1)}) custom-call(f32[12,128,128]{2,1,0:T(8,128)S(1)} %copy-done.2, f32[12,128,128]{2,1,0:T(8,128)S(1)} %copy-done.3, f32[12,128,128]{2,1,0:T(8,128)S(1)} %copy-done.4, ...), custom_call_target="tpu_custom_call" | custom-call | flops 4000000 | bytes 1000000 | tf_op jit(solution)/shard_map/pallas_call | solution.py:41
  16.7 0.2 shard_map.103
  16.9 0.4 collective-permute-done.2.refs_8_
  17.3 0.0 collective-permute-done.4.refs_10_
  17.3 0.0 collective-permute-done.3.refs_9_
  17.3 0.7 shard_map.105
  18.0 1.3 %collective-permute-start.5 = (f32[2,64,128]{2,1,0:T(8,128)S(1)}, f32[2,64,128]{2,1,0:T(8,128)S(1)}, u32[]{:S(2)}, u32[]{:S(2)}) collective-permute-start(f32[2,64,128]{2,1,0:T(8,128)S(1)} %get-tuple-element.91), channel_id=1, source_target_pairs={{0,2},{1,3},{2,4},{3,5},{4,6},{5,7},{6,0},{7,1},{8,10},{9,11},{10,... | collective-permute-start | bytes 196616 | tf_op jit(solution)/shard_map/ppermute | solution.py:590
  19.3 1.5 %collective-permute-start.7 = (f32[2,64,128]{2,1,0:T(8,128)S(1)}, f32[2,64,128]{2,1,0:T(8,128)S(1)}, u32[]{:S(2)}, u32[]{:S(2)}) collective-permute-start(f32[2,64,128]{2,1,0:T(8,128)S(1)} %get-tuple-element.93), channel_id=1, source_target_pairs={{0,6},{1,7},{2,0},{3,1},{4,2},{5,3},{6,4},{7,5},{8,14},{9,15},{10,... | collective-permute-start | bytes 196616 | tf_op jit(solution)/shard_map/ppermute | solution.py:591
  20.9 1.6 %collective-permute-start.6 = (f32[64,128]{1,0:T(8,128)S(1)}, f32[64,128]{1,0:T(8,128)S(1)}, u32[]{:S(2)}, u32[]{:S(2)}) collective-permute-start(f32[64,128]{1,0:T(8,128)S(1)} %get-tuple-element.92), channel_id=1, source_target_pairs={{0,4},{1,5},{2,6},{3,7},{4,0},{5,1},{6,2},{7,3},{8,12},{9,13},{10,... | collective-permute-start | bytes 98312 | tf_op jit(solution)/shard_map/ppermute | solution.py:589
  22.4 2.7 %collective-permute-done.6.refs_8_ = f32[64,128]{1,0:T(8,128)S(1)} collective-permute-done((f32[64,128]{1,0:T(8,128)S(1)}, f32[64,128]{1,0:T(8,128)S(1)}, u32[]{:S(2)}, u32[]{:S(2)}) %collective-permute-start.6) | collective-permute-done | bytes 32800 | tf_op jit(solution)/shard_map/ppermute | solution.py:589
  25.1 0.0 collective-permute-done.5.refs_7_
  25.1 0.0 collective-permute-done.7.refs_9_
  25.1 0.6 shard_map.106
  25.8 5.4 %collective-permute-start.8 = (f32[48,128]{1,0:T(8,128)S(1)}, f32[48,128]{1,0:T(8,128)S(1)}, u32[]{:S(2)}, u32[]{:S(2)}) collective-permute-start(f32[48,128]{1,0:T(8,128)S(1)} %get-tuple-element.102), channel_id=1, source_target_pairs={{0,1},{1,0},{2,3},{3,2},{4,5},{5,4},{6,7},{7,6},{8,9},{9,8},{10,11... | collective-permute-start | bytes 73736 | tf_op jit(solution)/shard_map/ppermute | solution.py:583
  31.2 0.0 collective-permute-start.9
  31.2 2.7 %collective-permute-start.11 = (f32[48,128]{1,0:T(8,128)S(1)}, f32[48,128]{1,0:T(8,128)S(1)}, u32[]{:S(2)}, u32[]{:S(2)}) collective-permute-start(f32[48,128]{1,0:T(8,128)S(1)} %get-tuple-element.104.refs_11_), channel_id=1, source_target_pairs={{0,24},{8,0},{16,8},{24,16},{1,25},{9,1},{17,9},{25,17},{2,26},{10... | collective-permute-start | bytes 73736 | tf_op jit(solution)/shard_map/ppermute | solution.py:576
  33.8 1.6 %shard_map.107 = (f32[24,64,128]{2,1,0:T(8,128)S(1)}, f32[24,64,128]{2,1,0:T(8,128)S(1)}, f32[24,64,128]{2,1,0:T(8,128)S(1)}, f32[48,128]{1,0:T(8,128)S(1)}, f32...) custom-call(f32[24,64,128]{2,1,0:T(8,128)S(1)} %get-tuple-element.94.refs_0_, ...), custom_call_target="tpu_custom_call" | custom-call | flops 4000000 | bytes 1000000 | tf_op jit(solution)/shard_map/pallas_call | solution.py:41
  35.5 0.0 collective-permute-done.8.refs_7_
  35.5 2.2 %collective-permute-done.10.refs_9_ = f32[48,128]{1,0:T(8,128)S(1)} collective-permute-done((f32[48,128]{1,0:T(8,128)S(1)}, f32[48,128]{1,0:T(8,128)S(1)}, u32[]{:S(2)}, u32[]{:S(2)}) %collective-permute-start.10) | collective-permute-done | bytes 24608 | tf_op jit(solution)/shard_map/ppermute | solution.py:575
  37.7 0.7 shard_map.108
  38.5 0.2 collective-permute-start.12
  38.6 2.6 %collective-permute-start.14 = (f32[2,64,128]{2,1,0:T(8,128)S(1)}, f32[2,64,128]{2,1,0:T(8,128)S(1)}, u32[]{:S(2)}, u32[]{:S(2)}) collective-permute-start(f32[2,64,128]{2,1,0:T(8,128)S(1)} %get-tuple-element.114), channel_id=1, source_target_pairs={{0,6},{1,7},{2,0},{3,1},{4,2},{5,3},{6,4},{7,5},{8,14},{9,15},{10,... | collective-permute-start | bytes 196616 | tf_op jit(solution)/shard_map/ppermute | solution.py:591
  41.2 0.5 collective-permute-start.13
  41.7 3.8 %collective-permute-done.13.refs_8_ = f32[64,128]{1,0:T(8,128)S(1)} collective-permute-done((f32[64,128]{1,0:T(8,128)S(1)}, f32[64,128]{1,0:T(8,128)S(1)}, u32[]{:S(2)}, u32[]{:S(2)}) %collective-permute-start.13) | collective-permute-done | bytes 32800 | tf_op jit(solution)/shard_map/ppermute | solution.py:589
  45.5 0.7 shard_map.109
  46.2 5.6 %collective-permute-start.15 = (f32[48,128]{1,0:T(8,128)S(1)}, f32[48,128]{1,0:T(8,128)S(1)}, u32[]{:S(2)}, u32[]{:S(2)}) collective-permute-start(f32[48,128]{1,0:T(8,128)S(1)} %get-tuple-element.125), channel_id=1, source_target_pairs={{0,1},{1,0},{2,3},{3,2},{4,5},{5,4},{6,7},{7,6},{8,9},{9,8},{10,11... | collective-permute-start | bytes 73736 | tf_op jit(solution)/shard_map/ppermute | solution.py:583
  51.7 0.0 collective-permute-start.16
  51.7 0.0 collective-permute-start.18
  51.7 1.5 %collective-permute-start.17 = (f32[48,128]{1,0:T(8,128)S(1)}, f32[48,128]{1,0:T(8,128)S(1)}, u32[]{:S(2)}, u32[]{:S(2)}) collective-permute-start(f32[48,128]{1,0:T(8,128)S(1)} %get-tuple-element.127.refs_11_), channel_id=1, source_target_pairs={{0,8},{8,16},{16,24},{24,0},{1,9},{9,17},{17,25},{25,1},{2,10},{10... | collective-permute-start | bytes 73736 | tf_op jit(solution)/shard_map/ppermute | solution.py:575
  53.2 1.6 %shard_map.110 = (f32[24,64,128]{2,1,0:T(8,128)S(1)}, f32[24,64,128]{2,1,0:T(8,128)S(1)}, f32[24,64,128]{2,1,0:T(8,128)S(1)}, f32[48,128]{1,0:T(8,128)S(1)}, f32...) custom-call(f32[24,64,128]{2,1,0:T(8,128)S(1)} %get-tuple-element.115.refs_0_, ...), custom_call_target="tpu_custom_call" | custom-call | flops 4000000 | bytes 1000000 | tf_op jit(solution)/shard_map/pallas_call | solution.py:41
  54.8 0.0 collective-permute-done.15.refs_7_
  54.8 0.1 collective-permute-done.16.refs_8_
  55.0 0.9 %collective-permute-done.17.refs_9_ = f32[48,128]{1,0:T(8,128)S(1)} collective-permute-done((f32[48,128]{1,0:T(8,128)S(1)}, f32[48,128]{1,0:T(8,128)S(1)}, u32[]{:S(2)}, u32[]{:S(2)}) %collective-permute-start.17) | collective-permute-done | bytes 24608 | tf_op jit(solution)/shard_map/ppermute | solution.py:575
  55.9 0.7 shard_map.111
  56.6 0.4 shard_map.112
  57.0 2.1 %collective-permute-start.19 = (f32[4,12,64,128]{3,2,1,0:T(8,128)S(1)}, f32[4,12,64,128]{3,2,1,0:T(8,128)S(1)}, u32[]{:S(2)}, u32[]{:S(2)}) collective-permute-start(f32[4,12,64,128]{3,2,1,0:T(8,128)S(1)} %get-tuple-element.137), channel_id=1, source_target_pairs={{0,1},{1,0},{2,3},{3,2},{4,5},{5,4},{6,7},{7,6},{8,9},{9,8},{10,11... | collective-permute-start | bytes 4718600 | tf_op jit(solution)/shard_map/ppermute | solution.py:599
  59.1 0.0 collective-permute-start.20
  59.1 2.7 %collective-permute-start.22 = (f32[2,64,128]{2,1,0:T(8,128)S(1)}, f32[2,64,128]{2,1,0:T(8,128)S(1)}, u32[]{:S(2)}, u32[]{:S(2)}) collective-permute-start(f32[2,64,128]{2,1,0:T(8,128)S(1)} %get-tuple-element.143), channel_id=1, source_target_pairs={{0,6},{1,7},{2,0},{3,1},{4,2},{5,3},{6,4},{7,5},{8,14},{9,15},{10,... | collective-permute-start | bytes 196616 | tf_op jit(solution)/shard_map/ppermute | solution.py:591
  61.8 4.3 %collective-permute-done.21.refs_8_ = f32[64,128]{1,0:T(8,128)S(1)} collective-permute-done((f32[64,128]{1,0:T(8,128)S(1)}, f32[64,128]{1,0:T(8,128)S(1)}, u32[]{:S(2)}, u32[]{:S(2)}) %collective-permute-start.21) | collective-permute-done | bytes 32800 | tf_op jit(solution)/shard_map/ppermute | solution.py:589
  66.1 0.7 shard_map.114
  66.8 1.9 %collective-permute-start.23 = (f32[14,64,128]{2,1,0:T(8,128)S(1)}, f32[14,64,128]{2,1,0:T(8,128)S(1)}, u32[]{:S(2)}, u32[]{:S(2)}) collective-permute-start(f32[14,64,128]{2,1,0:T(8,128)S(1)} %get-tuple-element.145), channel_id=1, source_target_pairs={{0,1},{1,0},{2,3},{3,2},{4,5},{5,4},{6,7},{7,6},{8,9},{9,8},{10,11... | collective-permute-start | bytes 1376264 | tf_op jit(solution)/shard_map/ppermute | solution.py:601
  68.7 0.0 collective-permute-done.19.got
  68.7 1.2 %shard_map.113 = (f32[12,128,128]{2,1,0:T(8,128)}, f32[12,128,128]{2,1,0:T(8,128)}) custom-call(f32[2,12,64,128]{3,2,1,0:T(8,128)S(1)} %get-tuple-element.136.own, f32[4,12,64,128]{3,2,1,0:T(8,128)S(1)} %collective-permute-done.19.got), custom_call_target="tpu_custom_call" | custom-call | flops 4000000 | bytes 1000000 | tf_op jit(solution)/shard_map/pallas_call | solution.py:41
  69.9 0.3 collective-permute-done.23.got_wind
  70.1 1.5 %shard_map.115 = (f32[12,128,128]{2,1,0:T(8,128)}, f32[12,128,128]{2,1,0:T(8,128)}, f32[12,128,128]{2,1,0:T(8,128)}) custom-call(f32[3,12,64,128]{3,2,1,0:T(8,128)S(1)} %get-tuple-element.144.own, f32[4,12,64,128]{3,2,1,0:T(8,128)S(1)} %collective-permute-done.19.got, f32[14,64,128]{2,1,0:T(8,128)S(1)} %collective-permute-done.23.got_wind, ...), custom_call_target="tpu_custom_call" | custom-call | flops 4000000 | bytes 1000000 | tf_op jit(solution)/shard_map/pallas_call | solution.py:41
  (22 shorter events, 0.1 us)
Async XLA Ops:
  3.5 0.6 copy-start.5
  4.1 10.9 %copy-start.2 = (f32[12,128,128]{2,1,0:T(8,128)S(1)}, f32[12,128,128]{2,1,0:T(8,128)}, u32[]{:S(2)}) copy-start(f32[12,128,128]{2,1,0:T(8,128)} %refs_0_.3) | copy-start | bytes 2359300
  4.2 11.0 %copy-start.3 = (f32[12,128,128]{2,1,0:T(8,128)S(1)}, f32[12,128,128]{2,1,0:T(8,128)}, u32[]{:S(2)}) copy-start(f32[12,128,128]{2,1,0:T(8,128)} %refs_1_.3) | copy-start | bytes 2359300
  4.2 4.1 %collective-permute-start = (f32[144,128]{1,0:T(8,128)S(1)}, f32[144,128]{1,0:T(8,128)S(1)}, u32[]{:S(2)}, u32[]{:S(2)}) collective-permute-start(f32[144,128]{1,0:T(8,128)S(1)} %get-tuple-element.78), channel_id=1, source_target_pairs={{0,1},{1,0},{2,3},{3,2},{4,5},{5,4},{6,7},{7,6},{8,9},{9,8},{10,11... | collective-permute-start | bytes 221192 | tf_op jit(solution)/shard_map/ppermute | solution.py:555
  8.2 0.6 copy-start.7
  8.8 6.2 %collective-permute-start.1 = (f32[5,12,64,128]{3,2,1,0:T(8,128)}, f32[5,12,64,128]{3,2,1,0:T(8,128)S(1)}, u32[]{:S(2)}, u32[]{:S(2)}) collective-permute-start(f32[5,12,64,128]{3,2,1,0:T(8,128)} %get-tuple-element.79), channel_id=1, source_target_pairs={{0,1},{1,0},{2,3},{3,2},{4,5},{5,4},{6,7},{7,6},{8,9},{9,8},{10,11... | collective-permute-start | bytes 5898248 | tf_op jit(solution)/shard_map/ppermute | solution.py:558
  9.2 5.9 %copy-start.4 = (f32[12,128,128]{2,1,0:T(8,128)S(1)}, f32[12,128,128]{2,1,0:T(8,128)}, u32[]{:S(2)}) copy-start(f32[12,128,128]{2,1,0:T(8,128)} %refs_2_.3) | copy-start | bytes 2359300
  10.4 0.9 %copy-start.6 = (f32[144,128]{1,0:T(8,128)S(1)}, f32[144,128]{1,0:T(8,128)}, u32[]{:S(2)}) copy-start(f32[144,128]{1,0:T(8,128)} %copy-done.5) | copy-start | bytes 221188
  11.3 0.9 %copy-start.8 = (f32[144,128]{1,0:T(8,128)S(1)}, f32[144,128]{1,0:T(8,128)}, u32[]{:S(2)}) copy-start(f32[144,128]{1,0:T(8,128)} %copy-done.7) | copy-start | bytes 221188
  12.2 5.1 %collective-permute-start.4 = (f32[96,128]{1,0:T(8,128)S(1)}, f32[96,128]{1,0:T(8,128)S(1)}, u32[]{:S(2)}, u32[]{:S(2)}) collective-permute-start(f32[96,128]{1,0:T(8,128)S(1)} %get-tuple-element.87.refs_11_), channel_id=1, source_target_pairs={{0,24},{8,0},{16,8},{24,16},{1,25},{9,1},{17,9},{25,17},{2,26},{10... | collective-permute-start | bytes 147464 | tf_op jit(solution)/shard_map/ppermute | solution.py:576
  13.1 4.2 %collective-permute-start.3 = (f32[96,128]{1,0:T(8,128)S(1)}, f32[96,128]{1,0:T(8,128)S(1)}, u32[]{:S(2)}, u32[]{:S(2)}) collective-permute-start(f32[96,128]{1,0:T(8,128)S(1)} %get-tuple-element.87.refs_11_), channel_id=1, source_target_pairs={{0,8},{8,16},{16,24},{24,0},{1,9},{9,17},{17,25},{25,1},{2,10},{10... | collective-permute-start | bytes 147464 | tf_op jit(solution)/shard_map/ppermute | solution.py:575
  13.8 3.5 %collective-permute-start.2 = (f32[96,128]{1,0:T(8,128)S(1)}, f32[96,128]{1,0:T(8,128)S(1)}, u32[]{:S(2)}, u32[]{:S(2)}) collective-permute-start(f32[96,128]{1,0:T(8,128)S(1)} %get-tuple-element.86), channel_id=1, source_target_pairs={{0,225},{1,32},{2,227},{3,34},{4,229},{5,36},{6,231},{7,38},{32,1}... | collective-permute-start | bytes 147464 | tf_op jit(solution)/shard_map/ppermute | solution.py:577
  15.1 1.7 %copy-start = (f32[12,128,128]{2,1,0:T(8,128)S(1)}, f32[12,128,128]{2,1,0:T(8,128)}, u32[]{:S(2)}) copy-start(f32[12,128,128]{2,1,0:T(8,128)} %wind.1) | copy-start | bytes 2359300
  15.1 1.7 %copy-start.1 = (f32[12,128,128]{2,1,0:T(8,128)S(1)}, f32[12,128,128]{2,1,0:T(8,128)}, u32[]{:S(2)}) copy-start(f32[12,128,128]{2,1,0:T(8,128)} %geo.1) | copy-start | bytes 2359300
  18.0 7.1 %collective-permute-start.5 = (f32[2,64,128]{2,1,0:T(8,128)S(1)}, f32[2,64,128]{2,1,0:T(8,128)S(1)}, u32[]{:S(2)}, u32[]{:S(2)}) collective-permute-start(f32[2,64,128]{2,1,0:T(8,128)S(1)} %get-tuple-element.91), channel_id=1, source_target_pairs={{0,2},{1,3},{2,4},{3,5},{4,6},{5,7},{6,0},{7,1},{8,10},{9,11},{10,... | collective-permute-start | bytes 196616 | tf_op jit(solution)/shard_map/ppermute | solution.py:590
  19.3 5.8 %collective-permute-start.7 = (f32[2,64,128]{2,1,0:T(8,128)S(1)}, f32[2,64,128]{2,1,0:T(8,128)S(1)}, u32[]{:S(2)}, u32[]{:S(2)}) collective-permute-start(f32[2,64,128]{2,1,0:T(8,128)S(1)} %get-tuple-element.93), channel_id=1, source_target_pairs={{0,6},{1,7},{2,0},{3,1},{4,2},{5,3},{6,4},{7,5},{8,14},{9,15},{10,... | collective-permute-start | bytes 196616 | tf_op jit(solution)/shard_map/ppermute | solution.py:591
  20.9 4.3 %collective-permute-start.6 = (f32[64,128]{1,0:T(8,128)S(1)}, f32[64,128]{1,0:T(8,128)S(1)}, u32[]{:S(2)}, u32[]{:S(2)}) collective-permute-start(f32[64,128]{1,0:T(8,128)S(1)} %get-tuple-element.92), channel_id=1, source_target_pairs={{0,4},{1,5},{2,6},{3,7},{4,0},{5,1},{6,2},{7,3},{8,12},{9,13},{10,... | collective-permute-start | bytes 98312 | tf_op jit(solution)/shard_map/ppermute | solution.py:589
  25.8 9.7 %collective-permute-start.8 = (f32[48,128]{1,0:T(8,128)S(1)}, f32[48,128]{1,0:T(8,128)S(1)}, u32[]{:S(2)}, u32[]{:S(2)}) collective-permute-start(f32[48,128]{1,0:T(8,128)S(1)} %get-tuple-element.102), channel_id=1, source_target_pairs={{0,1},{1,0},{2,3},{3,2},{4,5},{5,4},{6,7},{7,6},{8,9},{9,8},{10,11... | collective-permute-start | bytes 73736 | tf_op jit(solution)/shard_map/ppermute | solution.py:583
  31.2 4.3 %collective-permute-start.9 = (f32[48,128]{1,0:T(8,128)S(1)}, f32[48,128]{1,0:T(8,128)S(1)}, u32[]{:S(2)}, u32[]{:S(2)}) collective-permute-start(f32[48,128]{1,0:T(8,128)S(1)} %get-tuple-element.103), channel_id=1, source_target_pairs={{0,225},{1,32},{2,227},{3,34},{4,229},{5,36},{6,231},{7,38},{32,1}... | collective-permute-start | bytes 73736 | tf_op jit(solution)/shard_map/ppermute | solution.py:577
  31.2 4.3 %collective-permute-start.11 = (f32[48,128]{1,0:T(8,128)S(1)}, f32[48,128]{1,0:T(8,128)S(1)}, u32[]{:S(2)}, u32[]{:S(2)}) collective-permute-start(f32[48,128]{1,0:T(8,128)S(1)} %get-tuple-element.104.refs_11_), channel_id=1, source_target_pairs={{0,24},{8,0},{16,8},{24,16},{1,25},{9,1},{17,9},{25,17},{2,26},{10... | collective-permute-start | bytes 73736 | tf_op jit(solution)/shard_map/ppermute | solution.py:576
  33.8 3.9 %collective-permute-start.10 = (f32[48,128]{1,0:T(8,128)S(1)}, f32[48,128]{1,0:T(8,128)S(1)}, u32[]{:S(2)}, u32[]{:S(2)}) collective-permute-start(f32[48,128]{1,0:T(8,128)S(1)} %get-tuple-element.104.refs_11_), channel_id=1, source_target_pairs={{0,8},{8,16},{16,24},{24,0},{1,9},{9,17},{17,25},{25,1},{2,10},{10... | collective-permute-start | bytes 73736 | tf_op jit(solution)/shard_map/ppermute | solution.py:575
  38.5 7.0 %collective-permute-start.12 = (f32[2,64,128]{2,1,0:T(8,128)S(1)}, f32[2,64,128]{2,1,0:T(8,128)S(1)}, u32[]{:S(2)}, u32[]{:S(2)}) collective-permute-start(f32[2,64,128]{2,1,0:T(8,128)S(1)} %get-tuple-element.112), channel_id=1, source_target_pairs={{0,2},{1,3},{2,4},{3,5},{4,6},{5,7},{6,0},{7,1},{8,10},{9,11},{10,... | collective-permute-start | bytes 196616 | tf_op jit(solution)/shard_map/ppermute | solution.py:590
  38.6 6.9 %collective-permute-start.14 = (f32[2,64,128]{2,1,0:T(8,128)S(1)}, f32[2,64,128]{2,1,0:T(8,128)S(1)}, u32[]{:S(2)}, u32[]{:S(2)}) collective-permute-start(f32[2,64,128]{2,1,0:T(8,128)S(1)} %get-tuple-element.114), channel_id=1, source_target_pairs={{0,6},{1,7},{2,0},{3,1},{4,2},{5,3},{6,4},{7,5},{8,14},{9,15},{10,... | collective-permute-start | bytes 196616 | tf_op jit(solution)/shard_map/ppermute | solution.py:591
  41.2 4.3 %collective-permute-start.13 = (f32[64,128]{1,0:T(8,128)S(1)}, f32[64,128]{1,0:T(8,128)S(1)}, u32[]{:S(2)}, u32[]{:S(2)}) collective-permute-start(f32[64,128]{1,0:T(8,128)S(1)} %get-tuple-element.113), channel_id=1, source_target_pairs={{0,4},{1,5},{2,6},{3,7},{4,0},{5,1},{6,2},{7,3},{8,12},{9,13},{10,... | collective-permute-start | bytes 98312 | tf_op jit(solution)/shard_map/ppermute | solution.py:589
  46.2 8.7 %collective-permute-start.15 = (f32[48,128]{1,0:T(8,128)S(1)}, f32[48,128]{1,0:T(8,128)S(1)}, u32[]{:S(2)}, u32[]{:S(2)}) collective-permute-start(f32[48,128]{1,0:T(8,128)S(1)} %get-tuple-element.125), channel_id=1, source_target_pairs={{0,1},{1,0},{2,3},{3,2},{4,5},{5,4},{6,7},{7,6},{8,9},{9,8},{10,11... | collective-permute-start | bytes 73736 | tf_op jit(solution)/shard_map/ppermute | solution.py:583
  51.7 3.3 %collective-permute-start.16 = (f32[48,128]{1,0:T(8,128)S(1)}, f32[48,128]{1,0:T(8,128)S(1)}, u32[]{:S(2)}, u32[]{:S(2)}) collective-permute-start(f32[48,128]{1,0:T(8,128)S(1)} %get-tuple-element.126), channel_id=1, source_target_pairs={{0,225},{1,32},{2,227},{3,34},{4,229},{5,36},{6,231},{7,38},{32,1}... | collective-permute-start | bytes 73736 | tf_op jit(solution)/shard_map/ppermute | solution.py:577
  51.7 3.3 %collective-permute-start.18 = (f32[48,128]{1,0:T(8,128)S(1)}, f32[48,128]{1,0:T(8,128)S(1)}, u32[]{:S(2)}, u32[]{:S(2)}) collective-permute-start(f32[48,128]{1,0:T(8,128)S(1)} %get-tuple-element.127.refs_11_), channel_id=1, source_target_pairs={{0,24},{8,0},{16,8},{24,16},{1,25},{9,1},{17,9},{25,17},{2,26},{10... | collective-permute-start | bytes 73736 | tf_op jit(solution)/shard_map/ppermute | solution.py:576
  51.7 4.2 %collective-permute-start.17 = (f32[48,128]{1,0:T(8,128)S(1)}, f32[48,128]{1,0:T(8,128)S(1)}, u32[]{:S(2)}, u32[]{:S(2)}) collective-permute-start(f32[48,128]{1,0:T(8,128)S(1)} %get-tuple-element.127.refs_11_), channel_id=1, source_target_pairs={{0,8},{8,16},{16,24},{24,0},{1,9},{9,17},{17,25},{25,1},{2,10},{10... | collective-permute-start | bytes 73736 | tf_op jit(solution)/shard_map/ppermute | solution.py:575
  57.0 11.6 %collective-permute-start.19 = (f32[4,12,64,128]{3,2,1,0:T(8,128)S(1)}, f32[4,12,64,128]{3,2,1,0:T(8,128)S(1)}, u32[]{:S(2)}, u32[]{:S(2)}) collective-permute-start(f32[4,12,64,128]{3,2,1,0:T(8,128)S(1)} %get-tuple-element.137), channel_id=1, source_target_pairs={{0,1},{1,0},{2,3},{3,2},{4,5},{5,4},{6,7},{7,6},{8,9},{9,8},{10,11... | collective-permute-start | bytes 4718600 | tf_op jit(solution)/shard_map/ppermute | solution.py:599
  59.1 7.0 %collective-permute-start.20 = (f32[2,64,128]{2,1,0:T(8,128)S(1)}, f32[2,64,128]{2,1,0:T(8,128)S(1)}, u32[]{:S(2)}, u32[]{:S(2)}) collective-permute-start(f32[2,64,128]{2,1,0:T(8,128)S(1)} %get-tuple-element.141), channel_id=1, source_target_pairs={{0,2},{1,3},{2,4},{3,5},{4,6},{5,7},{6,0},{7,1},{8,10},{9,11},{10,... | collective-permute-start | bytes 196616 | tf_op jit(solution)/shard_map/ppermute | solution.py:590
  59.1 7.0 %collective-permute-start.22 = (f32[2,64,128]{2,1,0:T(8,128)S(1)}, f32[2,64,128]{2,1,0:T(8,128)S(1)}, u32[]{:S(2)}, u32[]{:S(2)}) collective-permute-start(f32[2,64,128]{2,1,0:T(8,128)S(1)} %get-tuple-element.143), channel_id=1, source_target_pairs={{0,6},{1,7},{2,0},{3,1},{4,2},{5,3},{6,4},{7,5},{8,14},{9,15},{10,... | collective-permute-start | bytes 196616 | tf_op jit(solution)/shard_map/ppermute | solution.py:591
  61.8 4.3 %collective-permute-start.21 = (f32[64,128]{1,0:T(8,128)S(1)}, f32[64,128]{1,0:T(8,128)S(1)}, u32[]{:S(2)}, u32[]{:S(2)}) collective-permute-start(f32[64,128]{1,0:T(8,128)S(1)} %get-tuple-element.142), channel_id=1, source_target_pairs={{0,4},{1,5},{2,6},{3,7},{4,0},{5,1},{6,2},{7,3},{8,12},{9,13},{10,... | collective-permute-start | bytes 98312 | tf_op jit(solution)/shard_map/ppermute | solution.py:589
  66.8 3.3 %collective-permute-start.23 = (f32[14,64,128]{2,1,0:T(8,128)S(1)}, f32[14,64,128]{2,1,0:T(8,128)S(1)}, u32[]{:S(2)}, u32[]{:S(2)}) collective-permute-start(f32[14,64,128]{2,1,0:T(8,128)S(1)} %get-tuple-element.145), channel_id=1, source_target_pairs={{0,1},{1,0},{2,3},{3,2},{4,5},{5,4},{6,7},{7,6},{8,9},{9,8},{10,11... | collective-permute-start | bytes 1376264 | tf_op jit(solution)/shard_map/ppermute | solution.py:601

commit v2 on v1

--- a/solution.py
+++ b/solution.py
@@ -305,16 +305,17 @@
 
 
 def rim_kernel(first, last, *refs):
-    (star_in, heave, ends, mass, rate, up, down, mid, outer, left, right, own_cols) = refs[:12]
+    (star_in, heave, ends, mass, rate, up, down, mid, outer, across, around, own_cols) = refs[:12]
     refs = refs[12:]
     if not first:
         (north_fix_in, east_edge, north_own, north_edge), refs = refs[:4], refs[4:]
-    (star, forced, to_next, to_far, to_prev, east_fix, north_fix) = refs[:7]
+    (star, forced, to_across, to_far, to_around, east_fix, north_fix) = refs[:7]
     if not last:
         east_edge_out, north_own_out, north_edge_out = refs[7:]
     core, chip = core_of(), chip_of()
     lane = lanes()
     quarter = lane % 4
+    second = (quarter < 2) == (lax.rem(lax.axis_index("gy"), 2) == 0)
     rim_lane = jnp.logical_or(lane < 2, lane >= LN - 2)
     row = lax.broadcasted_iota(jnp.int32, (8, LN), 0)
     odd = row % 2 == 1
@@ -325,7 +326,7 @@
         more = slice(EDGE + 8 * g, EDGE + 8 * g + 8)
         p_low = jnp.where(core == 0, outer[rows, :], mid[rows, :])
         p_high = jnp.where(core == 0, mid[rows, :], outer[rows, :])
-        p_edge = jnp.where(quarter < 2, left[rows, :], right[rows, :])
+        p_edge = jnp.where(second, around[rows, :], across[rows, :])
         p_own = own_cols[rows, :]
         if first:
             e_edge = jnp.where(
@@ -333,7 +334,7 @@
                 jnp.where(core == 0, outer[more, :], mid[more, :]),
                 jnp.where(core == 0, mid[more, :], outer[more, :]),
             )
-            n_own, n_edge = own_cols[more, :], jnp.where(quarter < 2, left[more, :], right[more, :])
+            n_own, n_edge = own_cols[more, :], jnp.where(second, around[more, :], across[more, :])
         else:
             e_edge, n_own, n_edge = east_edge[rows, :], north_own[rows, :], north_edge[rows, :]
         own_up, own_down = roll_lanes(p_own, -1), roll_lanes(p_own, 1)
@@ -401,11 +402,13 @@
             power = rho if k == 0 else power * rho
         total = total + inv * up[LV + 1, tile, :] * top
         tail = tail + power * (down[LV + 1, tile, :] * top)
-        to_next[0, tile, :] = jnp.where(chip < 3, total, tail)
-        to_next[1, tile, :] = top
-        to_far[tile, :] = jnp.where(chip < 2, total, tail)
-        to_prev[0, tile, :] = jnp.where(chip > 0, tail, total)
-        to_prev[1, tile, :] = bottom
+        even = lax.rem(chip, 2) == 0
+        low = chip < 2
+        to_across[0, tile, :] = jnp.where(even, total, tail)
+        to_across[1, tile, :] = jnp.where(even, top, bottom)
+        to_around[0, tile, :] = jnp.where(low, total, tail)
+        to_around[1, tile, :] = jnp.where(low, top, bottom)
+        to_far[tile, :] = jnp.where(low, total, tail)
 
 
 def rim(first, last, *args):
@@ -418,7 +421,7 @@
 
 
 def solve_kernel(last, *refs):
-    (star, forced, geo, mass, rate, up, down, from_prev, from_far, from_next) = refs[:10]
+    (star, forced, geo, mass, rate, up, down, from_across, from_far, from_around) = refs[:10]
     refs = refs[10:]
     if last:
         (mine, wind_theirs, sums, wind, geo_out, press) = refs
@@ -430,20 +433,14 @@
         tile = slice(8 * t, 8 * t + 8)
         ratio, inverse, deep, scale = (rate[i, tile, :] for i in range(4))
         zero = jnp.zeros((8, LN), F32)
-        prev, far, after = from_prev[0, tile, :], from_far[tile, :], from_next[0, tile, :]
-        star_under = jnp.where(chip > 0, from_prev[1, tile, :], zero)
-        star_over = jnp.where(chip < 3, from_next[1, tile, :], zero)
-        far_deep = deep * far
-        enter = jnp.where(
-            chip == 0,
-            zero,
-            prev + jnp.where(chip >= 2, far_deep, zero) + jnp.where(chip == 3, deep * deep * after, zero),
-        )
-        above = jnp.where(
-            chip == 3,
-            zero,
-            after + jnp.where(chip <= 1, far_deep, zero) + jnp.where(chip == 0, deep * deep * prev, zero),
-        )
+        near, far, turn = from_across[0, tile, :], deep * from_far[tile, :], from_around[0, tile, :]
+        even = lax.rem(chip, 2) == 0
+        star_near, star_turn = from_across[1, tile, :], from_around[1, tile, :]
+        star_under = jnp.where(even, jnp.where(chip == 2, star_turn, zero), star_near)
+        star_over = jnp.where(even, star_near, jnp.where(chip == 1, star_turn, zero))
+        turn = jnp.where((chip == 0) | (chip == 3), deep * deep * turn, turn)
+        enter = jnp.where(even, zero, near) + jnp.where(chip >= 2, far + turn, zero)
+        above = jnp.where(even, near, zero) + jnp.where(chip <= 1, far + turn, zero)
         enter = enter - inverse * up[1, tile, :] * star_under - up[0, tile, :] * (scale * star[0, tile, :])
         above = above + inverse * down[LV, tile, :] * star_over + down[LV + 1, tile, :] * (scale * star[LV - 1, tile, :])
 
@@ -539,16 +536,18 @@
     core, chip = core_of(), chip_of()
     swap = [(i, i ^ 1) for i in range(pieces)]
 
-    def along(distance):
-        return [(i, (i + 2 * distance) % pieces) for i in range(pieces)]
-
+    across_chip = [(i, i ^ 2) for i in range(pieces)]
+    around_chip = [(i, (pieces // 2 - 1 - i // 2) * 2 + i % 2) for i in range(pieces)]
+    far_chip = [(i, (i + 4) % pieces) for i in range(pieces)]
     outward = [
         (a * pieces + z, (a + (1 if z % 2 else -1)) % columns * pieces + (z ^ 1))
         for a in range(columns)
         for z in range(pieces)
     ]
-    east_ring = [(i, (i + 1) % tiles) for i in range(tiles)]
-    west_ring = [(i, (i - 1) % tiles) for i in range(tiles)]
+    across_tile = [(i, i ^ 1) for i in range(tiles)]
+    around_tile = [(i, tiles - 1 - i) for i in range(tiles)]
+    if tiles != 4 or pieces != 8:
+        raise ValueError("sizes")
 
     fields = (pressure, east_wind, north_wind, vertical_wind, geopotential)
     send, keep, give = split(*fields)
@@ -572,8 +571,8 @@
     field = shape(LV, RX, LN)
     for substep in range(ITERS):
         first, last = substep == 0, substep == ITERS - 1
-        left = lax.ppermute(cols, "gy", east_ring)
-        right = lax.ppermute(cols, "gy", west_ring)
+        across = lax.ppermute(cols, "gy", across_tile)
+        around = lax.ppermute(cols, "gy", around_tile)
         outer_in = lax.ppermute(outer, ("gx", "gz"), outward)
         if first:
             mid_in = mid
@@ -582,14 +581,14 @@
         else:
             mid_in = lax.ppermute(mid, "gz", swap)
             east, north, star, ends, heave, geo = inner(first, press, east, north, wind, geo, mass, east_fix)
-        args = [star, heave, ends, mass, rate, up, down, mid_in, outer_in, left, right, cols]
+        args = [star, heave, ends, mass, rate, up, down, mid_in, outer_in, across, around, cols]
         if not first:
             args += [north_fix, *edges]
-        star, forced, to_next, to_far, to_prev, east_fix, north_fix, *edges = rim(first, last, *args)
-        from_far = lax.ppermute(to_far, "gz", along(2))
-        from_prev = lax.ppermute(to_next, "gz", along(1))
-        from_next = lax.ppermute(to_prev, "gz", along(3))
-        args = [star, forced, geo, mass, rate, up, down, from_prev, from_far, from_next]
+        star, forced, to_across, to_far, to_around, east_fix, north_fix, *edges = rim(first, last, *args)
+        from_far = lax.ppermute(to_far, "gz", far_chip)
+        from_across = lax.ppermute(to_across, "gz", across_chip)
+        from_around = lax.ppermute(to_around, "gz", around_chip)
+        args = [star, forced, geo, mass, rate, up, down, from_across, from_far, from_around]
         if last:
             own_part, send_part = call(
                 sort_kernel,

time: 71.9 us -> 68.9 us (0.958)
  waiting for transfers between devices: 15.6 us -> 12.4 us
    ppermute x15, waiting for transfers between devices: 13.9 us -> 10.9 us  [the longest x3 8.98 us: local(): from_far = lax.ppermute(to_far, 'gz', far_chip)]
    ppermute x15, starting transfers between devices: 16 us -> 14.9 us  [the longest x3 4.28 us: local(): from_around = lax.ppermute(to_around, 'gz', around_chip)]
    ppermute x3, starting transfers between devices: 1.27 us -> 2.19 us  [local(): outer_in = lax.ppermute(outer, ('gx', 'gz'), outward)]
  transfers between devices with their start and end apart: 24 -> 24, of which waited for: 9 -> 10; matrix products, arithmetic and copies ran while one was open for 2% -> 2% of each run, Pallas kernels for 10% -> 10%
where the time goes in v2:
time: 68.9 us; the launch traced here: 68.7 us
  starting transfers between devices  35.9 us (52%)
  Pallas kernels  15.1 us (22%)
  waiting for transfers between devices  12.4 us (18%)
  local copies, waits for them, and re-layouts  3.05 us (4%)
  other arithmetic  1.23 us (2%)
  between operations  1.03 us (1%)
    pallas_call x15, Pallas kernels, call(): pl.pallas_call(body, out_shape=outs, in_specs=in_specs or [VMEM] * len(ar...  15.1 us
    ppermute x2, starting transfers between devices, local(): mid_in = lax.ppermute(mid, 'gz', swap)  10.7 us
    ppermute x3, waiting for transfers between devices, local(): from_far = lax.ppermute(to_far, 'gz', far_chip)  8.98 us
    ppermute x3, starting transfers between devices, local(): from_around = lax.ppermute(to_around, 'gz', around_chip)  4.28 us
    ppermute x3, starting transfers between devices, local(): from_far = lax.ppermute(to_far, 'gz', far_chip)  3.82 us
    ppermute x3, starting transfers between devices, local(): around = lax.ppermute(cols, 'gy', around_tile)  3.4 us
    ppermute x1, starting transfers between devices, local(): got_edges = lax.ppermute(give, 'gz', swap)  3.2 us
    unnamed x18, local copies, waits for them, and re-layouts  3.05 us
  transfers between devices with their start and end apart: 24, of which 10 were waited for; matrix products, arithmetic and copies ran while one was open for 2% of the time, Pallas kernels for 10%

profile of v2, /device:TPU:1, one launch (start us, length us, event | category | flops | bytes accessed | tf_op | source)
XLA Modules:
  0.0 68.7 jit_solution(3159241898966157679)
XLA Ops:
  0.6 2.8 %shard_map.101 = (f32[5,12,64,128]{3,2,1,0:T(8,128)}, f32[144,128]{1,0:T(8,128)S(1)}, f32[144,128]{1,0:T(8,128)S(1)}) custom-call(f32[12,128,128]{2,1,0:T(8,128)} %refs_0_.3, f32[12,128,128]{2,1,0:T(8,128)} %refs_1_.3, f32[12,128,128]{2,1,0:T(8,128)} %refs_2_.3, f32[12,128,128]{2,1,0:T(8,128)} %wind.1, f32[12,128,128]{2,1,0:T(8,128)} %geo.1), custom_call_target="tpu_custom_call" | custom-call | flops 4000000 | bytes 1000000 | tf_op jit(solution)/shard_map/pallas_call | solution.py:41
  3.4 0.0 copy-start.5
  3.4 0.6 copy-done.5
  4.1 3.2 %collective-permute-start = (f32[144,128]{1,0:T(8,128)S(1)}, f32[144,128]{1,0:T(8,128)S(1)}, u32[]{:S(2)}, u32[]{:S(2)}) collective-permute-start(f32[144,128]{1,0:T(8,128)S(1)} %get-tuple-element.78), channel_id=1, source_target_pairs={{0,1},{1,0},{2,3},{3,2},{4,5},{5,4},{6,7},{7,6},{8,9},{9,8},{10,11... | collective-permute-start | bytes 221192 | tf_op jit(solution)/shard_map/ppermute | solution.py:554
  7.3 0.9 %collective-permute-done.got = f32[144,128]{1,0:T(8,128)S(1)} collective-permute-done((f32[144,128]{1,0:T(8,128)S(1)}, f32[144,128]{1,0:T(8,128)S(1)}, u32[]{:S(2)}, u32[]{:S(2)}) %collective-permute-start) | collective-permute-done | bytes 73760 | tf_op jit(solution)/shard_map/ppermute | solution.py:554
  8.2 0.6 copy-done.7
  8.8 0.4 collective-permute-start.1
  9.2 0.9 %fusion.1 = (f32[64,128]{1,0:T(8,128)S(1)}, f32[64,128]{1,0:T(8,128)S(1)}, f32[64,128]{1,0:T(8,128)S(1)}) fusion(f32[128,128]{1,0:T(8,128)} %param.11, s32[]{:T(128)S(6)} %select_n.6, s32[]{:T(128)S(6)} %select_n.7), kind=kLoop, calls=%fused_computation.9 | loop fusion | flops 49152 | bytes 163848 | tf_op jit(solution)/shard_map/log | solution.py:564
  10.0 0.1 fusion.2
  10.1 0.3 exponential_subtract_fusion
  10.4 0.0 copy-start.6
  10.4 0.9 %copy-done.6 = f32[144,128]{1,0:T(8,128)S(1)} copy-done((f32[144,128]{1,0:T(8,128)S(1)}, f32[144,128]{1,0:T(8,128)}, u32[]{:S(2)}) %copy-start.6) | copy-done | bytes 73752
  11.3 0.9 %copy-done.8 = f32[144,128]{1,0:T(8,128)S(1)} copy-done((f32[144,128]{1,0:T(8,128)S(1)}, f32[144,128]{1,0:T(8,128)}, u32[]{:S(2)}) %copy-start.8) | copy-done | bytes 73752
  12.2 0.9 %collective-permute-start.4 = (f32[96,128]{1,0:T(8,128)S(1)}, f32[96,128]{1,0:T(8,128)S(1)}, u32[]{:S(2)}, u32[]{:S(2)}) collective-permute-start(f32[96,128]{1,0:T(8,128)S(1)} %get-tuple-element.87.refs_11_), channel_id=1, source_target_pairs={{0,24},{8,16},{16,8},{24,0},{1,25},{9,17},{17,9},{25,1},{2,26},{10... | collective-permute-start | bytes 147464 | tf_op jit(solution)/shard_map/ppermute | solution.py:575
  13.1 2.2 %collective-permute-start.2 = (f32[96,128]{1,0:T(8,128)S(1)}, f32[96,128]{1,0:T(8,128)S(1)}, u32[]{:S(2)}, u32[]{:S(2)}) collective-permute-start(f32[96,128]{1,0:T(8,128)S(1)} %get-tuple-element.86), channel_id=1, source_target_pairs={{0,225},{1,32},{2,227},{3,34},{4,229},{5,36},{6,231},{7,38},{32,1}... | collective-permute-start | bytes 147464 | tf_op jit(solution)/shard_map/ppermute | solution.py:576
  15.2 0.0 copy-start
  15.3 0.0 copy-start.1
  15.3 0.0 collective-permute-done.1.refs_3_.got
  15.3 1.6 %shard_map.102 = (f32[24,64,128]{2,1,0:T(8,128)S(1)}, f32[24,64,128]{2,1,0:T(8,128)S(1)}, f32[24,64,128]{2,1,0:T(8,128)S(1)}, f32[48,128]{1,0:T(8,128)S(1)}) custom-call(f32[12,128,128]{2,1,0:T(8,128)S(1)} %copy-done.2, f32[12,128,128]{2,1,0:T(8,128)S(1)} %copy-done.3, f32[12,128,128]{2,1,0:T(8,128)S(1)} %copy-done.4, ...), custom_call_target="tpu_custom_call" | custom-call | flops 4000000 | bytes 1000000 | tf_op jit(solution)/shard_map/pallas_call | solution.py:41
  16.9 0.2 shard_map.103
  17.1 0.2 collective-permute-done.2.refs_8_
  17.3 0.0 collective-permute-done.4.refs_10_
  17.3 0.7 %shard_map.105 = (f32[24,64,128]{2,1,0:T(8,128)S(1)}, f32[24,64,128]{2,1,0:T(8,128)S(1)}, f32[2,64,128]{2,1,0:T(8,128)S(1)}, f32[64,128]{1,0:T(8,128)S(1)}, f32[...) custom-call(f32[24,64,128]{2,1,0:T(8,128)S(1)} %get-tuple-element.80, ...), custom_call_target="tpu_custom_call" | custom-call | flops 4000000 | bytes 1000000 | tf_op jit(solution)/shard_map/pallas_call | solution.py:41
  18.0 1.3 %collective-permute-start.5 = (f32[2,64,128]{2,1,0:T(8,128)S(1)}, f32[2,64,128]{2,1,0:T(8,128)S(1)}, u32[]{:S(2)}, u32[]{:S(2)}) collective-permute-start(f32[2,64,128]{2,1,0:T(8,128)S(1)} %get-tuple-element.91), channel_id=1, source_target_pairs={{0,2},{1,3},{2,0},{3,1},{4,6},{5,7},{6,4},{7,5},{8,10},{9,11},{10,... | collective-permute-start | bytes 196616 | tf_op jit(solution)/shard_map/ppermute | solution.py:589
  19.3 1.9 %collective-permute-start.7 = (f32[2,64,128]{2,1,0:T(8,128)S(1)}, f32[2,64,128]{2,1,0:T(8,128)S(1)}, u32[]{:S(2)}, u32[]{:S(2)}) collective-permute-start(f32[2,64,128]{2,1,0:T(8,128)S(1)} %get-tuple-element.93), channel_id=1, source_target_pairs={{0,6},{1,7},{2,4},{3,5},{4,2},{5,3},{6,0},{7,1},{8,14},{9,15},{10,... | collective-permute-start | bytes 196616 | tf_op jit(solution)/shard_map/ppermute | solution.py:590
  21.2 0.7 %collective-permute-start.6 = (f32[64,128]{1,0:T(8,128)S(1)}, f32[64,128]{1,0:T(8,128)S(1)}, u32[]{:S(2)}, u32[]{:S(2)}) collective-permute-start(f32[64,128]{1,0:T(8,128)S(1)} %get-tuple-element.92), channel_id=1, source_target_pairs={{0,4},{1,5},{2,6},{3,7},{4,0},{5,1},{6,2},{7,3},{8,12},{9,13},{10,... | collective-permute-start | bytes 98312 | tf_op jit(solution)/shard_map/ppermute | solution.py:588
  21.9 3.5 %collective-permute-done.6.refs_8_ = f32[64,128]{1,0:T(8,128)S(1)} collective-permute-done((f32[64,128]{1,0:T(8,128)S(1)}, f32[64,128]{1,0:T(8,128)S(1)}, u32[]{:S(2)}, u32[]{:S(2)}) %collective-permute-start.6) | collective-permute-done | bytes 32800 | tf_op jit(solution)/shard_map/ppermute | solution.py:588
  25.5 0.0 collective-permute-done.5.refs_7_
  25.5 0.0 collective-permute-done.7.refs_9_
  25.5 0.7 shard_map.106
  26.1 5.5 %collective-permute-start.8 = (f32[48,128]{1,0:T(8,128)S(1)}, f32[48,128]{1,0:T(8,128)S(1)}, u32[]{:S(2)}, u32[]{:S(2)}) collective-permute-start(f32[48,128]{1,0:T(8,128)S(1)} %get-tuple-element.102), channel_id=1, source_target_pairs={{0,1},{1,0},{2,3},{3,2},{4,5},{5,4},{6,7},{7,6},{8,9},{9,8},{10,11... | collective-permute-start | bytes 73736 | tf_op jit(solution)/shard_map/ppermute | solution.py:582
  31.7 0.0 collective-permute-start.9
  31.7 0.8 %collective-permute-start.11 = (f32[48,128]{1,0:T(8,128)S(1)}, f32[48,128]{1,0:T(8,128)S(1)}, u32[]{:S(2)}, u32[]{:S(2)}) collective-permute-start(f32[48,128]{1,0:T(8,128)S(1)} %get-tuple-element.104.refs_11_), channel_id=1, source_target_pairs={{0,24},{8,16},{16,8},{24,0},{1,25},{9,17},{17,9},{25,1},{2,26},{10... | collective-permute-start | bytes 73736 | tf_op jit(solution)/shard_map/ppermute | solution.py:575
  32.5 0.7 collective-permute-start.10
  33.2 1.6 %shard_map.107 = (f32[24,64,128]{2,1,0:T(8,128)S(1)}, f32[24,64,128]{2,1,0:T(8,128)S(1)}, f32[24,64,128]{2,1,0:T(8,128)S(1)}, f32[48,128]{1,0:T(8,128)S(1)}, f32...) custom-call(f32[24,64,128]{2,1,0:T(8,128)S(1)} %get-tuple-element.94.refs_0_, ...), custom_call_target="tpu_custom_call" | custom-call | flops 4000000 | bytes 1000000 | tf_op jit(solution)/shard_map/pallas_call | solution.py:41
  34.8 0.0 collective-permute-done.8.refs_7_
  34.8 0.1 collective-permute-done.9.refs_8_
  34.9 0.9 %collective-permute-done.11.refs_10_ = f32[48,128]{1,0:T(8,128)S(1)} collective-permute-done((f32[48,128]{1,0:T(8,128)S(1)}, f32[48,128]{1,0:T(8,128)S(1)}, u32[]{:S(2)}, u32[]{:S(2)}) %collective-permute-start.11) | collective-permute-done | bytes 24608 | tf_op jit(solution)/shard_map/ppermute | solution.py:575
  35.9 0.0 collective-permute-done.10.refs_9_
  35.9 0.7 %shard_map.108 = (f32[24,64,128]{2,1,0:T(8,128)S(1)}, f32[24,64,128]{2,1,0:T(8,128)S(1)}, f32[2,64,128]{2,1,0:T(8,128)S(1)}, f32[64,128]{1,0:T(8,128)S(1)}, f32[...) custom-call(f32[24,64,128]{2,1,0:T(8,128)S(1)} %get-tuple-element.99, ...), custom_call_target="tpu_custom_call" | custom-call | flops 4000000 | bytes 1000000 | tf_op jit(solution)/shard_map/pallas_call | solution.py:41
  36.6 0.5 collective-permute-start.12
  37.1 0.5 collective-permute-start.14
  37.6 2.4 %collective-permute-start.13 = (f32[64,128]{1,0:T(8,128)S(1)}, f32[64,128]{1,0:T(8,128)S(1)}, u32[]{:S(2)}, u32[]{:S(2)}) collective-permute-start(f32[64,128]{1,0:T(8,128)S(1)} %get-tuple-element.113), channel_id=1, source_target_pairs={{0,4},{1,5},{2,6},{3,7},{4,0},{5,1},{6,2},{7,3},{8,12},{9,13},{10,... | collective-permute-start | bytes 98312 | tf_op jit(solution)/shard_map/ppermute | solution.py:588
  39.9 1.9 %collective-permute-done.13.refs_8_ = f32[64,128]{1,0:T(8,128)S(1)} collective-permute-done((f32[64,128]{1,0:T(8,128)S(1)}, f32[64,128]{1,0:T(8,128)S(1)}, u32[]{:S(2)}, u32[]{:S(2)}) %collective-permute-start.13) | collective-permute-done | bytes 32800 | tf_op jit(solution)/shard_map/ppermute | solution.py:588
  41.8 0.0 collective-permute-done.12.refs_7_
  41.8 0.7 %shard_map.109 = (f32[26,64,128]{2,1,0:T(8,128)S(1)}, f32[24,64,128]{2,1,0:T(8,128)S(1)}, f32[48,128]{1,0:T(8,128)S(1)}, f32[48,128]{1,0:T(8,128)S(1)}, f32[48,128]{1,0:T(8,128)S(1)}) custom-call(f32[24,64,128]{2,1,0:T(8,128)S(1)} %get-tuple-element.109.refs_0_, f32[24,64,128]{2,1,0:T(8,128)S(1)} %get-tuple-element.110.refs_1_, ...), custom_call_target="tpu_custom_call" | custom-call | flops 4000000 | bytes 1000000 | tf_op jit(solution)/shard_map/pallas_call | solution.py:41
  42.5 5.1 %collective-permute-start.15 = (f32[48,128]{1,0:T(8,128)S(1)}, f32[48,128]{1,0:T(8,128)S(1)}, u32[]{:S(2)}, u32[]{:S(2)}) collective-permute-start(f32[48,128]{1,0:T(8,128)S(1)} %get-tuple-element.125), channel_id=1, source_target_pairs={{0,1},{1,0},{2,3},{3,2},{4,5},{5,4},{6,7},{7,6},{8,9},{9,8},{10,11... | collective-permute-start | bytes 73736 | tf_op jit(solution)/shard_map/ppermute | solution.py:582
  47.7 1.7 %collective-permute-start.18 = (f32[48,128]{1,0:T(8,128)S(1)}, f32[48,128]{1,0:T(8,128)S(1)}, u32[]{:S(2)}, u32[]{:S(2)}) collective-permute-start(f32[48,128]{1,0:T(8,128)S(1)} %get-tuple-element.127.refs_11_), channel_id=1, source_target_pairs={{0,24},{8,16},{16,8},{24,0},{1,25},{9,17},{17,9},{25,1},{2,26},{10... | collective-permute-start | bytes 73736 | tf_op jit(solution)/shard_map/ppermute | solution.py:575
  49.4 0.1 collective-permute-start.17
  49.5 1.6 %shard_map.110 = (f32[24,64,128]{2,1,0:T(8,128)S(1)}, f32[24,64,128]{2,1,0:T(8,128)S(1)}, f32[24,64,128]{2,1,0:T(8,128)S(1)}, f32[48,128]{1,0:T(8,128)S(1)}, f32...) custom-call(f32[24,64,128]{2,1,0:T(8,128)S(1)} %get-tuple-element.115.refs_0_, ...), custom_call_target="tpu_custom_call" | custom-call | flops 4000000 | bytes 1000000 | tf_op jit(solution)/shard_map/pallas_call | solution.py:41
  51.1 0.7 %collective-permute-done.18.refs_10_ = f32[48,128]{1,0:T(8,128)S(1)} collective-permute-done((f32[48,128]{1,0:T(8,128)S(1)}, f32[48,128]{1,0:T(8,128)S(1)}, u32[]{:S(2)}, u32[]{:S(2)}) %collective-permute-start.18) | collective-permute-done | bytes 24608 | tf_op jit(solution)/shard_map/ppermute | solution.py:575
  51.8 0.3 collective-permute-done.17.refs_9_
  52.1 0.7 %shard_map.111 = (f32[24,64,128]{2,1,0:T(8,128)S(1)}, f32[24,64,128]{2,1,0:T(8,128)S(1)}, f32[2,64,128]{2,1,0:T(8,128)S(1)}, f32[64,128]{1,0:T(8,128)S(1)}, f32[...) custom-call(f32[24,64,128]{2,1,0:T(8,128)S(1)} %get-tuple-element.122.refs_0_, ...), custom_call_target="tpu_custom_call" | custom-call | flops 4000000 | bytes 1000000 | tf_op jit(solution)/shard_map/pallas_call | solution.py:41
  52.8 0.4 shard_map.112
  53.2 2.6 %collective-permute-start.19 = (f32[4,12,64,128]{3,2,1,0:T(8,128)S(1)}, f32[4,12,64,128]{3,2,1,0:T(8,128)S(1)}, u32[]{:S(2)}, u32[]{:S(2)}) collective-permute-start(f32[4,12,64,128]{3,2,1,0:T(8,128)S(1)} %get-tuple-element.137), channel_id=1, source_target_pairs={{0,1},{1,0},{2,3},{3,2},{4,5},{5,4},{6,7},{7,6},{8,9},{9,8},{10,11... | collective-permute-start | bytes 4718600 | tf_op jit(solution)/shard_map/ppermute | solution.py:598
  55.9 0.9 %collective-permute-start.20 = (f32[2,64,128]{2,1,0:T(8,128)S(1)}, f32[2,64,128]{2,1,0:T(8,128)S(1)}, u32[]{:S(2)}, u32[]{:S(2)}) collective-permute-start(f32[2,64,128]{2,1,0:T(8,128)S(1)} %get-tuple-element.141), channel_id=1, source_target_pairs={{0,2},{1,3},{2,0},{3,1},{4,6},{5,7},{6,4},{7,5},{8,10},{9,11},{10,... | collective-permute-start | bytes 196616 | tf_op jit(solution)/shard_map/ppermute | solution.py:589
  56.8 1.9 %collective-permute-start.22 = (f32[2,64,128]{2,1,0:T(8,128)S(1)}, f32[2,64,128]{2,1,0:T(8,128)S(1)}, u32[]{:S(2)}, u32[]{:S(2)}) collective-permute-start(f32[2,64,128]{2,1,0:T(8,128)S(1)} %get-tuple-element.143), channel_id=1, source_target_pairs={{0,6},{1,7},{2,4},{3,5},{4,2},{5,3},{6,0},{7,1},{8,14},{9,15},{10,... | collective-permute-start | bytes 196616 | tf_op jit(solution)/shard_map/ppermute | solution.py:590
  58.7 0.7 %collective-permute-start.21 = (f32[64,128]{1,0:T(8,128)S(1)}, f32[64,128]{1,0:T(8,128)S(1)}, u32[]{:S(2)}, u32[]{:S(2)}) collective-permute-start(f32[64,128]{1,0:T(8,128)S(1)} %get-tuple-element.142), channel_id=1, source_target_pairs={{0,4},{1,5},{2,6},{3,7},{4,0},{5,1},{6,2},{7,3},{8,12},{9,13},{10,... | collective-permute-start | bytes 98312 | tf_op jit(solution)/shard_map/ppermute | solution.py:588
  59.4 3.5 %collective-permute-done.21.refs_8_ = f32[64,128]{1,0:T(8,128)S(1)} collective-permute-done((f32[64,128]{1,0:T(8,128)S(1)}, f32[64,128]{1,0:T(8,128)S(1)}, u32[]{:S(2)}, u32[]{:S(2)}) %collective-permute-start.21) | collective-permute-done | bytes 32800 | tf_op jit(solution)/shard_map/ppermute | solution.py:588
  63.0 0.7 %shard_map.114 = (f32[3,12,64,128]{3,2,1,0:T(8,128)S(1)}, f32[14,64,128]{2,1,0:T(8,128)S(1)}) custom-call(f32[24,64,128]{2,1,0:T(8,128)S(1)} %get-tuple-element.135.star.refs_0_, f32[24,64,128]{2,1,0:T(8,128)S(1)} %get-tuple-element.140.refs_1_, f32[24,64,128]{2,1,0:T(8,128)S(1)} %get-tuple-element.134.geo.refs_2_, ...), custom_call_target="tpu_custom_call" | custom-call | flops 4000000 | bytes 1000000 | tf_op jit(solution)/shard_map/pallas_call | solution.py:41
  63.7 1.9 %collective-permute-start.23 = (f32[14,64,128]{2,1,0:T(8,128)S(1)}, f32[14,64,128]{2,1,0:T(8,128)S(1)}, u32[]{:S(2)}, u32[]{:S(2)}) collective-permute-start(f32[14,64,128]{2,1,0:T(8,128)S(1)} %get-tuple-element.145), channel_id=1, source_target_pairs={{0,1},{1,0},{2,3},{3,2},{4,5},{5,4},{6,7},{7,6},{8,9},{9,8},{10,11... | collective-permute-start | bytes 1376264 | tf_op jit(solution)/shard_map/ppermute | solution.py:600
  65.6 1.2 %shard_map.113 = (f32[12,128,128]{2,1,0:T(8,128)}, f32[12,128,128]{2,1,0:T(8,128)}) custom-call(f32[2,12,64,128]{3,2,1,0:T(8,128)S(1)} %get-tuple-element.136.own, f32[4,12,64,128]{3,2,1,0:T(8,128)S(1)} %collective-permute-done.19.got), custom_call_target="tpu_custom_call" | custom-call | flops 4000000 | bytes 1000000 | tf_op jit(solution)/shard_map/pallas_call | solution.py:41
  66.8 0.3 collective-permute-done.23.got_wind
  67.1 1.5 %shard_map.115 = (f32[12,128,128]{2,1,0:T(8,128)}, f32[12,128,128]{2,1,0:T(8,128)}, f32[12,128,128]{2,1,0:T(8,128)}) custom-call(f32[3,12,64,128]{3,2,1,0:T(8,128)S(1)} %get-tuple-element.144.own, f32[4,12,64,128]{3,2,1,0:T(8,128)S(1)} %collective-permute-done.19.got, f32[14,64,128]{2,1,0:T(8,128)S(1)} %collective-permute-done.23.got_wind, ...), custom_call_target="tpu_custom_call" | custom-call | flops 4000000 | bytes 1000000 | tf_op jit(solution)/shard_map/pallas_call | solution.py:41
  (22 shorter events, 0.1 us)
Async XLA Ops:
  3.4 0.6 copy-start.5
  4.0 11.2 %copy-start.2 = (f32[12,128,128]{2,1,0:T(8,128)S(1)}, f32[12,128,128]{2,1,0:T(8,128)}, u32[]{:S(2)}) copy-start(f32[12,128,128]{2,1,0:T(8,128)} %refs_0_.3) | copy-start | bytes 2359300
  4.0 11.2 %copy-start.3 = (f32[12,128,128]{2,1,0:T(8,128)S(1)}, f32[12,128,128]{2,1,0:T(8,128)}, u32[]{:S(2)}) copy-start(f32[12,128,128]{2,1,0:T(8,128)} %refs_1_.3) | copy-start | bytes 2359300
  4.1 4.1 %collective-permute-start = (f32[144,128]{1,0:T(8,128)S(1)}, f32[144,128]{1,0:T(8,128)S(1)}, u32[]{:S(2)}, u32[]{:S(2)}) collective-permute-start(f32[144,128]{1,0:T(8,128)S(1)} %get-tuple-element.78), channel_id=1, source_target_pairs={{0,1},{1,0},{2,3},{3,2},{4,5},{5,4},{6,7},{7,6},{8,9},{9,8},{10,11... | collective-permute-start | bytes 221192 | tf_op jit(solution)/shard_map/ppermute | solution.py:554
  8.2 0.6 copy-start.7
  8.8 6.5 %collective-permute-start.1 = (f32[5,12,64,128]{3,2,1,0:T(8,128)}, f32[5,12,64,128]{3,2,1,0:T(8,128)S(1)}, u32[]{:S(2)}, u32[]{:S(2)}) collective-permute-start(f32[5,12,64,128]{3,2,1,0:T(8,128)} %get-tuple-element.79), channel_id=1, source_target_pairs={{0,1},{1,0},{2,3},{3,2},{4,5},{5,4},{6,7},{7,6},{8,9},{9,8},{10,11... | collective-permute-start | bytes 5898248 | tf_op jit(solution)/shard_map/ppermute | solution.py:557
  9.2 6.1 %copy-start.4 = (f32[12,128,128]{2,1,0:T(8,128)S(1)}, f32[12,128,128]{2,1,0:T(8,128)}, u32[]{:S(2)}) copy-start(f32[12,128,128]{2,1,0:T(8,128)} %refs_2_.3) | copy-start | bytes 2359300
  10.4 0.9 %copy-start.6 = (f32[144,128]{1,0:T(8,128)S(1)}, f32[144,128]{1,0:T(8,128)}, u32[]{:S(2)}) copy-start(f32[144,128]{1,0:T(8,128)} %copy-done.5) | copy-start | bytes 221188
  11.3 0.9 %copy-start.8 = (f32[144,128]{1,0:T(8,128)S(1)}, f32[144,128]{1,0:T(8,128)}, u32[]{:S(2)}) copy-start(f32[144,128]{1,0:T(8,128)} %copy-done.7) | copy-start | bytes 221188
  12.2 5.1 %collective-permute-start.4 = (f32[96,128]{1,0:T(8,128)S(1)}, f32[96,128]{1,0:T(8,128)S(1)}, u32[]{:S(2)}, u32[]{:S(2)}) collective-permute-start(f32[96,128]{1,0:T(8,128)S(1)} %get-tuple-element.87.refs_11_), channel_id=1, source_target_pairs={{0,24},{8,16},{16,8},{24,0},{1,25},{9,17},{17,9},{25,1},{2,26},{10... | collective-permute-start | bytes 147464 | tf_op jit(solution)/shard_map/ppermute | solution.py:575
  13.0 4.3 %collective-permute-start.3 = (f32[96,128]{1,0:T(8,128)S(1)}, f32[96,128]{1,0:T(8,128)S(1)}, u32[]{:S(2)}, u32[]{:S(2)}) collective-permute-start(f32[96,128]{1,0:T(8,128)S(1)} %get-tuple-element.87.refs_11_), channel_id=1, source_target_pairs={{0,8},{8,0},{16,24},{24,16},{1,9},{9,1},{17,25},{25,17},{2,10},{10... | collective-permute-start | bytes 147464 | tf_op jit(solution)/shard_map/ppermute | solution.py:574
  13.1 4.2 %collective-permute-start.2 = (f32[96,128]{1,0:T(8,128)S(1)}, f32[96,128]{1,0:T(8,128)S(1)}, u32[]{:S(2)}, u32[]{:S(2)}) collective-permute-start(f32[96,128]{1,0:T(8,128)S(1)} %get-tuple-element.86), channel_id=1, source_target_pairs={{0,225},{1,32},{2,227},{3,34},{4,229},{5,36},{6,231},{7,38},{32,1}... | collective-permute-start | bytes 147464 | tf_op jit(solution)/shard_map/ppermute | solution.py:576
  15.2 1.7 %copy-start = (f32[12,128,128]{2,1,0:T(8,128)S(1)}, f32[12,128,128]{2,1,0:T(8,128)}, u32[]{:S(2)}) copy-start(f32[12,128,128]{2,1,0:T(8,128)} %wind.1) | copy-start | bytes 2359300
  15.3 1.7 %copy-start.1 = (f32[12,128,128]{2,1,0:T(8,128)S(1)}, f32[12,128,128]{2,1,0:T(8,128)}, u32[]{:S(2)}) copy-start(f32[12,128,128]{2,1,0:T(8,128)} %geo.1) | copy-start | bytes 2359300
  18.0 7.4 %collective-permute-start.5 = (f32[2,64,128]{2,1,0:T(8,128)S(1)}, f32[2,64,128]{2,1,0:T(8,128)S(1)}, u32[]{:S(2)}, u32[]{:S(2)}) collective-permute-start(f32[2,64,128]{2,1,0:T(8,128)S(1)} %get-tuple-element.91), channel_id=1, source_target_pairs={{0,2},{1,3},{2,0},{3,1},{4,6},{5,7},{6,4},{7,5},{8,10},{9,11},{10,... | collective-permute-start | bytes 196616 | tf_op jit(solution)/shard_map/ppermute | solution.py:589
  19.3 6.2 %collective-permute-start.7 = (f32[2,64,128]{2,1,0:T(8,128)S(1)}, f32[2,64,128]{2,1,0:T(8,128)S(1)}, u32[]{:S(2)}, u32[]{:S(2)}) collective-permute-start(f32[2,64,128]{2,1,0:T(8,128)S(1)} %get-tuple-element.93), channel_id=1, source_target_pairs={{0,6},{1,7},{2,4},{3,5},{4,2},{5,3},{6,0},{7,1},{8,14},{9,15},{10,... | collective-permute-start | bytes 196616 | tf_op jit(solution)/shard_map/ppermute | solution.py:590
  21.2 4.3 %collective-permute-start.6 = (f32[64,128]{1,0:T(8,128)S(1)}, f32[64,128]{1,0:T(8,128)S(1)}, u32[]{:S(2)}, u32[]{:S(2)}) collective-permute-start(f32[64,128]{1,0:T(8,128)S(1)} %get-tuple-element.92), channel_id=1, source_target_pairs={{0,4},{1,5},{2,6},{3,7},{4,0},{5,1},{6,2},{7,3},{8,12},{9,13},{10,... | collective-permute-start | bytes 98312 | tf_op jit(solution)/shard_map/ppermute | solution.py:588
  26.1 8.6 %collective-permute-start.8 = (f32[48,128]{1,0:T(8,128)S(1)}, f32[48,128]{1,0:T(8,128)S(1)}, u32[]{:S(2)}, u32[]{:S(2)}) collective-permute-start(f32[48,128]{1,0:T(8,128)S(1)} %get-tuple-element.102), channel_id=1, source_target_pairs={{0,1},{1,0},{2,3},{3,2},{4,5},{5,4},{6,7},{7,6},{8,9},{9,8},{10,11... | collective-permute-start | bytes 73736 | tf_op jit(solution)/shard_map/ppermute | solution.py:582
  31.7 3.3 %collective-permute-start.9 = (f32[48,128]{1,0:T(8,128)S(1)}, f32[48,128]{1,0:T(8,128)S(1)}, u32[]{:S(2)}, u32[]{:S(2)}) collective-permute-start(f32[48,128]{1,0:T(8,128)S(1)} %get-tuple-element.103), channel_id=1, source_target_pairs={{0,225},{1,32},{2,227},{3,34},{4,229},{5,36},{6,231},{7,38},{32,1}... | collective-permute-start | bytes 73736 | tf_op jit(solution)/shard_map/ppermute | solution.py:576
  31.7 4.2 %collective-permute-start.11 = (f32[48,128]{1,0:T(8,128)S(1)}, f32[48,128]{1,0:T(8,128)S(1)}, u32[]{:S(2)}, u32[]{:S(2)}) collective-permute-start(f32[48,128]{1,0:T(8,128)S(1)} %get-tuple-element.104.refs_11_), channel_id=1, source_target_pairs={{0,24},{8,16},{16,8},{24,0},{1,25},{9,17},{17,9},{25,1},{2,26},{10... | collective-permute-start | bytes 73736 | tf_op jit(solution)/shard_map/ppermute | solution.py:575
  32.5 3.4 %collective-permute-start.10 = (f32[48,128]{1,0:T(8,128)S(1)}, f32[48,128]{1,0:T(8,128)S(1)}, u32[]{:S(2)}, u32[]{:S(2)}) collective-permute-start(f32[48,128]{1,0:T(8,128)S(1)} %get-tuple-element.104.refs_11_), channel_id=1, source_target_pairs={{0,8},{8,0},{16,24},{24,16},{1,9},{9,1},{17,25},{25,17},{2,10},{10... | collective-permute-start | bytes 73736 | tf_op jit(solution)/shard_map/ppermute | solution.py:574
  36.6 5.2 %collective-permute-start.12 = (f32[2,64,128]{2,1,0:T(8,128)S(1)}, f32[2,64,128]{2,1,0:T(8,128)S(1)}, u32[]{:S(2)}, u32[]{:S(2)}) collective-permute-start(f32[2,64,128]{2,1,0:T(8,128)S(1)} %get-tuple-element.112), channel_id=1, source_target_pairs={{0,2},{1,3},{2,0},{3,1},{4,6},{5,7},{6,4},{7,5},{8,10},{9,11},{10,... | collective-permute-start | bytes 196616 | tf_op jit(solution)/shard_map/ppermute | solution.py:589
  37.1 4.8 %collective-permute-start.14 = (f32[2,64,128]{2,1,0:T(8,128)S(1)}, f32[2,64,128]{2,1,0:T(8,128)S(1)}, u32[]{:S(2)}, u32[]{:S(2)}) collective-permute-start(f32[2,64,128]{2,1,0:T(8,128)S(1)} %get-tuple-element.114), channel_id=1, source_target_pairs={{0,6},{1,7},{2,4},{3,5},{4,2},{5,3},{6,0},{7,1},{8,14},{9,15},{10,... | collective-permute-start | bytes 196616 | tf_op jit(solution)/shard_map/ppermute | solution.py:590
  37.6 4.3 %collective-permute-start.13 = (f32[64,128]{1,0:T(8,128)S(1)}, f32[64,128]{1,0:T(8,128)S(1)}, u32[]{:S(2)}, u32[]{:S(2)}) collective-permute-start(f32[64,128]{1,0:T(8,128)S(1)} %get-tuple-element.113), channel_id=1, source_target_pairs={{0,4},{1,5},{2,6},{3,7},{4,0},{5,1},{6,2},{7,3},{8,12},{9,13},{10,... | collective-permute-start | bytes 98312 | tf_op jit(solution)/shard_map/ppermute | solution.py:588
  42.5 8.6 %collective-permute-start.15 = (f32[48,128]{1,0:T(8,128)S(1)}, f32[48,128]{1,0:T(8,128)S(1)}, u32[]{:S(2)}, u32[]{:S(2)}) collective-permute-start(f32[48,128]{1,0:T(8,128)S(1)} %get-tuple-element.125), channel_id=1, source_target_pairs={{0,1},{1,0},{2,3},{3,2},{4,5},{5,4},{6,7},{7,6},{8,9},{9,8},{10,11... | collective-permute-start | bytes 73736 | tf_op jit(solution)/shard_map/ppermute | solution.py:582
  47.7 3.5 %collective-permute-start.16 = (f32[48,128]{1,0:T(8,128)S(1)}, f32[48,128]{1,0:T(8,128)S(1)}, u32[]{:S(2)}, u32[]{:S(2)}) collective-permute-start(f32[48,128]{1,0:T(8,128)S(1)} %get-tuple-element.126), channel_id=1, source_target_pairs={{0,225},{1,32},{2,227},{3,34},{4,229},{5,36},{6,231},{7,38},{32,1}... | collective-permute-start | bytes 73736 | tf_op jit(solution)/shard_map/ppermute | solution.py:576
  47.7 4.2 %collective-permute-start.18 = (f32[48,128]{1,0:T(8,128)S(1)}, f32[48,128]{1,0:T(8,128)S(1)}, u32[]{:S(2)}, u32[]{:S(2)}) collective-permute-start(f32[48,128]{1,0:T(8,128)S(1)} %get-tuple-element.127.refs_11_), channel_id=1, source_target_pairs={{0,24},{8,16},{16,8},{24,0},{1,25},{9,17},{17,9},{25,1},{2,26},{10... | collective-permute-start | bytes 73736 | tf_op jit(solution)/shard_map/ppermute | solution.py:575
  49.4 2.7 %collective-permute-start.17 = (f32[48,128]{1,0:T(8,128)S(1)}, f32[48,128]{1,0:T(8,128)S(1)}, u32[]{:S(2)}, u32[]{:S(2)}) collective-permute-start(f32[48,128]{1,0:T(8,128)S(1)} %get-tuple-element.127.refs_11_), channel_id=1, source_target_pairs={{0,8},{8,0},{16,24},{24,16},{1,9},{9,1},{17,25},{25,17},{2,10},{10... | collective-permute-start | bytes 73736 | tf_op jit(solution)/shard_map/ppermute | solution.py:574
  53.2 12.4 %collective-permute-start.19 = (f32[4,12,64,128]{3,2,1,0:T(8,128)S(1)}, f32[4,12,64,128]{3,2,1,0:T(8,128)S(1)}, u32[]{:S(2)}, u32[]{:S(2)}) collective-permute-start(f32[4,12,64,128]{3,2,1,0:T(8,128)S(1)} %get-tuple-element.137), channel_id=1, source_target_pairs={{0,1},{1,0},{2,3},{3,2},{4,5},{5,4},{6,7},{7,6},{8,9},{9,8},{10,11... | collective-permute-start | bytes 4718600 | tf_op jit(solution)/shard_map/ppermute | solution.py:598
  55.9 7.1 %collective-permute-start.20 = (f32[2,64,128]{2,1,0:T(8,128)S(1)}, f32[2,64,128]{2,1,0:T(8,128)S(1)}, u32[]{:S(2)}, u32[]{:S(2)}) collective-permute-start(f32[2,64,128]{2,1,0:T(8,128)S(1)} %get-tuple-element.141), channel_id=1, source_target_pairs={{0,2},{1,3},{2,0},{3,1},{4,6},{5,7},{6,4},{7,5},{8,10},{9,11},{10,... | collective-permute-start | bytes 196616 | tf_op jit(solution)/shard_map/ppermute | solution.py:589
  56.8 6.2 %collective-permute-start.22 = (f32[2,64,128]{2,1,0:T(8,128)S(1)}, f32[2,64,128]{2,1,0:T(8,128)S(1)}, u32[]{:S(2)}, u32[]{:S(2)}) collective-permute-start(f32[2,64,128]{2,1,0:T(8,128)S(1)} %get-tuple-element.143), channel_id=1, source_target_pairs={{0,6},{1,7},{2,4},{3,5},{4,2},{5,3},{6,0},{7,1},{8,14},{9,15},{10,... | collective-permute-start | bytes 196616 | tf_op jit(solution)/shard_map/ppermute | solution.py:590
  58.7 4.3 %collective-permute-start.21 = (f32[64,128]{1,0:T(8,128)S(1)}, f32[64,128]{1,0:T(8,128)S(1)}, u32[]{:S(2)}, u32[]{:S(2)}) collective-permute-start(f32[64,128]{1,0:T(8,128)S(1)} %get-tuple-element.142), channel_id=1, source_target_pairs={{0,4},{1,5},{2,6},{3,7},{4,0},{5,1},{6,2},{7,3},{8,12},{9,13},{10,... | collective-permute-start | bytes 98312 | tf_op jit(solution)/shard_map/ppermute | solution.py:588
  63.7 3.3 %collective-permute-start.23 = (f32[14,64,128]{2,1,0:T(8,128)S(1)}, f32[14,64,128]{2,1,0:T(8,128)S(1)}, u32[]{:S(2)}, u32[]{:S(2)}) collective-permute-start(f32[14,64,128]{2,1,0:T(8,128)S(1)} %get-tuple-element.145), channel_id=1, source_target_pairs={{0,1},{1,0},{2,3},{3,2},{4,5},{5,4},{6,7},{7,6},{8,9},{9,8},{10,11... | collective-permute-start | bytes 1376264 | tf_op jit(solution)/shard_map/ppermute | solution.py:600

commit v3 on v2

--- a/solution.py
+++ b/solution.py
@@ -172,20 +172,7 @@
                 out[at : at + PART, :] = jnp.where(core == piece, keep[part, :], got[part, :])
 
 
-def winds_out_kernel(own, got, east, north, sem):
-    core = core_of()
-    copies = []
-    for f, out in enumerate((east, north)):
-        for which, src in ((core, own), (1 - core, got)):
-            rows = pl.ds(pl.multiple_of(which * RX, RX), RX)
-            copy = pltpu.make_async_copy(src.at[f], out.at[:, rows, :], sem.at[len(copies)])
-            copy.start()
-            copies.append(copy)
-    for copy in copies:
-        copy.wait()
-
-
-def solved_out_kernel(own, got, got_wind, mass, wind, geo, press, fill, sem):
+def outputs_kernel(own, own_winds, got, got_wind, mass, east, north, wind, geo, press, fill, sem):
     core = core_of()
     copies = []
 
@@ -197,6 +184,9 @@
     for f, out in enumerate((wind, geo, press)):
         write(own.at[f], out, core)
     write(got_wind.at[pl.ds(1, HALF)], wind, 1 - core)
+    for f, out in enumerate((east, north)):
+        write(own_winds.at[f], out, core)
+        write(got.at[f], out, 1 - core)
     flux = level_flux * mass[...]
     for f, out in enumerate((geo, press)):
         for k in range(HALF):
@@ -598,13 +588,12 @@
             got_part = lax.ppermute(send_part, "gz", swap)
             solved, send_solved = solve(last, *args)
             got_solved = lax.ppermute(send_solved, "gz", swap)
-            winds_after = write_out(winds_out_kernel, 2, (), own_part, got_part)
             other = lax.dynamic_slice_in_dim(column_mass, (1 - core) * RX, RX, 0)
             fill = pltpu.VMEM((2, HALF, RX, LN), F32)
-            solved_after = write_out(solved_out_kernel, 3, (fill,), solved, got_part, got_solved, other)
+            outputs = write_out(outputs_kernel, 5, (fill,), solved, own_part, got_part, got_solved, other)
         else:
             wind, press, mid, outer, cols = solve(last, *args)
-    return *winds_after, *solved_after
+    return tuple(outputs)
 
 
 def solution(mesh):

time: 68.9 us -> 69.4 us (level)
  waiting for transfers between devices: 12.4 us -> 13.6 us
    ppermute x1, waiting for transfers between devices: 0.26 us -> 1.44 us  [local(): got_solved = lax.ppermute(send_solved, 'gz', swap)]
    pallas_call x15 -> x14, Pallas kernels: 15.1 us -> 14.5 us  [call(): pl.pallas_call(body, out_shape=outs, in_specs=in_specs or [VMEM] * len(ar...]
  transfers between devices with their start and end apart: 24 -> 24, of which waited for: 10 -> 10; matrix products, arithmetic and copies ran while one was open for 2% -> 2% of each run, Pallas kernels for 10% -> 8%
where the time goes in v3:
time: 69.4 us; the launch traced here: 69.2 us
  starting transfers between devices  35.9 us (52%)
  Pallas kernels  14.5 us (21%)
  waiting for transfers between devices  13.6 us (20%)
  local copies, waits for them, and re-layouts  3.05 us (4%)
  other arithmetic  1.23 us (2%)
  between operations  1.02 us (1%)
    pallas_call x14, Pallas kernels, call(): pl.pallas_call(body, out_shape=outs, in_specs=in_specs or [VMEM] * len(ar...  14.5 us
    ppermute x2, starting transfers between devices, local(): mid_in = lax.ppermute(mid, 'gz', swap)  10.7 us
    ppermute x3, waiting for transfers between devices, local(): from_far = lax.ppermute(to_far, 'gz', far_chip)  8.98 us
    ppermute x3, starting transfers between devices, local(): from_around = lax.ppermute(to_around, 'gz', around_chip)  4.28 us
    ppermute x3, starting transfers between devices, local(): from_far = lax.ppermute(to_far, 'gz', far_chip)  3.82 us
    ppermute x3, starting transfers between devices, local(): around = lax.ppermute(cols, 'gy', around_tile)  3.4 us
    ppermute x1, starting transfers between devices, local(): got_edges = lax.ppermute(give, 'gz', swap)  3.2 us
    unnamed x18, local copies, waits for them, and re-layouts  3.05 us
  transfers between devices with their start and end apart: 24, of which 10 were waited for; matrix products, arithmetic and copies ran while one was open for 2% of the time, Pallas kernels for 8%

profile of v3, /device:TPU:1, one launch (start us, length us, event | category | flops | bytes accessed | tf_op | source)
XLA Modules:
  0.0 69.2 jit_solution(16247558442024246319)
XLA Ops:
  0.6 2.8 %shard_map.101 = (f32[5,12,64,128]{3,2,1,0:T(8,128)}, f32[144,128]{1,0:T(8,128)S(1)}, f32[144,128]{1,0:T(8,128)S(1)}) custom-call(f32[12,128,128]{2,1,0:T(8,128)} %refs_0_.3, f32[12,128,128]{2,1,0:T(8,128)} %refs_1_.3, f32[12,128,128]{2,1,0:T(8,128)} %refs_2_.3, f32[12,128,128]{2,1,0:T(8,128)} %wind.1, f32[12,128,128]{2,1,0:T(8,128)} %geo.1), custom_call_target="tpu_custom_call" | custom-call | flops 4000000 | bytes 1000000 | tf_op jit(solution)/shard_map/pallas_call | solution.py:41
  3.4 0.0 copy-start.5
  3.4 0.6 copy-done.5
  4.0 3.2 %collective-permute-start = (f32[144,128]{1,0:T(8,128)S(1)}, f32[144,128]{1,0:T(8,128)S(1)}, u32[]{:S(2)}, u32[]{:S(2)}) collective-permute-start(f32[144,128]{1,0:T(8,128)S(1)} %get-tuple-element.73), channel_id=1, source_target_pairs={{0,1},{1,0},{2,3},{3,2},{4,5},{5,4},{6,7},{7,6},{8,9},{9,8},{10,11... | collective-permute-start | bytes 221192 | tf_op jit(solution)/shard_map/ppermute | solution.py:544
  7.2 0.9 %collective-permute-done.got = f32[144,128]{1,0:T(8,128)S(1)} collective-permute-done((f32[144,128]{1,0:T(8,128)S(1)}, f32[144,128]{1,0:T(8,128)S(1)}, u32[]{:S(2)}, u32[]{:S(2)}) %collective-permute-start) | collective-permute-done | bytes 73760 | tf_op jit(solution)/shard_map/ppermute | solution.py:544
  8.2 0.6 copy-done.7
  8.8 0.4 collective-permute-start.1
  9.2 0.9 %fusion.1 = (f32[64,128]{1,0:T(8,128)S(1)}, f32[64,128]{1,0:T(8,128)S(1)}, f32[64,128]{1,0:T(8,128)S(1)}) fusion(f32[128,128]{1,0:T(8,128)} %param.11, s32[]{:T(128)S(6)} %select_n.6, s32[]{:T(128)S(6)} %select_n.7), kind=kLoop, calls=%fused_computation.9 | loop fusion | flops 49152 | bytes 163848 | tf_op jit(solution)/shard_map/log | solution.py:554
  10.0 0.1 fusion.2
  10.1 0.3 exponential_subtract_fusion
  10.4 0.0 copy-start.6
  10.4 0.9 %copy-done.6 = f32[144,128]{1,0:T(8,128)S(1)} copy-done((f32[144,128]{1,0:T(8,128)S(1)}, f32[144,128]{1,0:T(8,128)}, u32[]{:S(2)}) %copy-start.6) | copy-done | bytes 73752
  11.3 0.9 %copy-done.8 = f32[144,128]{1,0:T(8,128)S(1)} copy-done((f32[144,128]{1,0:T(8,128)S(1)}, f32[144,128]{1,0:T(8,128)}, u32[]{:S(2)}) %copy-start.8) | copy-done | bytes 73752
  12.2 0.9 %collective-permute-start.4 = (f32[96,128]{1,0:T(8,128)S(1)}, f32[96,128]{1,0:T(8,128)S(1)}, u32[]{:S(2)}, u32[]{:S(2)}) collective-permute-start(f32[96,128]{1,0:T(8,128)S(1)} %get-tuple-element.82.refs_11_), channel_id=1, source_target_pairs={{0,24},{8,16},{16,8},{24,0},{1,25},{9,17},{17,9},{25,1},{2,26},{10... | collective-permute-start | bytes 147464 | tf_op jit(solution)/shard_map/ppermute | solution.py:565
  13.0 0.0 collective-permute-start.3
  13.0 2.2 %collective-permute-start.2 = (f32[96,128]{1,0:T(8,128)S(1)}, f32[96,128]{1,0:T(8,128)S(1)}, u32[]{:S(2)}, u32[]{:S(2)}) collective-permute-start(f32[96,128]{1,0:T(8,128)S(1)} %get-tuple-element.81), channel_id=1, source_target_pairs={{0,225},{1,32},{2,227},{3,34},{4,229},{5,36},{6,231},{7,38},{32,1}... | collective-permute-start | bytes 147464 | tf_op jit(solution)/shard_map/ppermute | solution.py:566
  15.2 0.0 copy-start
  15.3 0.0 copy-start.1
  15.3 0.0 collective-permute-done.1.refs_3_.got
  15.3 1.6 %shard_map.102 = (f32[24,64,128]{2,1,0:T(8,128)S(1)}, f32[24,64,128]{2,1,0:T(8,128)S(1)}, f32[24,64,128]{2,1,0:T(8,128)S(1)}, f32[48,128]{1,0:T(8,128)S(1)}) custom-call(f32[12,128,128]{2,1,0:T(8,128)S(1)} %copy-done.2, f32[12,128,128]{2,1,0:T(8,128)S(1)} %copy-done.3, f32[12,128,128]{2,1,0:T(8,128)S(1)} %copy-done.4, ...), custom_call_target="tpu_custom_call" | custom-call | flops 4000000 | bytes 1000000 | tf_op jit(solution)/shard_map/pallas_call | solution.py:41
  16.9 0.2 shard_map.103
  17.1 0.2 collective-permute-done.2.refs_8_
  17.3 0.0 collective-permute-done.4.refs_10_
  17.3 0.7 %shard_map.105 = (f32[24,64,128]{2,1,0:T(8,128)S(1)}, f32[24,64,128]{2,1,0:T(8,128)S(1)}, f32[2,64,128]{2,1,0:T(8,128)S(1)}, f32[64,128]{1,0:T(8,128)S(1)}, f32[...) custom-call(f32[24,64,128]{2,1,0:T(8,128)S(1)} %get-tuple-element.75, ...), custom_call_target="tpu_custom_call" | custom-call | flops 4000000 | bytes 1000000 | tf_op jit(solution)/shard_map/pallas_call | solution.py:41
  18.0 1.3 %collective-permute-start.5 = (f32[2,64,128]{2,1,0:T(8,128)S(1)}, f32[2,64,128]{2,1,0:T(8,128)S(1)}, u32[]{:S(2)}, u32[]{:S(2)}) collective-permute-start(f32[2,64,128]{2,1,0:T(8,128)S(1)} %get-tuple-element.86), channel_id=1, source_target_pairs={{0,2},{1,3},{2,0},{3,1},{4,6},{5,7},{6,4},{7,5},{8,10},{9,11},{10,... | collective-permute-start | bytes 196616 | tf_op jit(solution)/shard_map/ppermute | solution.py:579
  19.3 1.9 %collective-permute-start.7 = (f32[2,64,128]{2,1,0:T(8,128)S(1)}, f32[2,64,128]{2,1,0:T(8,128)S(1)}, u32[]{:S(2)}, u32[]{:S(2)}) collective-permute-start(f32[2,64,128]{2,1,0:T(8,128)S(1)} %get-tuple-element.88), channel_id=1, source_target_pairs={{0,6},{1,7},{2,4},{3,5},{4,2},{5,3},{6,0},{7,1},{8,14},{9,15},{10,... | collective-permute-start | bytes 196616 | tf_op jit(solution)/shard_map/ppermute | solution.py:580
  21.2 0.7 %collective-permute-start.6 = (f32[64,128]{1,0:T(8,128)S(1)}, f32[64,128]{1,0:T(8,128)S(1)}, u32[]{:S(2)}, u32[]{:S(2)}) collective-permute-start(f32[64,128]{1,0:T(8,128)S(1)} %get-tuple-element.87), channel_id=1, source_target_pairs={{0,4},{1,5},{2,6},{3,7},{4,0},{5,1},{6,2},{7,3},{8,12},{9,13},{10,... | collective-permute-start | bytes 98312 | tf_op jit(solution)/shard_map/ppermute | solution.py:578
  21.9 3.5 %collective-permute-done.6.refs_8_ = f32[64,128]{1,0:T(8,128)S(1)} collective-permute-done((f32[64,128]{1,0:T(8,128)S(1)}, f32[64,128]{1,0:T(8,128)S(1)}, u32[]{:S(2)}, u32[]{:S(2)}) %collective-permute-start.6) | collective-permute-done | bytes 32800 | tf_op jit(solution)/shard_map/ppermute | solution.py:578
  25.5 0.7 shard_map.106
  26.2 5.5 %collective-permute-start.8 = (f32[48,128]{1,0:T(8,128)S(1)}, f32[48,128]{1,0:T(8,128)S(1)}, u32[]{:S(2)}, u32[]{:S(2)}) collective-permute-start(f32[48,128]{1,0:T(8,128)S(1)} %get-tuple-element.97), channel_id=1, source_target_pairs={{0,1},{1,0},{2,3},{3,2},{4,5},{5,4},{6,7},{7,6},{8,9},{9,8},{10,11... | collective-permute-start | bytes 73736 | tf_op jit(solution)/shard_map/ppermute | solution.py:572
  31.7 0.0 collective-permute-start.9
  31.7 0.8 %collective-permute-start.11 = (f32[48,128]{1,0:T(8,128)S(1)}, f32[48,128]{1,0:T(8,128)S(1)}, u32[]{:S(2)}, u32[]{:S(2)}) collective-permute-start(f32[48,128]{1,0:T(8,128)S(1)} %get-tuple-element.99.refs_11_), channel_id=1, source_target_pairs={{0,24},{8,16},{16,8},{24,0},{1,25},{9,17},{17,9},{25,1},{2,26},{10... | collective-permute-start | bytes 73736 | tf_op jit(solution)/shard_map/ppermute | solution.py:565
  32.5 0.7 collective-permute-start.10
  33.2 1.6 %shard_map.107 = (f32[24,64,128]{2,1,0:T(8,128)S(1)}, f32[24,64,128]{2,1,0:T(8,128)S(1)}, f32[24,64,128]{2,1,0:T(8,128)S(1)}, f32[48,128]{1,0:T(8,128)S(1)}, f32...) custom-call(f32[24,64,128]{2,1,0:T(8,128)S(1)} %get-tuple-element.89.refs_0_, ...), custom_call_target="tpu_custom_call" | custom-call | flops 4000000 | bytes 1000000 | tf_op jit(solution)/shard_map/pallas_call | solution.py:41
  34.8 0.1 collective-permute-done.9.refs_8_
  34.9 0.9 %collective-permute-done.11.refs_10_ = f32[48,128]{1,0:T(8,128)S(1)} collective-permute-done((f32[48,128]{1,0:T(8,128)S(1)}, f32[48,128]{1,0:T(8,128)S(1)}, u32[]{:S(2)}, u32[]{:S(2)}) %collective-permute-start.11) | collective-permute-done | bytes 24608 | tf_op jit(solution)/shard_map/ppermute | solution.py:565
  35.9 0.7 %shard_map.108 = (f32[24,64,128]{2,1,0:T(8,128)S(1)}, f32[24,64,128]{2,1,0:T(8,128)S(1)}, f32[2,64,128]{2,1,0:T(8,128)S(1)}, f32[64,128]{1,0:T(8,128)S(1)}, f32[...) custom-call(f32[24,64,128]{2,1,0:T(8,128)S(1)} %get-tuple-element.94, ...), custom_call_target="tpu_custom_call" | custom-call | flops 4000000 | bytes 1000000 | tf_op jit(solution)/shard_map/pallas_call | solution.py:41
  36.6 0.5 collective-permute-start.12
  37.1 0.5 collective-permute-start.14
  37.6 2.4 %collective-permute-start.13 = (f32[64,128]{1,0:T(8,128)S(1)}, f32[64,128]{1,0:T(8,128)S(1)}, u32[]{:S(2)}, u32[]{:S(2)}) collective-permute-start(f32[64,128]{1,0:T(8,128)S(1)} %get-tuple-element.108), channel_id=1, source_target_pairs={{0,4},{1,5},{2,6},{3,7},{4,0},{5,1},{6,2},{7,3},{8,12},{9,13},{10,... | collective-permute-start | bytes 98312 | tf_op jit(solution)/shard_map/ppermute | solution.py:578
  39.9 1.9 %collective-permute-done.13.refs_8_ = f32[64,128]{1,0:T(8,128)S(1)} collective-permute-done((f32[64,128]{1,0:T(8,128)S(1)}, f32[64,128]{1,0:T(8,128)S(1)}, u32[]{:S(2)}, u32[]{:S(2)}) %collective-permute-start.13) | collective-permute-done | bytes 32800 | tf_op jit(solution)/shard_map/ppermute | solution.py:578
  41.8 0.0 collective-permute-done.12.refs_7_
  41.8 0.0 collective-permute-done.14.refs_9_
  41.8 0.7 %shard_map.109 = (f32[26,64,128]{2,1,0:T(8,128)S(1)}, f32[24,64,128]{2,1,0:T(8,128)S(1)}, f32[48,128]{1,0:T(8,128)S(1)}, f32[48,128]{1,0:T(8,128)S(1)}, f32[48,128]{1,0:T(8,128)S(1)}) custom-call(f32[24,64,128]{2,1,0:T(8,128)S(1)} %get-tuple-element.104.refs_0_, f32[24,64,128]{2,1,0:T(8,128)S(1)} %get-tuple-element.105.refs_1_, ...), custom_call_target="tpu_custom_call" | custom-call | flops 4000000 | bytes 1000000 | tf_op jit(solution)/shard_map/pallas_call | solution.py:41
  42.5 5.1 %collective-permute-start.15 = (f32[48,128]{1,0:T(8,128)S(1)}, f32[48,128]{1,0:T(8,128)S(1)}, u32[]{:S(2)}, u32[]{:S(2)}) collective-permute-start(f32[48,128]{1,0:T(8,128)S(1)} %get-tuple-element.118), channel_id=1, source_target_pairs={{0,1},{1,0},{2,3},{3,2},{4,5},{5,4},{6,7},{7,6},{8,9},{9,8},{10,11... | collective-permute-start | bytes 73736 | tf_op jit(solution)/shard_map/ppermute | solution.py:572
  47.7 1.7 %collective-permute-start.18 = (f32[48,128]{1,0:T(8,128)S(1)}, f32[48,128]{1,0:T(8,128)S(1)}, u32[]{:S(2)}, u32[]{:S(2)}) collective-permute-start(f32[48,128]{1,0:T(8,128)S(1)} %get-tuple-element.120.refs_11_), channel_id=1, source_target_pairs={{0,24},{8,16},{16,8},{24,0},{1,25},{9,17},{17,9},{25,1},{2,26},{10... | collective-permute-start | bytes 73736 | tf_op jit(solution)/shard_map/ppermute | solution.py:565
  49.4 0.1 collective-permute-start.17
  49.5 1.6 %shard_map.110 = (f32[24,64,128]{2,1,0:T(8,128)S(1)}, f32[24,64,128]{2,1,0:T(8,128)S(1)}, f32[24,64,128]{2,1,0:T(8,128)S(1)}, f32[48,128]{1,0:T(8,128)S(1)}, f32...) custom-call(f32[24,64,128]{2,1,0:T(8,128)S(1)} %get-tuple-element.110.refs_0_, ...), custom_call_target="tpu_custom_call" | custom-call | flops 4000000 | bytes 1000000 | tf_op jit(solution)/shard_map/pallas_call | solution.py:41
  51.1 0.0 collective-permute-done.16.refs_8_
  51.1 0.7 %collective-permute-done.18.refs_10_ = f32[48,128]{1,0:T(8,128)S(1)} collective-permute-done((f32[48,128]{1,0:T(8,128)S(1)}, f32[48,128]{1,0:T(8,128)S(1)}, u32[]{:S(2)}, u32[]{:S(2)}) %collective-permute-start.18) | collective-permute-done | bytes 24608 | tf_op jit(solution)/shard_map/ppermute | solution.py:565
  51.8 0.3 collective-permute-done.17.refs_9_
  52.1 0.7 %shard_map.111 = (f32[24,64,128]{2,1,0:T(8,128)S(1)}, f32[24,64,128]{2,1,0:T(8,128)S(1)}, f32[2,64,128]{2,1,0:T(8,128)S(1)}, f32[64,128]{1,0:T(8,128)S(1)}, f32[...) custom-call(f32[24,64,128]{2,1,0:T(8,128)S(1)} %get-tuple-element.115.refs_0_, ...), custom_call_target="tpu_custom_call" | custom-call | flops 4000000 | bytes 1000000 | tf_op jit(solution)/shard_map/pallas_call | solution.py:41
  52.8 0.4 shard_map.113
  53.2 2.6 %collective-permute-start.22 = (f32[4,12,64,128]{3,2,1,0:T(8,128)S(1)}, f32[4,12,64,128]{3,2,1,0:T(8,128)S(1)}, u32[]{:S(2)}, u32[]{:S(2)}) collective-permute-start(f32[4,12,64,128]{3,2,1,0:T(8,128)S(1)} %get-tuple-element.137), channel_id=1, source_target_pairs={{0,1},{1,0},{2,3},{3,2},{4,5},{5,4},{6,7},{7,6},{8,9},{9,8},{10,11... | collective-permute-start | bytes 4718600 | tf_op jit(solution)/shard_map/ppermute | solution.py:588
  55.9 0.9 %collective-permute-start.19 = (f32[2,64,128]{2,1,0:T(8,128)S(1)}, f32[2,64,128]{2,1,0:T(8,128)S(1)}, u32[]{:S(2)}, u32[]{:S(2)}) collective-permute-start(f32[2,64,128]{2,1,0:T(8,128)S(1)} %get-tuple-element.128), channel_id=1, source_target_pairs={{0,2},{1,3},{2,0},{3,1},{4,6},{5,7},{6,4},{7,5},{8,10},{9,11},{10,... | collective-permute-start | bytes 196616 | tf_op jit(solution)/shard_map/ppermute | solution.py:579
  56.8 1.9 %collective-permute-start.21 = (f32[2,64,128]{2,1,0:T(8,128)S(1)}, f32[2,64,128]{2,1,0:T(8,128)S(1)}, u32[]{:S(2)}, u32[]{:S(2)}) collective-permute-start(f32[2,64,128]{2,1,0:T(8,128)S(1)} %get-tuple-element.130), channel_id=1, source_target_pairs={{0,6},{1,7},{2,4},{3,5},{4,2},{5,3},{6,0},{7,1},{8,14},{9,15},{10,... | collective-permute-start | bytes 196616 | tf_op jit(solution)/shard_map/ppermute | solution.py:580
  58.7 0.7 %collective-permute-start.20 = (f32[64,128]{1,0:T(8,128)S(1)}, f32[64,128]{1,0:T(8,128)S(1)}, u32[]{:S(2)}, u32[]{:S(2)}) collective-permute-start(f32[64,128]{1,0:T(8,128)S(1)} %get-tuple-element.129), channel_id=1, source_target_pairs={{0,4},{1,5},{2,6},{3,7},{4,0},{5,1},{6,2},{7,3},{8,12},{9,13},{10,... | collective-permute-start | bytes 98312 | tf_op jit(solution)/shard_map/ppermute | solution.py:578
  59.4 3.5 %collective-permute-done.20.refs_8_ = f32[64,128]{1,0:T(8,128)S(1)} collective-permute-done((f32[64,128]{1,0:T(8,128)S(1)}, f32[64,128]{1,0:T(8,128)S(1)}, u32[]{:S(2)}, u32[]{:S(2)}) %collective-permute-start.20) | collective-permute-done | bytes 32800 | tf_op jit(solution)/shard_map/ppermute | solution.py:578
  63.0 0.0 collective-permute-done.19.refs_7_
  63.0 0.0 collective-permute-done.21.refs_9_
  63.0 0.8 %shard_map.112 = (f32[3,12,64,128]{3,2,1,0:T(8,128)S(1)}, f32[14,64,128]{2,1,0:T(8,128)S(1)}) custom-call(f32[24,64,128]{2,1,0:T(8,128)S(1)} %get-tuple-element.125.refs_0_.star, f32[24,64,128]{2,1,0:T(8,128)S(1)} %get-tuple-element.126.refs_1_, f32[24,64,128]{2,1,0:T(8,128)S(1)} %get-tuple-element.127.refs_2_.geo, ...), custom_call_target="tpu_custom_call" | custom-call | flops 4000000 | bytes 1000000 | tf_op jit(solution)/shard_map/pallas_call | solution.py:41
  63.7 1.9 %collective-permute-start.23 = (f32[14,64,128]{2,1,0:T(8,128)S(1)}, f32[14,64,128]{2,1,0:T(8,128)S(1)}, u32[]{:S(2)}, u32[]{:S(2)}) collective-permute-start(f32[14,64,128]{2,1,0:T(8,128)S(1)} %get-tuple-element.138), channel_id=1, source_target_pairs={{0,1},{1,0},{2,3},{3,2},{4,5},{5,4},{6,7},{7,6},{8,9},{9,8},{10,11... | collective-permute-start | bytes 1376264 | tf_op jit(solution)/shard_map/ppermute | solution.py:590
  65.6 1.4 %collective-permute-done.23.got_wind = f32[14,64,128]{2,1,0:T(8,128)S(1)} collective-permute-done((f32[14,64,128]{2,1,0:T(8,128)S(1)}, f32[14,64,128]{2,1,0:T(8,128)S(1)}, u32[]{:S(2)}, u32[]{:S(2)}) %collective-permute-start.23) | collective-permute-done | bytes 458784 | tf_op jit(solution)/shard_map/ppermute | solution.py:590
  67.1 2.0 %shard_map.114 = (f32[12,128,128]{2,1,0:T(8,128)}, f32[12,128,128]{2,1,0:T(8,128)}, f32[12,128,128]{2,1,0:T(8,128)}, f32[12,128,128]{2,1,0:T(8,128)}, f32[12,128,128]{2,1,0:T(8,128)}) custom-call(f32[3,12,64,128]{3,2,1,0:T(8,128)S(1)} %get-tuple-element.131.own, f32[2,12,64,128]{3,2,1,0:T(8,128)S(1)} %get-tuple-element.136.own_winds, ...), custom_call_target="tpu_custom_call" | custom-call | flops 4000000 | bytes 1000000 | tf_op jit(solution)/shard_map/pallas_call | solution.py:41
  (21 shorter events, 0.1 us)
Async XLA Ops:
  3.4 0.6 copy-start.5
  4.0 11.2 %copy-start.2 = (f32[12,128,128]{2,1,0:T(8,128)S(1)}, f32[12,128,128]{2,1,0:T(8,128)}, u32[]{:S(2)}) copy-start(f32[12,128,128]{2,1,0:T(8,128)} %refs_0_.3) | copy-start | bytes 2359300
  4.0 11.2 %copy-start.3 = (f32[12,128,128]{2,1,0:T(8,128)S(1)}, f32[12,128,128]{2,1,0:T(8,128)}, u32[]{:S(2)}) copy-start(f32[12,128,128]{2,1,0:T(8,128)} %refs_1_.3) | copy-start | bytes 2359300
  4.0 4.1 %collective-permute-start = (f32[144,128]{1,0:T(8,128)S(1)}, f32[144,128]{1,0:T(8,128)S(1)}, u32[]{:S(2)}, u32[]{:S(2)}) collective-permute-start(f32[144,128]{1,0:T(8,128)S(1)} %get-tuple-element.73), channel_id=1, source_target_pairs={{0,1},{1,0},{2,3},{3,2},{4,5},{5,4},{6,7},{7,6},{8,9},{9,8},{10,11... | collective-permute-start | bytes 221192 | tf_op jit(solution)/shard_map/ppermute | solution.py:544
  8.2 0.6 copy-start.7
  8.8 6.5 %collective-permute-start.1 = (f32[5,12,64,128]{3,2,1,0:T(8,128)}, f32[5,12,64,128]{3,2,1,0:T(8,128)S(1)}, u32[]{:S(2)}, u32[]{:S(2)}) collective-permute-start(f32[5,12,64,128]{3,2,1,0:T(8,128)} %get-tuple-element.74), channel_id=1, source_target_pairs={{0,1},{1,0},{2,3},{3,2},{4,5},{5,4},{6,7},{7,6},{8,9},{9,8},{10,11... | collective-permute-start | bytes 5898248 | tf_op jit(solution)/shard_map/ppermute | solution.py:547
  9.1 6.1 %copy-start.4 = (f32[12,128,128]{2,1,0:T(8,128)S(1)}, f32[12,128,128]{2,1,0:T(8,128)}, u32[]{:S(2)}) copy-start(f32[12,128,128]{2,1,0:T(8,128)} %refs_2_.3) | copy-start | bytes 2359300
  10.4 0.9 %copy-start.6 = (f32[144,128]{1,0:T(8,128)S(1)}, f32[144,128]{1,0:T(8,128)}, u32[]{:S(2)}) copy-start(f32[144,128]{1,0:T(8,128)} %copy-done.5) | copy-start | bytes 221188
  11.3 0.9 %copy-start.8 = (f32[144,128]{1,0:T(8,128)S(1)}, f32[144,128]{1,0:T(8,128)}, u32[]{:S(2)}) copy-start(f32[144,128]{1,0:T(8,128)} %copy-done.7) | copy-start | bytes 221188
  12.2 5.1 %collective-permute-start.4 = (f32[96,128]{1,0:T(8,128)S(1)}, f32[96,128]{1,0:T(8,128)S(1)}, u32[]{:S(2)}, u32[]{:S(2)}) collective-permute-start(f32[96,128]{1,0:T(8,128)S(1)} %get-tuple-element.82.refs_11_), channel_id=1, source_target_pairs={{0,24},{8,16},{16,8},{24,0},{1,25},{9,17},{17,9},{25,1},{2,26},{10... | collective-permute-start | bytes 147464 | tf_op jit(solution)/shard_map/ppermute | solution.py:565
  13.0 4.3 %collective-permute-start.3 = (f32[96,128]{1,0:T(8,128)S(1)}, f32[96,128]{1,0:T(8,128)S(1)}, u32[]{:S(2)}, u32[]{:S(2)}) collective-permute-start(f32[96,128]{1,0:T(8,128)S(1)} %get-tuple-element.82.refs_11_), channel_id=1, source_target_pairs={{0,8},{8,0},{16,24},{24,16},{1,9},{9,1},{17,25},{25,17},{2,10},{10... | collective-permute-start | bytes 147464 | tf_op jit(solution)/shard_map/ppermute | solution.py:564
  13.0 4.2 %collective-permute-start.2 = (f32[96,128]{1,0:T(8,128)S(1)}, f32[96,128]{1,0:T(8,128)S(1)}, u32[]{:S(2)}, u32[]{:S(2)}) collective-permute-start(f32[96,128]{1,0:T(8,128)S(1)} %get-tuple-element.81), channel_id=1, source_target_pairs={{0,225},{1,32},{2,227},{3,34},{4,229},{5,36},{6,231},{7,38},{32,1}... | collective-permute-start | bytes 147464 | tf_op jit(solution)/shard_map/ppermute | solution.py:566
  15.2 1.7 %copy-start = (f32[12,128,128]{2,1,0:T(8,128)S(1)}, f32[12,128,128]{2,1,0:T(8,128)}, u32[]{:S(2)}) copy-start(f32[12,128,128]{2,1,0:T(8,128)} %wind.1) | copy-start | bytes 2359300
  15.3 1.7 %copy-start.1 = (f32[12,128,128]{2,1,0:T(8,128)S(1)}, f32[12,128,128]{2,1,0:T(8,128)}, u32[]{:S(2)}) copy-start(f32[12,128,128]{2,1,0:T(8,128)} %geo.1) | copy-start | bytes 2359300
  18.0 7.4 %collective-permute-start.5 = (f32[2,64,128]{2,1,0:T(8,128)S(1)}, f32[2,64,128]{2,1,0:T(8,128)S(1)}, u32[]{:S(2)}, u32[]{:S(2)}) collective-permute-start(f32[2,64,128]{2,1,0:T(8,128)S(1)} %get-tuple-element.86), channel_id=1, source_target_pairs={{0,2},{1,3},{2,0},{3,1},{4,6},{5,7},{6,4},{7,5},{8,10},{9,11},{10,... | collective-permute-start | bytes 196616 | tf_op jit(solution)/shard_map/ppermute | solution.py:579
  19.3 6.2 %collective-permute-start.7 = (f32[2,64,128]{2,1,0:T(8,128)S(1)}, f32[2,64,128]{2,1,0:T(8,128)S(1)}, u32[]{:S(2)}, u32[]{:S(2)}) collective-permute-start(f32[2,64,128]{2,1,0:T(8,128)S(1)} %get-tuple-element.88), channel_id=1, source_target_pairs={{0,6},{1,7},{2,4},{3,5},{4,2},{5,3},{6,0},{7,1},{8,14},{9,15},{10,... | collective-permute-start | bytes 196616 | tf_op jit(solution)/shard_map/ppermute | solution.py:580
  21.2 4.3 %collective-permute-start.6 = (f32[64,128]{1,0:T(8,128)S(1)}, f32[64,128]{1,0:T(8,128)S(1)}, u32[]{:S(2)}, u32[]{:S(2)}) collective-permute-start(f32[64,128]{1,0:T(8,128)S(1)} %get-tuple-element.87), channel_id=1, source_target_pairs={{0,4},{1,5},{2,6},{3,7},{4,0},{5,1},{6,2},{7,3},{8,12},{9,13},{10,... | collective-permute-start | bytes 98312 | tf_op jit(solution)/shard_map/ppermute | solution.py:578
  26.2 8.6 %collective-permute-start.8 = (f32[48,128]{1,0:T(8,128)S(1)}, f32[48,128]{1,0:T(8,128)S(1)}, u32[]{:S(2)}, u32[]{:S(2)}) collective-permute-start(f32[48,128]{1,0:T(8,128)S(1)} %get-tuple-element.97), channel_id=1, source_target_pairs={{0,1},{1,0},{2,3},{3,2},{4,5},{5,4},{6,7},{7,6},{8,9},{9,8},{10,11... | collective-permute-start | bytes 73736 | tf_op jit(solution)/shard_map/ppermute | solution.py:572
  31.7 3.3 %collective-permute-start.9 = (f32[48,128]{1,0:T(8,128)S(1)}, f32[48,128]{1,0:T(8,128)S(1)}, u32[]{:S(2)}, u32[]{:S(2)}) collective-permute-start(f32[48,128]{1,0:T(8,128)S(1)} %get-tuple-element.98), channel_id=1, source_target_pairs={{0,225},{1,32},{2,227},{3,34},{4,229},{5,36},{6,231},{7,38},{32,1}... | collective-permute-start | bytes 73736 | tf_op jit(solution)/shard_map/ppermute | solution.py:566
  31.7 4.2 %collective-permute-start.11 = (f32[48,128]{1,0:T(8,128)S(1)}, f32[48,128]{1,0:T(8,128)S(1)}, u32[]{:S(2)}, u32[]{:S(2)}) collective-permute-start(f32[48,128]{1,0:T(8,128)S(1)} %get-tuple-element.99.refs_11_), channel_id=1, source_target_pairs={{0,24},{8,16},{16,8},{24,0},{1,25},{9,17},{17,9},{25,1},{2,26},{10... | collective-permute-start | bytes 73736 | tf_op jit(solution)/shard_map/ppermute | solution.py:565
  32.5 3.4 %collective-permute-start.10 = (f32[48,128]{1,0:T(8,128)S(1)}, f32[48,128]{1,0:T(8,128)S(1)}, u32[]{:S(2)}, u32[]{:S(2)}) collective-permute-start(f32[48,128]{1,0:T(8,128)S(1)} %get-tuple-element.99.refs_11_), channel_id=1, source_target_pairs={{0,8},{8,0},{16,24},{24,16},{1,9},{9,1},{17,25},{25,17},{2,10},{10... | collective-permute-start | bytes 73736 | tf_op jit(solution)/shard_map/ppermute | solution.py:564
  36.6 5.2 %collective-permute-start.12 = (f32[2,64,128]{2,1,0:T(8,128)S(1)}, f32[2,64,128]{2,1,0:T(8,128)S(1)}, u32[]{:S(2)}, u32[]{:S(2)}) collective-permute-start(f32[2,64,128]{2,1,0:T(8,128)S(1)} %get-tuple-element.107), channel_id=1, source_target_pairs={{0,2},{1,3},{2,0},{3,1},{4,6},{5,7},{6,4},{7,5},{8,10},{9,11},{10,... | collective-permute-start | bytes 196616 | tf_op jit(solution)/shard_map/ppermute | solution.py:579
  37.1 4.8 %collective-permute-start.14 = (f32[2,64,128]{2,1,0:T(8,128)S(1)}, f32[2,64,128]{2,1,0:T(8,128)S(1)}, u32[]{:S(2)}, u32[]{:S(2)}) collective-permute-start(f32[2,64,128]{2,1,0:T(8,128)S(1)} %get-tuple-element.109), channel_id=1, source_target_pairs={{0,6},{1,7},{2,4},{3,5},{4,2},{5,3},{6,0},{7,1},{8,14},{9,15},{10,... | collective-permute-start | bytes 196616 | tf_op jit(solution)/shard_map/ppermute | solution.py:580
  37.6 4.3 %collective-permute-start.13 = (f32[64,128]{1,0:T(8,128)S(1)}, f32[64,128]{1,0:T(8,128)S(1)}, u32[]{:S(2)}, u32[]{:S(2)}) collective-permute-start(f32[64,128]{1,0:T(8,128)S(1)} %get-tuple-element.108), channel_id=1, source_target_pairs={{0,4},{1,5},{2,6},{3,7},{4,0},{5,1},{6,2},{7,3},{8,12},{9,13},{10,... | collective-permute-start | bytes 98312 | tf_op jit(solution)/shard_map/ppermute | solution.py:578
  42.5 8.6 %collective-permute-start.15 = (f32[48,128]{1,0:T(8,128)S(1)}, f32[48,128]{1,0:T(8,128)S(1)}, u32[]{:S(2)}, u32[]{:S(2)}) collective-permute-start(f32[48,128]{1,0:T(8,128)S(1)} %get-tuple-element.118), channel_id=1, source_target_pairs={{0,1},{1,0},{2,3},{3,2},{4,5},{5,4},{6,7},{7,6},{8,9},{9,8},{10,11... | collective-permute-start | bytes 73736 | tf_op jit(solution)/shard_map/ppermute | solution.py:572
  47.7 3.5 %collective-permute-start.16 = (f32[48,128]{1,0:T(8,128)S(1)}, f32[48,128]{1,0:T(8,128)S(1)}, u32[]{:S(2)}, u32[]{:S(2)}) collective-permute-start(f32[48,128]{1,0:T(8,128)S(1)} %get-tuple-element.119), channel_id=1, source_target_pairs={{0,225},{1,32},{2,227},{3,34},{4,229},{5,36},{6,231},{7,38},{32,1}... | collective-permute-start | bytes 73736 | tf_op jit(solution)/shard_map/ppermute | solution.py:566
  47.7 4.2 %collective-permute-start.18 = (f32[48,128]{1,0:T(8,128)S(1)}, f32[48,128]{1,0:T(8,128)S(1)}, u32[]{:S(2)}, u32[]{:S(2)}) collective-permute-start(f32[48,128]{1,0:T(8,128)S(1)} %get-tuple-element.120.refs_11_), channel_id=1, source_target_pairs={{0,24},{8,16},{16,8},{24,0},{1,25},{9,17},{17,9},{25,1},{2,26},{10... | collective-permute-start | bytes 73736 | tf_op jit(solution)/shard_map/ppermute | solution.py:565
  49.4 2.7 %collective-permute-start.17 = (f32[48,128]{1,0:T(8,128)S(1)}, f32[48,128]{1,0:T(8,128)S(1)}, u32[]{:S(2)}, u32[]{:S(2)}) collective-permute-start(f32[48,128]{1,0:T(8,128)S(1)} %get-tuple-element.120.refs_11_), channel_id=1, source_target_pairs={{0,8},{8,0},{16,24},{24,16},{1,9},{9,1},{17,25},{25,17},{2,10},{10... | collective-permute-start | bytes 73736 | tf_op jit(solution)/shard_map/ppermute | solution.py:564
  53.2 13.8 %collective-permute-start.22 = (f32[4,12,64,128]{3,2,1,0:T(8,128)S(1)}, f32[4,12,64,128]{3,2,1,0:T(8,128)S(1)}, u32[]{:S(2)}, u32[]{:S(2)}) collective-permute-start(f32[4,12,64,128]{3,2,1,0:T(8,128)S(1)} %get-tuple-element.137), channel_id=1, source_target_pairs={{0,1},{1,0},{2,3},{3,2},{4,5},{5,4},{6,7},{7,6},{8,9},{9,8},{10,11... | collective-permute-start | bytes 4718600 | tf_op jit(solution)/shard_map/ppermute | solution.py:588
  55.9 7.1 %collective-permute-start.19 = (f32[2,64,128]{2,1,0:T(8,128)S(1)}, f32[2,64,128]{2,1,0:T(8,128)S(1)}, u32[]{:S(2)}, u32[]{:S(2)}) collective-permute-start(f32[2,64,128]{2,1,0:T(8,128)S(1)} %get-tuple-element.128), channel_id=1, source_target_pairs={{0,2},{1,3},{2,0},{3,1},{4,6},{5,7},{6,4},{7,5},{8,10},{9,11},{10,... | collective-permute-start | bytes 196616 | tf_op jit(solution)/shard_map/ppermute | solution.py:579
  56.8 6.2 %collective-permute-start.21 = (f32[2,64,128]{2,1,0:T(8,128)S(1)}, f32[2,64,128]{2,1,0:T(8,128)S(1)}, u32[]{:S(2)}, u32[]{:S(2)}) collective-permute-start(f32[2,64,128]{2,1,0:T(8,128)S(1)} %get-tuple-element.130), channel_id=1, source_target_pairs={{0,6},{1,7},{2,4},{3,5},{4,2},{5,3},{6,0},{7,1},{8,14},{9,15},{10,... | collective-permute-start | bytes 196616 | tf_op jit(solution)/shard_map/ppermute | solution.py:580
  58.7 4.3 %collective-permute-start.20 = (f32[64,128]{1,0:T(8,128)S(1)}, f32[64,128]{1,0:T(8,128)S(1)}, u32[]{:S(2)}, u32[]{:S(2)}) collective-permute-start(f32[64,128]{1,0:T(8,128)S(1)} %get-tuple-element.129), channel_id=1, source_target_pairs={{0,4},{1,5},{2,6},{3,7},{4,0},{5,1},{6,2},{7,3},{8,12},{9,13},{10,... | collective-permute-start | bytes 98312 | tf_op jit(solution)/shard_map/ppermute | solution.py:578
  63.7 3.3 %collective-permute-start.23 = (f32[14,64,128]{2,1,0:T(8,128)S(1)}, f32[14,64,128]{2,1,0:T(8,128)S(1)}, u32[]{:S(2)}, u32[]{:S(2)}) collective-permute-start(f32[14,64,128]{2,1,0:T(8,128)S(1)} %get-tuple-element.138), channel_id=1, source_target_pairs={{0,1},{1,0},{2,3},{3,2},{4,5},{5,4},{6,7},{7,6},{8,9},{9,8},{10,11... | collective-permute-start | bytes 1376264 | tf_op jit(solution)/shard_map/ppermute | solution.py:590
